TPU v7x, 128 devices: a whole 4x4x4 slice. The times are simulated.
128 devices in a mesh: blk: 8 (over y, x_lo), inner: 16 (over z, x_hi, core).
Axes of the slice: x: 4 (x_hi: 2, x_lo: 2; x = x_hi * 2 + x_lo), y: 4, z: 4, core: 2. Of those that a mesh axis runs over, the one named last changes fastest.
Arguments:
- points: float32 [16384, 128], P(('blk', 'inner')), may hold values from -8 to 8
- lengthscales: float32 [128], replicated, may hold values from 6 to 24
- noise_level: float32 [1], replicated, may hold values from 1 to 10
- iterate: float32 [16384, 64], P(('blk', 'inner')), may hold values from -6 to 6
- residual: float32 [16384, 64], P(('blk', 'inner')), may hold values from -6 to 6
- direction: float32 [16384, 64], P(('blk', 'inner')), may hold values from -6 to 6
Outputs:
- new_iterate: float32 [16384, 64], P(('blk', 'inner'))
- new_residual: float32 [16384, 64], P(('blk', 'inner'))
- new_direction: float32 [16384, 64], P(('blk', 'inner'))
All inputs are finite; a program needn't handle non-finite values.
Results may differ from a plain program's by a relative error of at most 0.00014.
Values sent between devices are 32-bit elements; how exact they have to be, the bound alone decides.
No kernel may reach another device: no remote copies, remote signals or barrier semaphores. Data moves between devices by JAX's collectives and lax.ppermute only.
A program may use at most 64 MiB of HBM per device.

v0:
```python
import jax
import jax.numpy as jnp
from jax import lax
from jax.sharding import PartitionSpec as P


def sent_together(arrays, axis, dim, along):
    both = jnp.concatenate(arrays, axis=along)
    whole, at, outs = (lax.all_gather(both, axis, axis=dim, tiled=True), 0, [])
    for a in arrays:
        outs.append(lax.slice_in_dim(whole, at, at + a.shape[along], axis=along))
        at += a.shape[along]
    return tuple(outs)


def from_behind(value, axis, by):
    size = lax.axis_size(axis)
    return lax.ppermute(value, axis, [(i, (i + by) % size) for i in range(size)])


def split_up(value, dim, size):
    dims = value.shape
    blocks = value.reshape(*dims[:dim], size, dims[dim] // size, *dims[dim + 1 :])
    return jnp.moveaxis(blocks, dim, 0)


def sum_at_owner(value, axis, dim):
    size = lax.axis_size(axis)
    blocks = lax.all_to_all(split_up(value, dim, size), axis, 0, 0, tiled=True)
    return jnp.sum(blocks, axis=0)


def kernel_block(left, left_sq, right, right_sq):
    products = lax.dot_general(
        left,
        right,
        (((1,), (1,)), ((), ())),
        precision=lax.Precision.HIGHEST,
        preferred_element_type=jnp.float32,
    )
    return jnp.exp(-0.5 * (left_sq[:, None] + right_sq[None, :] - 2.0 * products))


def matmul(left, right):
    return jnp.dot(left, right, precision=lax.Precision.HIGHEST, preferred_element_type=jnp.float32)


def transposed(left, right):
    return lax.dot_general(
        left,
        right,
        (((0,), (0,)), ((), ())),
        precision=lax.Precision.HIGHEST,
        preferred_element_type=jnp.float32,
    )


def chol_solve(matrix, rhs_side):
    factor = jnp.linalg.cholesky(matrix)
    return jax.scipy.linalg.cho_solve((factor, True), rhs_side)


def on_device(points, lengthscales, noise_level, iterate, residual, direction):
    scaled = points / lengthscales[None, :]
    sq_norms = jnp.sum(scaled * scaled, axis=1)
    cycle_size = lax.axis_size("blk")
    group_pts, group_dir = sent_together((scaled, direction), "inner", 0, 1)
    group_sq = jnp.sum(group_pts * group_pts, axis=1)
    partial_value = jnp.zeros((group_pts.shape[0], direction.shape[1]), jnp.float32)
    halfway = cycle_size // 2
    visitor = (scaled, sq_norms, direction, jnp.zeros_like(direction))
    returned = jnp.zeros_like(direction)
    for offset in range(halfway + 1):
        if offset > 0:
            visitor = from_behind((visitor[0], visitor[1], visitor[2], visitor[3]), "blk", 1)
        kernel_tile = kernel_block(group_pts, group_sq, visitor[0], visitor[1])
        partial_value = partial_value + matmul(kernel_tile, visitor[2])
        if 1 <= offset <= halfway - 1:
            carried = visitor[3] + transposed(kernel_tile, group_dir)
            visitor = (visitor[0], visitor[1], visitor[2], carried)
            if offset == halfway - 1:
                returned = from_behind(carried, "blk", -(halfway - 1))
    owned = sum_at_owner(partial_value, "inner", 0)
    image = owned + returned + noise_level[0] * direction
    local_gram = transposed(direction, image)
    local_res = transposed(residual, residual)
    local_cross = transposed(image, residual)
    local_image = transposed(image, image)
    gram_raw, res_gram, cross_gram, image_gram = lax.psum(
        (local_gram, local_res, local_cross, local_image), ("blk", "inner")
    )
    gram_matrix = 0.5 * (gram_raw + gram_raw.T)
    step_size = chol_solve(gram_matrix, res_gram)
    new_residual = residual - matmul(image, step_size)
    cross_term = transposed(step_size, cross_gram)
    new_gram = (
        res_gram - cross_term - cross_term.T + transposed(step_size, matmul(image_gram, step_size))
    )
    new_iterate = iterate + matmul(direction, step_size)
    correction = chol_solve(res_gram, new_gram)
    new_direction = new_residual + matmul(direction, correction)
    return (new_iterate, new_residual, new_direction)


def solution(mesh):
    return jax.shard_map(
        on_device,
        mesh=mesh,
        in_specs=(
            P(("blk", "inner"), None),
            P(),
            P(),
            P(("blk", "inner"), None),
            P(("blk", "inner"), None),
            P(("blk", "inner"), None),
        ),
        out_specs=(P(("blk", "inner"), None), P(("blk", "inner"), None), P(("blk", "inner"), None)),
        check_vma=False,
    )
```

profile of v0, /device:TPU:0, one launch (start us, length us, event | category | flops | bytes accessed | tf_op | source)
XLA Modules:
  0.0 288.0 jit_solution(3452829028754681316)
XLA Ops:
  7.2 0.8 copy.16
  8.1 1.0 multiply_reduce_fusion.1
  9.7 1.7 collective-permute-start.1
  11.4 4.8 %collective-permute-done.1 = f32[128,128]{1,0:T(8,128)S(1)} collective-permute-done((f32[128,128]{1,0:T(8,128)S(1)}, f32[128,128]{1,0:T(8,128)S(1)}, u32[]{:S(2)}, u32[]{:S(2)}) %collective-permute-start.1) | collective-permute-done | bytes 65568 | tf_op jit(solution)/shard_map/ppermute | solution.py:18
  16.2 1.9 collective-permute-start.2
  18.1 4.8 %collective-permute-done.2 = f32[128,64]{0,1:T(8,128)S(1)} collective-permute-done((f32[128,64]{0,1:T(8,128)}, f32[128,64]{0,1:T(8,128)S(1)}, u32[]{:S(2)}, u32[]{:S(2)}) %collective-permute-start.2) | collective-permute-done | bytes 32800 | tf_op jit(solution)/shard_map/ppermute | solution.py:18
  22.9 0.8 collective-permute-start.7
  23.7 5.5 %collective-permute-done.5 = f32[128,64]{0,1:T(8,128)S(1)} collective-permute-done((f32[128,64]{0,1:T(8,128)S(1)}, f32[128,64]{0,1:T(8,128)S(1)}, u32[]{:S(2)}, u32[]{:S(2)}) %collective-permute-start.5) | collective-permute-done | bytes 32800 | tf_op jit(solution)/shard_map/ppermute | solution.py:18
  29.3 6.1 %collective-permute-done = f32[128]{0:T(128)S(1)} collective-permute-done((f32[128]{0:T(128)S(1)}, f32[128]{0:T(128)S(1)}, u32[]{:S(2)}, u32[]{:S(2)}) %collective-permute-start) | collective-permute-done | bytes 544 | tf_op jit(solution)/shard_map/ppermute | solution.py:18
  35.4 5.7 %collective-permute-done.3 = f32[128]{0:T(128)S(1)} collective-permute-done((f32[128]{0:T(128)S(1)}, f32[128]{0:T(128)S(1)}, u32[]{:S(2)}, u32[]{:S(2)}) %collective-permute-start.3) | collective-permute-done | bytes 544 | tf_op jit(solution)/shard_map/ppermute | solution.py:18
  41.1 5.7 %collective-permute-done.6 = f32[128]{0:T(128)S(1)} collective-permute-done((f32[128]{0:T(128)S(1)}, f32[128]{0:T(128)S(1)}, u32[]{:S(2)}, u32[]{:S(2)}) %collective-permute-start.6) | collective-permute-done | bytes 544 | tf_op jit(solution)/shard_map/ppermute | solution.py:18
  46.8 14.3 %all-gather.2.cloned.1.call-done = f32[2048,192]{1,0:T(8,128)} async-done(((f32[128,192]{1,0:T(8,128)}), f32[2048,192]{1,0:T(8,128)}) %all-gather.2.cloned.1.call-update) | async-done | bytes 1572880 | tf_op jit(solution)/shard_map/all_gather | solution.py:9
  61.2 1.7 multiply_reduce_fusion
  62.9 2.2 convolution_multiply_fusion.3
  65.2 1.1 fusion.2
  66.2 1.3 fusion.67
  67.5 2.2 convolution_add_fusion.5
  69.7 2.0 collective-permute-start.13
  71.7 1.0 convolution_multiply_fusion.1
  72.7 1.0 convolution_multiply_fusion.2
  73.7 1.0 convolution_multiply_fusion
  74.7 1.5 convolution_add_fusion.3
  76.2 1.5 convolution_add_fusion.2
  77.7 1.5 convolution_add_fusion.1
  79.2 2.2 fusion.15
  81.4 2.5 collective-permute-start.14
  83.8 1.5 fusion.3
  85.3 0.9 copy.28
  86.2 4.2 %all-to-all-start = ((f32[16,128,64]{1,2,0:T(8,128)}), f32[16,128,64]{1,2,0:T(8,128)}, u32[]{:S(2)}, u32[]{:S(2)}) async-start(f32[16,128,64]{1,2,0:T(8,128)} %bitcast.82), calls=%async_computation | async-start | bytes 1048576 | tf_op jit(solution)/shard_map/all_to_all | solution.py:29
  90.7 2.2 fusion.18
  92.9 2.1 collective-permute-start.15
  95.1 0.8 fusion.68
  96.5 6.6 %all-to-all-done = f32[16,128,64]{1,2,0:T(8,128)} async-done(((f32[16,128,64]{1,2,0:T(8,128)}), f32[16,128,64]{1,2,0:T(8,128)}, u32[]{:S(2)}, u32[]{:S(2)}) %all-to-all-start) | async-done | bytes 524320 | tf_op jit(solution)/shard_map/all_to_all | solution.py:29
  103.1 1.1 reduce_sum.29
  104.2 0.8 fusion.71
  106.7 140.5 %all-reduce.3.cloned.1.call-done = (f32[64,64]{0,1:T(8,128)}, f32[64,64]{1,0:T(8,128)}, f32[64,64]{1,0:T(8,128)}, f32[64,64]{1,0:T(8,128)}) async-done(((f32[64,64]{0,1:T(8,128)}, f32[64,64]{1,0:T(8,128)}, f32[64,64]{1,0:T(8,128)}, f32[64,64]{1,0:T(8,128)}), (f32[64,64]{0,1:T(8,128)}, f32[64,64]{1,0:T(8,128)}, f32[64,64]{1,0:T(8,128)}, f32[64,64]{1,0:T(8,128)})) %all-reduce.3.cloned.1.call-update) | async-done | bytes 65552 | tf_op jit(solution)/shard_map/psum | solution.py:89
  247.1 0.8 copy.19
  248.8 5.8 %cholesky.44 = f32[64,64]{1,0:T(8,128)S(1)} custom-call(f32[64,64]{1,0:T(8,128)S(1)} %fusion.58), custom_call_target="Cholesky" | custom-call | tf_op jit(solution)/shard_map/jit(cholesky)/cholesky | solution.py:59
  256.0 4.9 %custom-call.8 = f32[1,64,64]{1,2,0:T(8,128)S(1)} custom-call(f32[1,64,64]{2,1,0:T(8,128)S(1)} %fusion.47), custom_call_target="InvertDiagBlocksLowerTriangular" | custom-call | tf_op jit(solution)/shard_map/jit(_cho_solve)/triangular_solve | solution.py:60
  260.9 0.8 copy.22
  261.7 1.0 fusion.56
  263.2 1.0 fusion.70
  264.2 0.9 fusion.72
  265.2 0.9 fusion.5
  266.8 5.8 %cholesky.55 = f32[64,64]{1,0:T(8,128)S(1)} custom-call(f32[64,64]{1,0:T(8,128)S(1)} %fusion.53), custom_call_target="Cholesky" | custom-call | tf_op jit(solution)/shard_map/jit(cholesky)/cholesky | solution.py:59
  274.0 4.9 %custom-call.9 = f32[1,64,64]{1,2,0:T(8,128)S(1)} custom-call(f32[1,64,64]{2,1,0:T(8,128)S(1)} %fusion.48), custom_call_target="InvertDiagBlocksLowerTriangular" | custom-call | tf_op jit(solution)/shard_map/jit(_cho_solve)/triangular_solve | solution.py:60
  278.9 1.0 convolution_add_fusion.4
  280.3 0.9 fusion.4
  (54 shorter events, 7.9 us)
Async XLA Ops:
  7.2 54.0 %all-gather.2.cloned.1.call-start = ((), (), s32[]{:S(2)}) async-start(), calls=%async_computation.1 | async-start | bytes 2228224 | tf_op jit(solution)/shard_map/all_gather | solution.py:9
  9.7 6.4 %collective-permute-start.1 = (f32[128,128]{1,0:T(8,128)S(1)}, f32[128,128]{1,0:T(8,128)S(1)}, u32[]{:S(2)}, u32[]{:S(2)}) collective-permute-start(f32[128,128]{1,0:T(8,128)S(1)} %get-tuple-element.10), channel_id=1, source_target_pairs={{0,16},{16,32},{32,48},{48,64},{64,80},{80,96},{96,112},{112,0},{1... | collective-permute-start | bytes 196616 | tf_op jit(solution)/shard_map/ppermute | solution.py:18
  16.2 6.7 %collective-permute-start.4 = (f32[128,128]{1,0:T(8,128)S(1)}, f32[128,128]{1,0:T(8,128)S(1)}, u32[]{:S(2)}, u32[]{:S(2)}) collective-permute-start(f32[128,128]{1,0:T(8,128)S(1)} %collective-permute-done.1), channel_id=1, source_target_pairs={{0,16},{16,32},{32,48},{48,64},{64,80},{80,96},{96,112},{112,0},{1... | collective-permute-start | bytes 196616 | tf_op jit(solution)/shard_map/ppermute | solution.py:18
  16.2 6.7 %collective-permute-start.2 = (f32[128,64]{0,1:T(8,128)}, f32[128,64]{0,1:T(8,128)S(1)}, u32[]{:S(2)}, u32[]{:S(2)}) collective-permute-start(f32[128,64]{0,1:T(8,128)} %param.14), channel_id=1, source_target_pairs={{0,16},{16,32},{32,48},{48,64},{64,80},{80,96},{96,112},{112,0},{1... | collective-permute-start | bytes 98312 | tf_op jit(solution)/shard_map/ppermute | solution.py:18
  22.9 6.4 %collective-permute-start.5 = (f32[128,64]{0,1:T(8,128)S(1)}, f32[128,64]{0,1:T(8,128)S(1)}, u32[]{:S(2)}, u32[]{:S(2)}) collective-permute-start(f32[128,64]{0,1:T(8,128)S(1)} %collective-permute-done.2), channel_id=1, source_target_pairs={{0,16},{16,32},{32,48},{48,64},{64,80},{80,96},{96,112},{112,0},{1... | collective-permute-start | bytes 98312 | tf_op jit(solution)/shard_map/ppermute | solution.py:18
  22.9 23.9 %collective-permute-start.7 = (f32[128,128]{1,0:T(8,128)S(1)}, f32[128,128]{1,0:T(8,128)S(1)}, u32[]{:S(2)}, u32[]{:S(2)}) collective-permute-start(f32[128,128]{1,0:T(8,128)S(1)} %collective-permute-done.4), channel_id=1, source_target_pairs={{0,16},{16,32},{32,48},{48,64},{64,80},{80,96},{96,112},{112,0},{1... | collective-permute-start | bytes 196616 | tf_op jit(solution)/shard_map/ppermute | solution.py:18
  29.3 17.5 %collective-permute-start.8 = (f32[128,64]{0,1:T(8,128)S(1)}, f32[128,64]{0,1:T(8,128)S(1)}, u32[]{:S(2)}, u32[]{:S(2)}) collective-permute-start(f32[128,64]{0,1:T(8,128)S(1)} %collective-permute-done.5), channel_id=1, source_target_pairs={{0,16},{16,32},{32,48},{48,64},{64,80},{80,96},{96,112},{112,0},{1... | collective-permute-start | bytes 98312 | tf_op jit(solution)/shard_map/ppermute | solution.py:18
  29.3 6.1 %collective-permute-start = (f32[128]{0:T(128)S(1)}, f32[128]{0:T(128)S(1)}, u32[]{:S(2)}, u32[]{:S(2)}) collective-permute-start(f32[128]{0:T(128)S(1)} %get-tuple-element.9), channel_id=1, source_target_pairs={{0,16},{16,32},{32,48},{48,64},{64,80},{80,96},{96,112},{112,0},{1... | collective-permute-start | bytes 1544 | tf_op jit(solution)/shard_map/ppermute | solution.py:18
  35.4 5.7 %collective-permute-start.3 = (f32[128]{0:T(128)S(1)}, f32[128]{0:T(128)S(1)}, u32[]{:S(2)}, u32[]{:S(2)}) collective-permute-start(f32[128]{0:T(128)S(1)} %collective-permute-done), channel_id=1, source_target_pairs={{0,16},{16,32},{32,48},{48,64},{64,80},{80,96},{96,112},{112,0},{1... | collective-permute-start | bytes 1544 | tf_op jit(solution)/shard_map/ppermute | solution.py:18
  41.1 5.7 %collective-permute-start.6 = (f32[128]{0:T(128)S(1)}, f32[128]{0:T(128)S(1)}, u32[]{:S(2)}, u32[]{:S(2)}) collective-permute-start(f32[128]{0:T(128)S(1)} %collective-permute-done.3), channel_id=1, source_target_pairs={{0,16},{16,32},{32,48},{48,64},{64,80},{80,96},{96,112},{112,0},{1... | collective-permute-start | bytes 1544 | tf_op jit(solution)/shard_map/ppermute | solution.py:18
  41.1 26.4 %collective-permute-start.12 = (f32[128,64]{0,1:T(8,128)S(1)}, f32[128,64]{0,1:T(8,128)S(1)}, u32[]{:S(2)}, u32[]{:S(2)}) collective-permute-start(f32[128,64]{0,1:T(8,128)S(1)} %broadcast_in_dim.2), channel_id=1, source_target_pairs={{0,16},{16,32},{32,48},{48,64},{64,80},{80,96},{96,112},{112,0},{1... | collective-permute-start | bytes 98312 | tf_op jit(solution)/shard_map/ppermute | solution.py:18
  46.7 37.1 %collective-permute-start.9 = (f32[128]{0:T(128)S(1)}, f32[128]{0:T(128)S(1)}, u32[]{:S(2)}, u32[]{:S(2)}) collective-permute-start(f32[128]{0:T(128)S(1)} %collective-permute-done.6), channel_id=1, source_target_pairs={{0,16},{16,32},{32,48},{48,64},{64,80},{80,96},{96,112},{112,0},{1... | collective-permute-start | bytes 1544 | tf_op jit(solution)/shard_map/ppermute | solution.py:18
  46.7 37.1 %collective-permute-start.11 = (f32[128,64]{0,1:T(8,128)S(1)}, f32[128,64]{0,1:T(8,128)S(1)}, u32[]{:S(2)}, u32[]{:S(2)}) collective-permute-start(f32[128,64]{0,1:T(8,128)S(1)} %collective-permute-done.8), channel_id=1, source_target_pairs={{0,16},{16,32},{32,48},{48,64},{64,80},{80,96},{96,112},{112,0},{1... | collective-permute-start | bytes 98312 | tf_op jit(solution)/shard_map/ppermute | solution.py:18
  46.8 26.9 %collective-permute-start.10 = (f32[128,128]{1,0:T(8,128)S(1)}, f32[128,128]{1,0:T(8,128)S(1)}, u32[]{:S(2)}, u32[]{:S(2)}) collective-permute-start(f32[128,128]{1,0:T(8,128)S(1)} %collective-permute-done.7), channel_id=1, source_target_pairs={{0,16},{16,32},{32,48},{48,64},{64,80},{80,96},{96,112},{112,0},{1... | collective-permute-start | bytes 196616 | tf_op jit(solution)/shard_map/ppermute | solution.py:18
  61.2 4.0 %copy-start = (f32[2048,192]{1,0:T(8,128)S(1)}, f32[2048,192]{1,0:T(8,128)}, u32[]{:S(2)}) copy-start(f32[2048,192]{1,0:T(8,128)} %all-gather.2.cloned.1.call-done) | copy-start | bytes 4718596
  62.9 3.3 %copy-start.1 = (f32[128,64]{0,1:T(8,128)S(1)}, f32[128,64]{0,1:T(8,128)}, u32[]{:S(2)}) copy-start(f32[128,64]{0,1:T(8,128)} %param.14) | copy-start | bytes 98308
  69.7 9.5 %collective-permute-start.13 = (f32[128,64]{0,1:T(8,128)S(1)}, f32[128,64]{0,1:T(8,128)S(1)}, u32[]{:S(2)}, u32[]{:S(2)}) collective-permute-start(f32[128,64]{0,1:T(8,128)S(1)} %convolution_add_fusion.5), channel_id=1, source_target_pairs={{0,16},{16,32},{32,48},{48,64},{64,80},{80,96},{96,112},{112,0},{1... | collective-permute-start | bytes 98312 | tf_op jit(solution)/shard_map/ppermute | solution.py:18
  81.4 9.4 %collective-permute-start.14 = (f32[128,64]{0,1:T(8,128)S(1)}, f32[128,64]{0,1:T(8,128)S(1)}, u32[]{:S(2)}, u32[]{:S(2)}) collective-permute-start(f32[128,64]{0,1:T(8,128)S(1)} %fusion.15), channel_id=1, source_target_pairs={{0,16},{16,32},{32,48},{48,64},{64,80},{80,96},{96,112},{112,0},{1... | collective-permute-start | bytes 98312 | tf_op jit(solution)/shard_map/ppermute | solution.py:18
  85.3 9.7 %copy-start.2 = (f32[128,64]{0,1:T(8,128)S(1)}, f32[128,64]{0,1:T(8,128)}, u32[]{:S(2)}) copy-start(f32[128,64]{0,1:T(8,128)} %param.13) | copy-start | bytes 98308
  86.2 16.9 %all-to-all-start = ((f32[16,128,64]{1,2,0:T(8,128)}), f32[16,128,64]{1,2,0:T(8,128)}, u32[]{:S(2)}, u32[]{:S(2)}) async-start(f32[16,128,64]{1,2,0:T(8,128)} %bitcast.82), calls=%async_computation | async-start | bytes 1048576 | tf_op jit(solution)/shard_map/all_to_all | solution.py:29
  90.4 174.7 %copy-start.4 = (f32[128,64]{0,1:T(8,128)S(1)}, f32[128,64]{0,1:T(8,128)}, u32[]{:S(2)}) copy-start(f32[128,64]{0,1:T(8,128)} %param.12) | copy-start | bytes 98308
  90.5 156.7 %all-reduce.3.cloned.1.call-start = ((), (), s32[]{:S(2)}) async-start(), calls=%async_computation.2 | async-start | bytes 262144 | tf_op jit(solution)/shard_map/psum | solution.py:89
  92.9 11.3 %collective-permute-start.15 = (f32[128,64]{0,1:T(8,128)S(1)}, f32[128,64]{0,1:T(8,128)S(1)}, u32[]{:S(2)}, u32[]{:S(2)}) collective-permute-start(f32[128,64]{0,1:T(8,128)S(1)} %fusion.18), channel_id=1, source_target_pairs={{0,80},{16,96},{32,112},{48,0},{64,16},{80,32},{96,48},{112,64},{1... | collective-permute-start | bytes 98312 | tf_op jit(solution)/shard_map/ppermute | solution.py:18
  263.2 18.0 %copy-start.3 = (f32[128,64]{0,1:T(8,128)}, f32[128,64]{0,1:T(8,128)S(1)}, u32[]{:S(2)}) copy-start(f32[128,64]{0,1:T(8,128)S(1)} %convolution_subtract_fusion) | copy-start | bytes 98308
Sparse Core Ops, SparseCore 0:
  10.4 50.6 all-gather.1
  106.8 140.2 all-reduce.2
where the time goes:
time: 289 us; the launch traced here: 288 us
  waiting for transfers between devices  194 us (67%)
  other arithmetic  30.1 us (10%)
  matrix products  29.6 us (10%)
  starting transfers between devices  15.7 us (5%)
  between operations  15 us (5%)
  local copies, waits for them, and re-layouts  3.56 us (1%)
    psum x1, waiting for transfers between devices, on_device(): lax.psum((local_gram, local_res, local_cross, local_image), ('blk', 'inne...  140 us
    ppermute x16, waiting for transfers between devices, from_behind(): lax.ppermute(value, axis, [(i, (i + by) % size) for i in range(size)])  32.6 us
    all_gather x1, waiting for transfers between devices, sent_together(): whole, at, outs = (lax.all_gather(both, axis, axis=dim, tiled=True), 0, [])  14.3 us
    another operation x6, other arithmetic, chol_solve(): factor = jnp.linalg.cholesky(matrix)  13 us
    dot_general x9, matrix products, transposed(): lax.dot_general(left, right, (((0,), (0,)), ((), ())), precision=lax.Prec...  11.7 us
    ppermute x16, starting transfers between devices, from_behind(): lax.ppermute(value, axis, [(i, (i + by) % size) for i in range(size)])  11.1 us
    another operation x4, other arithmetic, chol_solve(): return jax.scipy.linalg.cho_solve((factor, True), rhs_side)  11.1 us
    dot_general x9, matrix products, matmul(): jnp.dot(left, right, precision=lax.Precision.HIGHEST, preferred_element_t...  10.2 us
  transfers between devices with their start and end apart: 19, of which 9 were waited for; matrix products, arithmetic and copies ran while one was open for 8% of the time, Pallas kernels for 0%

commit v1 on v0

v1 whole, which is shorter than its diff:
```python
import functools
import math

import jax
import jax.numpy as jnp
from jax import lax
from jax.experimental import pallas as pl
from jax.experimental.pallas import tpu as pltpu
from jax.sharding import Mesh, PartitionSpec as P

AXES = ("y", "xl", "z", "xh", "core")
BLK = ("y", "xl")
CHIPS = ("z", "xh")
N = 128
F = 128
Q = 64
G = 8
HI = lax.Precision.HIGHEST
ROOT = math.sqrt(math.log2(math.e))
VM = pl.BlockSpec(memory_space=pltpu.VMEM)


def call(body, outs, scratch=(), flops=10**6):
    return pl.pallas_call(
        body,
        out_shape=outs,
        out_specs=jax.tree.map(lambda _: VM, outs),
        scratch_shapes=list(scratch),
        cost_estimate=pl.CostEstimate(flops=flops, bytes_accessed=10**6, transcendentals=0),
    )


def f32(*shape):
    return jax.ShapeDtypeStruct(shape, jnp.float32)


def dot(a, b, ca=1, cb=0, precision=HI):
    return lax.dot_general(
        a, b, (((ca,), (cb,)), ((), ())), precision=precision, preferred_element_type=jnp.float32
    )


def low_lanes(shape):
    return lax.broadcasted_iota(jnp.int32, shape, 1) < Q


def fold(wide):
    half = wide.shape[0] // 2
    return jnp.where(low_lanes((half, 128)), wide[:half], wide[half:])


def unfold(packed):
    return jnp.concatenate([packed[:, :Q], packed[:, Q:]], axis=0)


def prep(points, scales, direction, residual, rows, cols):
    unit = points[...] / scales[...] * ROOT
    half = 0.5 * jnp.sum(unit * unit, axis=1, keepdims=True)
    as_row = jnp.broadcast_to(half, (N, N)).T[:8]
    gram = dot(residual[...], residual[...], 0, 0)
    for i in range(G):
        rows[i] = unit
        cols[i, :N, :F] = unit
        cols[i, :N, F : F + Q] = direction[...]
        cols[i, :Q, F + Q :] = gram
        cols[i, N:, :F] = as_row


def split(value):
    top = value.astype(jnp.bfloat16)
    rest = value - top.astype(jnp.float32)
    mid = rest.astype(jnp.bfloat16)
    low = (rest - mid.astype(jnp.float32)).astype(jnp.bfloat16)
    return top, mid, low


def products(first, tile, rows, cols, *refs):
    before, out, right, dirs, halves, left = refs if not first else (None, *refs)
    for j in range(G):
        at = slice(j * N, (j + 1) * N)
        top, mid, low = split(cols[j, :N, :F])
        right[at] = jnp.concatenate([top, mid, top, low, top, mid], axis=1)
        high, rest, _ = split(cols[j, :N, F : F + Q])
        dirs[at] = jnp.concatenate([high, rest], axis=1)
        halves[:, at] = cols[j, N:, :F]
    per = tile // N

    def step(i, carry):
        unit = rows[pl.ds(i * per, per)].reshape(tile, F)
        top, mid, low = split(unit)
        left[...] = jnp.concatenate([top, top, mid, top, low, mid], axis=1)
        half = 0.5 * jnp.sum(unit * unit, axis=1, keepdims=True)
        total = jnp.zeros((tile, 2 * Q), jnp.float32)
        for j in range(4):
            at = slice(j * 256, (j + 1) * 256)
            inner = dot(left[...], right[at], 1, 1, None)
            kernel = jnp.exp2(inner - half - halves[0:1, at])
            high = kernel.astype(jnp.bfloat16)
            rest = (kernel - high.astype(jnp.float32)).astype(jnp.bfloat16)
            total += dot(high, dirs[at], 1, 0, None) + dot(rest, dirs[at], 1, 0, None)
        if first:
            out[pl.ds(i * tile, tile)] = total
        else:
            total += before[pl.ds(i * tile, tile)]
            total += pltpu.roll(total, Q, 1)
            for b in range(per):
                out[i * per + b, :Q] = fold(total[b * N : (b + 1) * N])
        return carry

    lax.fori_loop(0, (G * N) // tile, step, 0)


def products_first(tile, rows, cols, *refs):
    products(True, tile, rows, cols, *refs)


def products_last(tile, rows, cols, mine, before, out, right, dirs, halves, left):
    products(False, tile, rows, cols, before, out, right, dirs, halves, left)
    gram = cols[0, :Q, F + Q :] + mine[0, :Q, F + Q :]
    for j in range(1, G):
        gram += cols[j, :Q, F + Q :] + mine[j, :Q, F + Q :]
    packed = fold(jnp.concatenate([gram, gram], axis=1))
    for j in range(G):
        out[j, Q:] = packed


def summed(pieces):
    total = pieces[0]
    for j in range(1, G):
        total += pieces[j]
    return total


def grams(pieces, noise, direction, residual, image_out, gram_out, sums):
    total = summed(pieces)
    image = unfold(total[:Q]) + noise[0, 0] * direction[...]
    image_out[...] = image
    gram_out[...] = unfold(total[Q:])
    side = jnp.concatenate([direction[...], residual[...]], axis=1)
    sums[:Q] = dot(image, side, 0, 0)
    square = dot(image, image, 0, 0)
    sums[Q:] = fold(jnp.concatenate([square, square], axis=1))


def eliminate(matrix):
    slabs = [matrix[8 * r : 8 * r + 8] for r in range(8)]
    sub = lax.broadcasted_iota(jnp.int32, (8, 128), 0)
    for k in range(8):
        spread = [
            [jnp.broadcast_to(slabs[r][:, 8 * k + j : 8 * k + j + 1], (8, 128)) for j in range(8)]
            for r in range(8)
        ]
        own, pivot = spread[k], slabs[k]
        for j in range(8):
            inverse = 1.0 / jnp.broadcast_to(own[j][j : j + 1], (8, 128))
            at = sub == j

            def cleared(value):
                row = jnp.broadcast_to(value[j : j + 1], (8, 128)) * inverse
                return jnp.where(at, row, value - own[j] * row)

            pivot = cleared(pivot)
            own = own[: j + 1] + [cleared(c) for c in own[j + 1 :]]
        for r in range(8):
            if r != k:
                for j in range(8):
                    slabs[r] = slabs[r] - spread[r][j] * jnp.broadcast_to(
                        pivot[j : j + 1], (8, 128)
                    )
        slabs[k] = pivot
    return jnp.concatenate(slabs, axis=0)[:, Q:]


def invert(gram, out):
    eye = lax.broadcasted_iota(jnp.int32, (Q, Q), 0) == lax.broadcasted_iota(jnp.int32, (Q, Q), 1)
    out[...] = eliminate(jnp.concatenate([gram[...], eye.astype(jnp.float32)], axis=1))


def pair_sum(a, b, out):
    total = a[...] + b[...]
    for j in range(G):
        out[j] = total


def chip_sum(pieces, out):
    total = summed(pieces)
    for j in range(G):
        out[j] = total


def finish(pieces, gram, inverse, image, iterate, residual, direction, x_out, r_out, d_out):
    total = summed(pieces)
    raw, cross = total[:Q, :Q], total[:Q, Q:]
    square = unfold(total[Q:])
    res = gram[...]
    step = eliminate(jnp.concatenate([0.5 * (raw + raw.T), res], axis=1))
    x_out[...] = iterate[...] + dot(direction[...], step)
    new_res = residual[...] - dot(image[...], step)
    r_out[...] = new_res
    term = dot(step, cross, 0, 0)
    new_gram = res - term - term.T + dot(step, dot(square, step), 0, 0)
    d_out[...] = new_res + dot(direction[...], dot(inverse[...], new_gram))


def swapped(value):
    return lax.ppermute(value, "core", [(0, 1), (1, 0)])


def exchanged(value, axes):
    return lax.all_to_all(value, axes, 0, 0, tiled=True)


def on_device(points, lengthscales, noise_level, iterate, residual, direction):
    rows, cols = call(prep, [f32(G, N, F), f32(G, N + 8, 256)])(
        points, lengthscales.reshape(1, F), direction, residual
    )
    cols = exchanged(cols, BLK)
    rows = exchanged(rows, CHIPS)
    other = swapped(cols)
    tile = 512
    scratch = [
        pltpu.VMEM((G * N, 6 * F), jnp.bfloat16),
        pltpu.VMEM((G * N, 2 * Q), jnp.bfloat16),
        pltpu.VMEM((8, G * N), jnp.float32),
        pltpu.VMEM((tile, 6 * F), jnp.bfloat16),
    ]
    part = call(
        functools.partial(products_first, tile), f32(G * N, 2 * Q), scratch, flops=4 * 10**9
    )(rows, cols)
    sent = call(
        functools.partial(products_last, tile), f32(G, Q + Q // 2, 128), scratch, flops=4 * 10**9
    )(rows, other, cols, part)
    pieces = exchanged(sent, CHIPS)
    image, gram, sums = call(grams, [f32(N, Q), f32(Q, Q), f32(Q + Q // 2, 128)])(
        pieces, noise_level.reshape(1, 1), direction, residual
    )
    both = call(pair_sum, f32(G, Q + Q // 2, 128))(sums, swapped(sums))
    inverse = call(invert, f32(Q, Q), flops=10**8)(gram)
    by_chip = call(chip_sum, f32(G, Q + Q // 2, 128))(exchanged(both, CHIPS))
    whole = exchanged(by_chip, BLK)
    return tuple(
        call(finish, [f32(N, Q)] * 3)(whole, gram, inverse, image, iterate, residual, direction)
    )


def solution(mesh):
    fine = Mesh(mesh.devices.reshape(4, 2, 4, 2, 2), AXES)
    split_rows = P(AXES, None)
    return jax.shard_map(
        on_device,
        mesh=fine,
        in_specs=(split_rows, P(), P(), split_rows, split_rows, split_rows),
        out_specs=(split_rows,) * 3,
        check_vma=False,
    )
```

time: 289 us -> 124 us (0.43)
  waiting for transfers between devices: 194 us -> 14.9 us
  blocking collectives: 0 us -> 57 us
  Pallas kernels: 0 us -> 31 us
  other arithmetic: 30.1 us -> 0 us
  matrix products: 29.6 us -> 0 us
  between operations: 15 us -> 1.32 us
  starting transfers between devices: 15.7 us -> 6.91 us
  local copies, waits for them, and re-layouts: 3.56 us -> 11.4 us
    psum x1 -> x0, waiting for transfers between devices: 140 us -> none  [on_device(): lax.psum((local_gram, local_res, local_cross, local_image), ('blk', 'inne...]
    all_to_all x0 -> x3, blocking collectives: none -> 57 us  [exchanged(): return lax.all_to_all(value, axes, 0, 0, tiled=True)]
    ppermute x16 -> x2, waiting for transfers between devices: 32.6 us -> 1.44 us  [swapped(): return lax.ppermute(value, 'core', [(0, 1), (1, 0)])]
    pallas_call x0 -> x8, Pallas kernels: none -> 31 us  [the longest x1 8.35 us: on_device(): call(functools.partial(products_last, tile), f32(G, Q + Q // 2, 128), scr...]
    dot_general x23 -> x0, matrix products: 28.1 us -> none  [the longest x9 11.7 us: transposed(): lax.dot_general(left, right, (((0,), (0,)), ((), ())), precision=lax.Prec...]
    another operation x10 -> x0, other arithmetic: 24.1 us -> none  [the longest x6 13 us: chol_solve(): factor = jnp.linalg.cholesky(matrix)]
    all_gather x1 -> x0, waiting for transfers between devices: 14.3 us -> none  [sent_together(): whole, at, outs = (lax.all_gather(both, axis, axis=dim, tiled=True), 0, [])]
    ppermute x16 -> x2, starting transfers between devices: 11.1 us -> 0.01 us  [swapped(): return lax.ppermute(value, 'core', [(0, 1), (1, 0)])]
  transfers between devices with their start and end apart: 19 -> 4, of which waited for: 9 -> 3; matrix products, arithmetic and copies ran while one was open for 8% -> 1% of each run, Pallas kernels for 0% -> 8%
where the time goes in v1:
time: 124 us; the launch traced here: 123 us
  blocking collectives  57 us (46%)
  Pallas kernels  31 us (25%)
  waiting for transfers between devices  14.9 us (12%)
  local copies, waits for them, and re-layouts  11.4 us (9%)
  starting transfers between devices  6.91 us (6%)
  between operations  1.32 us (1%)
    all_to_all x3, blocking collectives, exchanged(): return lax.all_to_all(value, axes, 0, 0, tiled=True)  57 us
    all_to_all x2, waiting for transfers between devices, exchanged(): return lax.all_to_all(value, axes, 0, 0, tiled=True)  13.5 us
    pallas_call x1, Pallas kernels, on_device(): call(functools.partial(products_last, tile), f32(G, Q + Q // 2, 128), scr...  8.35 us
    all_to_all x2, starting transfers between devices, exchanged(): return lax.all_to_all(value, axes, 0, 0, tiled=True)  6.9 us
    unnamed x17, local copies, waits for them, and re-layouts  6.79 us
    pallas_call x1, Pallas kernels, on_device(): call(functools.partial(products_first, tile), f32(G * N, 2 * Q), scratch,...  6.41 us
    pallas_call x1, Pallas kernels, on_device(): call(finish, [f32(N, Q)] * 3)  5.23 us
    pallas_call x3, local copies, waits for them, and re-layouts, on_device(): call(finish, [f32(N, Q)] * 3)  4.61 us
  transfers between devices with their start and end apart: 4, of which 3 were waited for; matrix products, arithmetic and copies ran while one was open for 1% of the time, Pallas kernels for 8%

profile of v1, /device:TPU:0, one launch (start us, length us, event | category | flops | bytes accessed | tf_op | source)
XLA Modules:
  0.0 122.5 jit_solution(9567400325199188397)
XLA Ops:
  0.6 1.5 %copy.10.residual = f32[128,64]{1,0:T(8,128)} copy(f32[128,64]{0,1:T(8,128)} %param.10) | data formatting | bytes 65536 | tf_op args[4]
  2.1 1.5 %copy.9.direction = f32[128,64]{1,0:T(8,128)} copy(f32[128,64]{0,1:T(8,128)} %param.11) | data formatting | bytes 65536 | tf_op args[5]
  3.6 2.2 %shard_map.85 = (f32[8,128,128]{2,1,0:T(8,128)}, f32[8,136,256]{2,1,0:T(8,128)}) custom-call(f32[128,128]{1,0:T(8,128)} %points.1, f32[1,128]{1,0:T(1,128)} %bitcast.3, f32[128,64]{1,0:T(8,128)} %copy.9.direction, f32[128,64]{1,0:T(8,128)} %copy.10.residual), custom_call_target="tpu_custom_call" | custom-call | flops 1000000 | bytes 1000000 | tf_op jit(solution)/shard_map/pallas_call | solution.py:214
  5.8 0.0 copy-start.3
  5.8 22.2 %all_to_all.25.cols.mine = f32[8,136,256]{2,1,0:T(8,128)S(1)} all-to-all(f32[8,136,256]{2,1,0:T(8,128)} %get-tuple-element.9), channel_id=1, replica_groups=mesh['y'=4,'xl'=2,'z'=4,'xh'=2,'core'=2] {'y','xl'}, dimensions={0} | all-to-all | bytes 2228224 | tf_op jit(solution)/shard_map/all_to_all | solution.py:210
  28.1 0.0 copy-start.2
  28.1 0.0 collective-permute-start
  28.1 0.0 copy-done.3
  28.1 19.6 %all_to_all.26.rows = f32[8,128,128]{2,1,0:T(8,128)} all-to-all(f32[8,128,128]{2,1,0:T(8,128)S(1)} %copy-done.3), channel_id=1, replica_groups=mesh['y'=4,'xl'=2,'z'=4,'xh'=2,'core'=2] {'z','xh'}, dimensions={0} | all-to-all | bytes 1048576 | tf_op jit(solution)/shard_map/all_to_all | solution.py:210
  47.7 0.0 copy-done.2
  47.7 6.4 %shard_map.86.before = f32[1024,128]{1,0:T(8,128)} custom-call(f32[8,128,128]{2,1,0:T(8,128)} %all_to_all.26.rows, f32[8,136,256]{2,1,0:T(8,128)} %copy-done.2), custom_call_target="tpu_custom_call" | custom-call | flops 4000000000 | bytes 1000000 | tf_op jit(solution)/shard_map/pallas_call | solution.py:227
  54.1 0.0 collective-permute-done.cols
  54.1 0.0 copy-start.6
  54.1 1.0 copy-done.6
  55.1 8.3 %shard_map.87 = f32[8,96,128]{2,1,0:T(8,128)} custom-call(f32[8,128,128]{2,1,0:T(8,128)} %all_to_all.26.rows, f32[8,136,256]{2,1,0:T(8,128)} %copy-done.6, f32[8,136,256]{2,1,0:T(8,128)} %copy-done.2, f32[1024,128]{1,0:T(8,128)} %shard_map.86.before), custom_call_target="tpu_custom_call" | custom-call | flops 4000000000 | bytes 1000000 | tf_op jit(solution)/shard_map/pallas_call | solution.py:230
  63.5 3.5 %all-to-all-start.2 = ((f32[8,96,128]{2,1,0:T(8,128)}), f32[8,96,128]{2,1,0:T(8,128)S(1)}, u32[]{:S(2)}, u32[]{:S(2)}) async-start(f32[8,96,128]{2,1,0:T(8,128)} %shard_map.87), calls=%async_computation.2 | async-start | bytes 786432 | tf_op jit(solution)/shard_map/all_to_all | solution.py:210
  67.6 9.3 %all-to-all-done.2.pieces = f32[8,96,128]{2,1,0:T(8,128)S(1)} async-done(((f32[8,96,128]{2,1,0:T(8,128)}), f32[8,96,128]{2,1,0:T(8,128)S(1)}, u32[]{:S(2)}, u32[]{:S(2)}) %all-to-all-start.2) | async-done | bytes 393248 | tf_op jit(solution)/shard_map/all_to_all | solution.py:210
  76.8 0.0 copy-start
  76.8 0.7 copy-done
  77.6 2.1 %shard_map.88 = (f32[128,64]{1,0:T(8,128)}, f32[64,64]{1,0:T(8,128)}, f32[96,128]{1,0:T(8,128)}) custom-call(f32[8,96,128]{2,1,0:T(8,128)} %copy-done, f32[1,1]{1,0:T(1,128)} %bitcast.2.noise, f32[128,64]{1,0:T(8,128)} %copy.9.direction, f32[128,64]{1,0:T(8,128)} %copy.10.residual), custom_call_target="tpu_custom_call" | custom-call | flops 1000000 | bytes 1000000 | tf_op jit(solution)/shard_map/pallas_call | solution.py:234
  79.7 0.0 collective-permute-start.1
  79.7 1.4 %collective-permute-done.1.b = f32[96,128]{1,0:T(8,128)S(1)} collective-permute-done((f32[96,128]{1,0:T(8,128)}, f32[96,128]{1,0:T(8,128)S(1)}, u32[]{:S(2)}, u32[]{:S(2)}) %collective-permute-start.1) | collective-permute-done | bytes 49184 | tf_op jit(solution)/shard_map/ppermute | solution.py:206
  81.1 0.0 copy-start.4
  81.1 0.6 copy-done.4
  81.7 1.6 %shard_map.89 = f32[8,96,128]{2,1,0:T(8,128)} custom-call(f32[96,128]{1,0:T(8,128)} %get-tuple-element.10.a, f32[96,128]{1,0:T(8,128)} %copy-done.4), custom_call_target="tpu_custom_call" | custom-call | flops 1000000 | bytes 1000000 | tf_op jit(solution)/shard_map/pallas_call | solution.py:237
  83.3 0.0 copy-start.5
  83.3 15.1 %all_to_all.27.pieces = f32[8,96,128]{2,1,0:T(8,128)} all-to-all(f32[8,96,128]{2,1,0:T(8,128)} %shard_map.89), channel_id=1, replica_groups=mesh['y'=4,'xl'=2,'z'=4,'xh'=2,'core'=2] {'z','xh'}, dimensions={0} | all-to-all | bytes 786432 | tf_op jit(solution)/shard_map/all_to_all | solution.py:210
  98.4 1.8 %shard_map.90 = f32[8,96,128]{2,1,0:T(8,128)} custom-call(f32[8,96,128]{2,1,0:T(8,128)} %all_to_all.27.pieces), custom_call_target="tpu_custom_call" | custom-call | flops 1000000 | bytes 1000000 | tf_op jit(solution)/shard_map/pallas_call | solution.py:239
  100.2 3.5 %all-to-all-start.4 = ((f32[8,96,128]{2,1,0:T(8,128)}), f32[8,96,128]{2,1,0:T(8,128)S(1)}, u32[]{:S(2)}, u32[]{:S(2)}) async-start(f32[8,96,128]{2,1,0:T(8,128)} %shard_map.90), calls=%async_computation.4 | async-start | bytes 786432 | tf_op jit(solution)/shard_map/all_to_all | solution.py:210
  103.7 0.0 copy-done.5
  103.7 0.7 copy.13.iterate
  104.4 3.3 %shard_map.91.inverse = f32[64,64]{1,0:T(8,128)} custom-call(f32[64,64]{1,0:T(8,128)} %get-tuple-element.11.gram), custom_call_target="tpu_custom_call" | custom-call | flops 100000000 | bytes 1000000 | tf_op jit(solution)/shard_map/pallas_call | solution.py:238
  107.7 4.2 %all-to-all-done.4.pieces = f32[8,96,128]{2,1,0:T(8,128)S(1)} async-done(((f32[8,96,128]{2,1,0:T(8,128)}), f32[8,96,128]{2,1,0:T(8,128)S(1)}, u32[]{:S(2)}, u32[]{:S(2)}) %all-to-all-start.4) | async-done | bytes 393248 | tf_op jit(solution)/shard_map/all_to_all | solution.py:210
  111.9 0.0 copy-start.1
  111.9 0.7 copy-done.1
  112.7 5.2 %shard_map.92 = (f32[128,64]{1,0:T(8,128)}, f32[128,64]{1,0:T(8,128)}, f32[128,64]{1,0:T(8,128)}) custom-call(f32[8,96,128]{2,1,0:T(8,128)} %copy-done.1, f32[64,64]{1,0:T(8,128)} %get-tuple-element.11.gram, f32[64,64]{1,0:T(8,128)} %shard_map.91.inverse, f32[128,64]{1,0:T(8,128)} %get-tuple-element.12.image, f32[128,64]{1,0:T(8,128)} %copy.13.iterate, ...), custom_call_target="tpu_custom_call" | custom-call | flops 1000000 | bytes 1000000 | tf_op jit(solution)/shard_map/pallas_call | solution.py:242
  117.9 1.5 %copy.16 = f32[128,64]{0,1:T(8,128)} copy(f32[128,64]{1,0:T(8,128)} %get-tuple-element.13) | data formatting | bytes 65536 | tf_op jit(solution)/shard_map/pallas_call | solution.py:242
  119.4 1.5 %copy.17 = f32[128,64]{0,1:T(8,128)} copy(f32[128,64]{1,0:T(8,128)} %get-tuple-element.14) | data formatting | bytes 65536 | tf_op jit(solution)/shard_map/pallas_call | solution.py:242
  121.0 1.5 %copy.18 = f32[128,64]{0,1:T(8,128)} copy(f32[128,64]{1,0:T(8,128)} %get-tuple-element.15) | data formatting | bytes 65536 | tf_op jit(solution)/shard_map/pallas_call | solution.py:242
Async XLA Ops:
  5.8 22.3 %copy-start.3 = (f32[8,128,128]{2,1,0:T(8,128)S(1)}, f32[8,128,128]{2,1,0:T(8,128)}, u32[]{:S(2)}) copy-start(f32[8,128,128]{2,1,0:T(8,128)} %get-tuple-element.8) | copy-start | bytes 1572868
  28.1 19.6 %copy-start.2 = (f32[8,136,256]{2,1,0:T(8,128)}, f32[8,136,256]{2,1,0:T(8,128)S(1)}, u32[]{:S(2)}) copy-start(f32[8,136,256]{2,1,0:T(8,128)S(1)} %all_to_all.25.cols.mine) | copy-start | bytes 3342340
  28.1 26.0 %collective-permute-start = (f32[8,136,256]{2,1,0:T(8,128)S(1)}, f32[8,136,256]{2,1,0:T(8,128)S(1)}, u32[]{:S(2)}, u32[]{:S(2)}) collective-permute-start(f32[8,136,256]{2,1,0:T(8,128)S(1)} %all_to_all.25.cols.mine), channel_id=1, source_target_pairs={{0,1},{1,0},{2,3},{3,2},{4,5},{5,4},{6,7},{7,6},{8,9},{9,8},{10,11... | collective-permute-start | bytes 3342344 | tf_op jit(solution)/shard_map/ppermute | solution.py:206
  54.1 1.0 copy-start.6
  63.5 13.4 %all-to-all-start.2 = ((f32[8,96,128]{2,1,0:T(8,128)}), f32[8,96,128]{2,1,0:T(8,128)S(1)}, u32[]{:S(2)}, u32[]{:S(2)}) async-start(f32[8,96,128]{2,1,0:T(8,128)} %shard_map.87), calls=%async_computation.2 | async-start | bytes 786432 | tf_op jit(solution)/shard_map/all_to_all | solution.py:210
  76.8 0.7 copy-start
  79.7 1.4 %collective-permute-start.1 = (f32[96,128]{1,0:T(8,128)}, f32[96,128]{1,0:T(8,128)S(1)}, u32[]{:S(2)}, u32[]{:S(2)}) collective-permute-start(f32[96,128]{1,0:T(8,128)} %get-tuple-element.10.a), channel_id=1, source_target_pairs={{0,1},{1,0},{2,3},{3,2},{4,5},{5,4},{6,7},{7,6},{8,9},{9,8},{10,11... | collective-permute-start | bytes 147464 | tf_op jit(solution)/shard_map/ppermute | solution.py:206
  81.1 0.6 copy-start.4
  83.3 20.3 %copy-start.5 = (f32[128,64]{0,1:T(8,128)S(1)}, f32[128,64]{0,1:T(8,128)}, u32[]{:S(2)}) copy-start(f32[128,64]{0,1:T(8,128)} %param.9) | copy-start | bytes 98308
  100.2 11.7 %all-to-all-start.4 = ((f32[8,96,128]{2,1,0:T(8,128)}), f32[8,96,128]{2,1,0:T(8,128)S(1)}, u32[]{:S(2)}, u32[]{:S(2)}) async-start(f32[8,96,128]{2,1,0:T(8,128)} %shard_map.90), calls=%async_computation.4 | async-start | bytes 786432 | tf_op jit(solution)/shard_map/all_to_all | solution.py:210
  111.9 0.7 copy-start.1

commit v2 on v1

--- a/solution.py
+++ b/solution.py
@@ -17,15 +17,19 @@
 G = 8
 HI = lax.Precision.HIGHEST
 ROOT = math.sqrt(math.log2(math.e))
+DIRS = N + Q
+GRAM = DIRS + Q // 2
+ROWS = GRAM + 8
 VM = pl.BlockSpec(memory_space=pltpu.VMEM)
 
 
-def call(body, outs, scratch=(), flops=10**6):
+def call(body, outs, scratch=(), flops=10**6, room=4):
     return pl.pallas_call(
         body,
         out_shape=outs,
         out_specs=jax.tree.map(lambda _: VM, outs),
         scratch_shapes=list(scratch),
+        compiler_params=pltpu.CompilerParams(vmem_limit_bytes=room * 2**20),
         cost_estimate=pl.CostEstimate(flops=flops, bytes_accessed=10**6, transcendentals=0),
     )
 
@@ -57,13 +61,14 @@
     unit = points[...] / scales[...] * ROOT
     half = 0.5 * jnp.sum(unit * unit, axis=1, keepdims=True)
     as_row = jnp.broadcast_to(half, (N, N)).T[:8]
-    gram = dot(residual[...], residual[...], 0, 0)
+    twice = jnp.concatenate([residual[...], residual[...]], axis=0)
+    gram = fold(dot(residual[...], twice, 1, 1))
     for i in range(G):
         rows[i] = unit
-        cols[i, :N, :F] = unit
-        cols[i, :N, F : F + Q] = direction[...]
-        cols[i, :Q, F + Q :] = gram
-        cols[i, N:, :F] = as_row
+        cols[i, :N] = unit
+        cols[i, N:DIRS] = direction[...]
+        cols[i, DIRS:GRAM] = gram
+        cols[i, GRAM:] = as_row
 
 
 def split(value):
@@ -78,11 +83,11 @@
     before, out, right, dirs, halves, left = refs if not first else (None, *refs)
     for j in range(G):
         at = slice(j * N, (j + 1) * N)
-        top, mid, low = split(cols[j, :N, :F])
+        top, mid, low = split(cols[j, :N])
         right[at] = jnp.concatenate([top, mid, top, low, top, mid], axis=1)
-        high, rest, _ = split(cols[j, :N, F : F + Q])
-        dirs[at] = jnp.concatenate([high, rest], axis=1)
-        halves[:, at] = cols[j, N:, :F]
+        high, rest, _ = split(cols[j, N:DIRS])
+        dirs[:, at] = jnp.concatenate([high, rest], axis=0)
+        halves[:, at] = cols[j, GRAM:]
     per = tile // N
 
     def step(i, carry):
@@ -97,7 +102,7 @@
             kernel = jnp.exp2(inner - half - halves[0:1, at])
             high = kernel.astype(jnp.bfloat16)
             rest = (kernel - high.astype(jnp.float32)).astype(jnp.bfloat16)
-            total += dot(high, dirs[at], 1, 0, None) + dot(rest, dirs[at], 1, 0, None)
+            total += dot(high, dirs[:, at], 1, 1, None) + dot(rest, dirs[:, at], 1, 1, None)
         if first:
             out[pl.ds(i * tile, tile)] = total
         else:
@@ -116,12 +121,11 @@
 
 def products_last(tile, rows, cols, mine, before, out, right, dirs, halves, left):
     products(False, tile, rows, cols, before, out, right, dirs, halves, left)
-    gram = cols[0, :Q, F + Q :] + mine[0, :Q, F + Q :]
+    gram = cols[0, DIRS:GRAM] + mine[0, DIRS:GRAM]
     for j in range(1, G):
-        gram += cols[j, :Q, F + Q :] + mine[j, :Q, F + Q :]
-    packed = fold(jnp.concatenate([gram, gram], axis=1))
-    for j in range(G):
-        out[j, Q:] = packed
+        gram += cols[j, DIRS:GRAM] + mine[j, DIRS:GRAM]
+    for j in range(G):
+        out[j, Q:] = gram
 
 
 def summed(pieces):
@@ -133,13 +137,14 @@
 
 def grams(pieces, noise, direction, residual, image_out, gram_out, sums):
     total = summed(pieces)
-    image = unfold(total[:Q]) + noise[0, 0] * direction[...]
+    turned = total[:Q].T
+    image = jnp.concatenate([turned[:Q], turned[Q:]], axis=1) + noise[0, 0] * direction[...]
     image_out[...] = image
     gram_out[...] = unfold(total[Q:])
-    side = jnp.concatenate([direction[...], residual[...]], axis=1)
-    sums[:Q] = dot(image, side, 0, 0)
-    square = dot(image, image, 0, 0)
-    sums[Q:] = fold(jnp.concatenate([square, square], axis=1))
+    side = jnp.concatenate([direction[...], residual[...], image, image], axis=0)
+    products_of = dot(image, side, 1, 1)
+    sums[:Q] = products_of[:, : 2 * Q]
+    sums[Q:] = fold(products_of[:, 2 * Q :])
 
 
 def eliminate(matrix):
@@ -194,12 +199,12 @@
     square = unfold(total[Q:])
     res = gram[...]
     step = eliminate(jnp.concatenate([0.5 * (raw + raw.T), res], axis=1))
-    x_out[...] = iterate[...] + dot(direction[...], step)
-    new_res = residual[...] - dot(image[...], step)
+    x_out[...] = iterate[...] + dot(step, direction[...], 0, 0)
+    new_res = residual[...] - dot(step, image[...], 0, 0)
     r_out[...] = new_res
     term = dot(step, cross, 0, 0)
     new_gram = res - term - term.T + dot(step, dot(square, step), 0, 0)
-    d_out[...] = new_res + dot(direction[...], dot(inverse[...], new_gram))
+    d_out[...] = new_res + dot(dot(inverse[...], new_gram), direction[...], 0, 0)
 
 
 def swapped(value):
@@ -211,7 +216,8 @@
 
 
 def on_device(points, lengthscales, noise_level, iterate, residual, direction):
-    rows, cols = call(prep, [f32(G, N, F), f32(G, N + 8, 256)])(
+    iterate, residual, direction = iterate.T, residual.T, direction.T
+    rows, cols = call(prep, [f32(G, N, F), f32(G, ROWS, 128)])(
         points, lengthscales.reshape(1, F), direction, residual
     )
     cols = exchanged(cols, BLK)
@@ -220,27 +226,28 @@
     tile = 512
     scratch = [
         pltpu.VMEM((G * N, 6 * F), jnp.bfloat16),
-        pltpu.VMEM((G * N, 2 * Q), jnp.bfloat16),
+        pltpu.VMEM((2 * Q, G * N), jnp.bfloat16),
         pltpu.VMEM((8, G * N), jnp.float32),
         pltpu.VMEM((tile, 6 * F), jnp.bfloat16),
     ]
     part = call(
-        functools.partial(products_first, tile), f32(G * N, 2 * Q), scratch, flops=4 * 10**9
+        functools.partial(products_first, tile), f32(G * N, 2 * Q), scratch, 4 * 10**9, 16
     )(rows, cols)
     sent = call(
-        functools.partial(products_last, tile), f32(G, Q + Q // 2, 128), scratch, flops=4 * 10**9
+        functools.partial(products_last, tile), f32(G, Q + Q // 2, 128), scratch, 4 * 10**9, 16
     )(rows, other, cols, part)
     pieces = exchanged(sent, CHIPS)
-    image, gram, sums = call(grams, [f32(N, Q), f32(Q, Q), f32(Q + Q // 2, 128)])(
+    image, gram, sums = call(grams, [f32(Q, N), f32(Q, Q), f32(Q + Q // 2, 128)])(
         pieces, noise_level.reshape(1, 1), direction, residual
     )
     both = call(pair_sum, f32(G, Q + Q // 2, 128))(sums, swapped(sums))
     inverse = call(invert, f32(Q, Q), flops=10**8)(gram)
     by_chip = call(chip_sum, f32(G, Q + Q // 2, 128))(exchanged(both, CHIPS))
     whole = exchanged(by_chip, BLK)
-    return tuple(
-        call(finish, [f32(N, Q)] * 3)(whole, gram, inverse, image, iterate, residual, direction)
-    )
+    outs = call(finish, [f32(Q, N)] * 3)(
+        whole, gram, inverse, image, iterate, residual, direction
+    )
+    return tuple(o.T for o in outs)
 
 
 def solution(mesh):

time: 124 us -> 99.7 us (0.80)
  Pallas kernels: 31 us -> 18 us
  local copies, waits for them, and re-layouts: 11.4 us -> 3.02 us
  blocking collectives: 57 us -> 52.9 us
  waiting for transfers between devices: 14.9 us -> 16.8 us
    pallas_call x3, Pallas kernels: 9.56 us -> 4.86 us  [the longest x1 4.18 us: on_device(): call(finish, [f32(Q, N)] * 3)]
    pallas_call x3 -> x0, local copies, waits for them, and re-layouts: 4.61 us -> none  [on_device(): call(finish, [f32(N, Q)] * 3)]
    all_to_all x3, blocking collectives: 57 us -> 52.9 us  [exchanged(): return lax.all_to_all(value, axes, 0, 0, tiled=True)]
    unnamed x17 -> x14, local copies, waits for them, and re-layouts: 6.79 us -> 3.02 us
    pallas_call x1, Pallas kernels: 6.41 us -> 4.11 us  [on_device(): call(functools.partial(products_first, tile), f32(G * N, 2 * Q), scratch,...]
    all_to_all x2, waiting for transfers between devices: 13.5 us -> 15.6 us  [exchanged(): return lax.all_to_all(value, axes, 0, 0, tiled=True)]
    pallas_call x1, Pallas kernels: 8.35 us -> 6.33 us  [on_device(): call(functools.partial(products_last, tile), f32(G, Q + Q // 2, 128), scr...]
    pallas_call x1, Pallas kernels: 1.59 us -> 0.03 us  [on_device(): both = call(pair_sum, f32(G, Q + Q // 2, 128))(sums, swapped(sums))]
  transfers between devices with their start and end apart: 4 -> 4, of which waited for: 3 -> 3; matrix products, arithmetic and copies ran while one was open for 1% -> 0% of each run, Pallas kernels for 8% -> 6%
where the time goes in v2:
time: 99.7 us; the launch traced here: 99.1 us
  blocking collectives  52.9 us (53%)
  Pallas kernels  18 us (18%)
  waiting for transfers between devices  16.8 us (17%)
  starting transfers between devices  7.12 us (7%)
  local copies, waits for them, and re-layouts  3.02 us (3%)
  between operations  1.35 us (1%)
    all_to_all x3, blocking collectives, exchanged(): return lax.all_to_all(value, axes, 0, 0, tiled=True)  52.9 us
    all_to_all x2, waiting for transfers between devices, exchanged(): return lax.all_to_all(value, axes, 0, 0, tiled=True)  15.6 us
    all_to_all x2, starting transfers between devices, exchanged(): return lax.all_to_all(value, axes, 0, 0, tiled=True)  7.03 us
    pallas_call x1, Pallas kernels, on_device(): call(functools.partial(products_last, tile), f32(G, Q + Q // 2, 128), scr...  6.33 us
    pallas_call x1, Pallas kernels, on_device(): call(finish, [f32(Q, N)] * 3)  4.18 us
    pallas_call x1, Pallas kernels, on_device(): call(functools.partial(products_first, tile), f32(G * N, 2 * Q), scratch,...  4.11 us
    unnamed x14, local copies, waits for them, and re-layouts  3.02 us
  transfers between devices with their start and end apart: 4, of which 3 were waited for; matrix products, arithmetic and copies ran while one was open for 0% of the time, Pallas kernels for 6%

profile of v2, /device:TPU:0, one launch (start us, length us, event | category | flops | bytes accessed | tf_op | source)
XLA Modules:
  0.0 99.1 jit_solution(10647554263199348608)
XLA Ops:
  0.6 0.0 copy-start.6
  0.6 0.6 copy-done.6
  1.3 0.0 copy-start
  1.3 0.8 copy-done
  2.0 0.0 copy-start.2
  2.0 0.8 copy-done.2
  2.8 0.0 copy-start.4
  2.8 0.8 copy-done.4
  3.6 0.3 shard_map.85
  3.9 20.0 %all_to_all.25.cols.mine = f32[8,232,128]{2,1,0:T(8,128)S(1)} all-to-all(f32[8,232,128]{2,1,0:T(8,128)S(1)} %get-tuple-element.12), channel_id=1, replica_groups=mesh['y'=4,'xl'=2,'z'=4,'xh'=2,'core'=2] {'y','xl'}, dimensions={0} | all-to-all | bytes 1900544 | tf_op jit(solution)/shard_map/all_to_all | solution.py:215
  23.9 0.0 collective-permute-start
  23.9 19.5 %all_to_all.26.rows = f32[8,128,128]{2,1,0:T(8,128)S(1)} all-to-all(f32[8,128,128]{2,1,0:T(8,128)S(1)} %get-tuple-element.11), channel_id=1, replica_groups=mesh['y'=4,'xl'=2,'z'=4,'xh'=2,'core'=2] {'z','xh'}, dimensions={0} | all-to-all | bytes 1048576 | tf_op jit(solution)/shard_map/all_to_all | solution.py:215
  43.5 4.1 %shard_map.86.before = f32[1024,128]{1,0:T(8,128)S(1)} custom-call(f32[8,128,128]{2,1,0:T(8,128)S(1)} %all_to_all.26.rows, f32[8,232,128]{2,1,0:T(8,128)S(1)} %all_to_all.25.cols.mine), custom_call_target="tpu_custom_call" | custom-call | flops 4000000000 | bytes 1000000 | tf_op jit(solution)/shard_map/pallas_call | solution.py:233
  47.6 0.0 collective-permute-done.cols
  47.6 6.3 %shard_map.87 = f32[8,96,128]{2,1,0:T(8,128)} custom-call(f32[8,128,128]{2,1,0:T(8,128)S(1)} %all_to_all.26.rows, f32[8,232,128]{2,1,0:T(8,128)S(1)} %collective-permute-done.cols, f32[8,232,128]{2,1,0:T(8,128)S(1)} %all_to_all.25.cols.mine, f32[1024,128]{1,0:T(8,128)S(1)} %shard_map.86.before), custom_call_target="tpu_custom_call" | custom-call | flops 4000000000 | bytes 1000000 | tf_op jit(solution)/shard_map/pallas_call | solution.py:236
  53.9 0.0 copy-start.1
  53.9 0.0 copy-start.3
  53.9 3.6 %all-to-all-start.2 = ((f32[8,96,128]{2,1,0:T(8,128)}), f32[8,96,128]{2,1,0:T(8,128)S(1)}, u32[]{:S(2)}, u32[]{:S(2)}) async-start(f32[8,96,128]{2,1,0:T(8,128)} %shard_map.87), calls=%async_computation.2 | async-start | bytes 786432 | tf_op jit(solution)/shard_map/all_to_all | solution.py:215
  58.2 9.3 %all-to-all-done.2.pieces = f32[8,96,128]{2,1,0:T(8,128)S(1)} async-done(((f32[8,96,128]{2,1,0:T(8,128)}), f32[8,96,128]{2,1,0:T(8,128)S(1)}, u32[]{:S(2)}, u32[]{:S(2)}) %all-to-all-start.2) | async-done | bytes 393248 | tf_op jit(solution)/shard_map/all_to_all | solution.py:215
  67.5 0.0 copy-done.1
  67.5 0.0 copy-done.3
  67.5 0.4 shard_map.88
  67.9 0.1 collective-permute-start.1
  68.0 1.2 %collective-permute-done.1.b = f32[96,128]{1,0:T(8,128)S(1)} collective-permute-done((f32[96,128]{1,0:T(8,128)S(1)}, f32[96,128]{1,0:T(8,128)S(1)}, u32[]{:S(2)}, u32[]{:S(2)}) %collective-permute-start.1) | collective-permute-done | bytes 49184 | tf_op jit(solution)/shard_map/ppermute | solution.py:211
  69.2 13.3 %all_to_all.27.pieces = f32[8,96,128]{2,1,0:T(8,128)S(1)} all-to-all(f32[8,96,128]{2,1,0:T(8,128)S(1)} %shard_map.89), channel_id=1, replica_groups=mesh['y'=4,'xl'=2,'z'=4,'xh'=2,'core'=2] {'z','xh'}, dimensions={0} | all-to-all | bytes 786432 | tf_op jit(solution)/shard_map/all_to_all | solution.py:215
  82.5 0.8 shard_map.90
  83.3 3.5 %all-to-all-start.4 = ((f32[8,96,128]{2,1,0:T(8,128)}), f32[8,96,128]{2,1,0:T(8,128)S(1)}, u32[]{:S(2)}, u32[]{:S(2)}) async-start(f32[8,96,128]{2,1,0:T(8,128)} %shard_map.90), calls=%async_computation.4 | async-start | bytes 786432 | tf_op jit(solution)/shard_map/all_to_all | solution.py:215
  86.8 0.0 copy-start.5
  86.8 1.9 %shard_map.91.inverse = f32[64,64]{1,0:T(8,128)S(1)} custom-call(f32[64,64]{1,0:T(8,128)S(1)} %get-tuple-element.14.gram), custom_call_target="tpu_custom_call" | custom-call | flops 100000000 | bytes 1000000 | tf_op jit(solution)/shard_map/pallas_call | solution.py:244
  88.6 6.3 %all-to-all-done.4.pieces = f32[8,96,128]{2,1,0:T(8,128)S(1)} async-done(((f32[8,96,128]{2,1,0:T(8,128)}), f32[8,96,128]{2,1,0:T(8,128)S(1)}, u32[]{:S(2)}, u32[]{:S(2)}) %all-to-all-start.4) | async-done | bytes 393248 | tf_op jit(solution)/shard_map/all_to_all | solution.py:215
  94.9 0.0 copy-done.5
  94.9 4.2 %shard_map.92 = (f32[64,128]{1,0:T(8,128)}, f32[64,128]{1,0:T(8,128)}, f32[64,128]{1,0:T(8,128)}) custom-call(f32[8,96,128]{2,1,0:T(8,128)S(1)} %all-to-all-done.4.pieces, f32[64,64]{1,0:T(8,128)S(1)} %get-tuple-element.14.gram, f32[64,64]{1,0:T(8,128)S(1)} %shard_map.91.inverse, f32[64,128]{1,0:T(8,128)S(1)} %get-tuple-element.15.image, ...), custom_call_target="tpu_custom_call" | custom-call | flops 1000000 | bytes 1000000 | tf_op jit(solution)/shard_map/pallas_call | solution.py:247
  (1 shorter events, 0.0 us)
Async XLA Ops:
  0.6 0.7 copy-start.6
  1.3 0.8 copy-start
  2.0 0.8 copy-start.2
  2.8 0.8 copy-start.4
  23.9 23.6 %collective-permute-start = (f32[8,232,128]{2,1,0:T(8,128)S(1)}, f32[8,232,128]{2,1,0:T(8,128)S(1)}, u32[]{:S(2)}, u32[]{:S(2)}) collective-permute-start(f32[8,232,128]{2,1,0:T(8,128)S(1)} %all_to_all.25.cols.mine), channel_id=1, source_target_pairs={{0,1},{1,0},{2,3},{3,2},{4,5},{5,4},{6,7},{7,6},{8,9},{9,8},{10,11... | collective-permute-start | bytes 2850824 | tf_op jit(solution)/shard_map/ppermute | solution.py:211
  53.9 13.5 %copy-start.1 = (f32[128,64]{0,1:T(8,128)S(1)}, f32[128,64]{0,1:T(8,128)}, u32[]{:S(2)}) copy-start(f32[128,64]{0,1:T(8,128)} %param.11) | copy-start | bytes 98308
  53.9 13.5 %copy-start.3 = (f32[128,64]{0,1:T(8,128)S(1)}, f32[128,64]{0,1:T(8,128)}, u32[]{:S(2)}) copy-start(f32[128,64]{0,1:T(8,128)} %param.10) | copy-start | bytes 98308
  53.9 13.5 %all-to-all-start.2 = ((f32[8,96,128]{2,1,0:T(8,128)}), f32[8,96,128]{2,1,0:T(8,128)S(1)}, u32[]{:S(2)}, u32[]{:S(2)}) async-start(f32[8,96,128]{2,1,0:T(8,128)} %shard_map.87), calls=%async_computation.2 | async-start | bytes 786432 | tf_op jit(solution)/shard_map/all_to_all | solution.py:215
  67.9 1.3 %collective-permute-start.1 = (f32[96,128]{1,0:T(8,128)S(1)}, f32[96,128]{1,0:T(8,128)S(1)}, u32[]{:S(2)}, u32[]{:S(2)}) collective-permute-start(f32[96,128]{1,0:T(8,128)S(1)} %get-tuple-element.13.a), channel_id=1, source_target_pairs={{0,1},{1,0},{2,3},{3,2},{4,5},{5,4},{6,7},{7,6},{8,9},{9,8},{10,11... | collective-permute-start | bytes 147464 | tf_op jit(solution)/shard_map/ppermute | solution.py:211
  83.3 11.6 %all-to-all-start.4 = ((f32[8,96,128]{2,1,0:T(8,128)}), f32[8,96,128]{2,1,0:T(8,128)S(1)}, u32[]{:S(2)}, u32[]{:S(2)}) async-start(f32[8,96,128]{2,1,0:T(8,128)} %shard_map.90), calls=%async_computation.4 | async-start | bytes 786432 | tf_op jit(solution)/shard_map/all_to_all | solution.py:215
  86.8 8.1 %copy-start.5 = (f32[128,64]{0,1:T(8,128)S(1)}, f32[128,64]{0,1:T(8,128)}, u32[]{:S(2)}) copy-start(f32[128,64]{0,1:T(8,128)} %param.9) | copy-start | bytes 98308

commit v3 on v2

--- a/solution.py
+++ b/solution.py
@@ -1,4 +1,3 @@
-import functools
 import math
 
 import jax
@@ -11,10 +10,15 @@
 AXES = ("y", "xl", "z", "xh", "core")
 BLK = ("y", "xl")
 CHIPS = ("z", "xh")
+PLANE = ("y", "xl", "xh")
 N = 128
 F = 128
 Q = 64
 G = 8
+R = 16
+C = 8
+TILE = 512
+CHUNK = 256
 HI = lax.Precision.HIGHEST
 ROOT = math.sqrt(math.log2(math.e))
 DIRS = N + Q
@@ -60,15 +64,13 @@
 def prep(points, scales, direction, residual, rows, cols):
     unit = points[...] / scales[...] * ROOT
     half = 0.5 * jnp.sum(unit * unit, axis=1, keepdims=True)
-    as_row = jnp.broadcast_to(half, (N, N)).T[:8]
     twice = jnp.concatenate([residual[...], residual[...]], axis=0)
-    gram = fold(dot(residual[...], twice, 1, 1))
-    for i in range(G):
+    for i in range(R):
         rows[i] = unit
-        cols[i, :N] = unit
-        cols[i, N:DIRS] = direction[...]
-        cols[i, DIRS:GRAM] = gram
-        cols[i, GRAM:] = as_row
+    cols[:N] = unit
+    cols[N:DIRS] = direction[...]
+    cols[DIRS:GRAM] = fold(dot(residual[...], twice, 1, 1))
+    cols[GRAM:] = jnp.broadcast_to(half, (N, N)).T[:8]
 
 
 def split(value):
@@ -79,58 +81,49 @@
     return top, mid, low
 
 
-def products(first, tile, rows, cols, *refs):
-    before, out, right, dirs, halves, left = refs if not first else (None, *refs)
-    for j in range(G):
+def spread_cols(*refs):
+    cols, (right, dirs, halves, gram) = refs[:C], refs[C:]
+    total = cols[0][DIRS:GRAM]
+    for j in range(C):
         at = slice(j * N, (j + 1) * N)
-        top, mid, low = split(cols[j, :N])
+        top, mid, low = split(cols[j][:N])
         right[at] = jnp.concatenate([top, mid, top, low, top, mid], axis=1)
-        high, rest, _ = split(cols[j, N:DIRS])
+        high, rest, _ = split(cols[j][N:DIRS])
         dirs[:, at] = jnp.concatenate([high, rest], axis=0)
-        halves[:, at] = cols[j, GRAM:]
-    per = tile // N
+        halves[:, at] = cols[j][GRAM:]
+        if j > 0:
+            total += cols[j][DIRS:GRAM]
+    gram[...] = total
+
+
+def products(rows, right, dirs, halves, gram, out, left):
+    per = TILE // N
 
     def step(i, carry):
-        unit = rows[pl.ds(i * per, per)].reshape(tile, F)
+        unit = rows[pl.ds(i * per, per)].reshape(TILE, F)
         top, mid, low = split(unit)
         left[...] = jnp.concatenate([top, top, mid, top, low, mid], axis=1)
         half = 0.5 * jnp.sum(unit * unit, axis=1, keepdims=True)
-        total = jnp.zeros((tile, 2 * Q), jnp.float32)
-        for j in range(4):
-            at = slice(j * 256, (j + 1) * 256)
+        total = jnp.zeros((TILE, 2 * Q), jnp.float32)
+        for j in range(C * N // CHUNK):
+            at = slice(j * CHUNK, (j + 1) * CHUNK)
             inner = dot(left[...], right[at], 1, 1, None)
             kernel = jnp.exp2(inner - half - halves[0:1, at])
             high = kernel.astype(jnp.bfloat16)
             rest = (kernel - high.astype(jnp.float32)).astype(jnp.bfloat16)
             total += dot(high, dirs[:, at], 1, 1, None) + dot(rest, dirs[:, at], 1, 1, None)
-        if first:
-            out[pl.ds(i * tile, tile)] = total
-        else:
-            total += before[pl.ds(i * tile, tile)]
-            total += pltpu.roll(total, Q, 1)
-            for b in range(per):
-                out[i * per + b, :Q] = fold(total[b * N : (b + 1) * N])
+        total += pltpu.roll(total, Q, 1)
+        for b in range(per):
+            out[i * per + b, :Q] = fold(total[b * N : (b + 1) * N])
+            out[i * per + b, Q:] = gram[...]
         return carry
 
-    lax.fori_loop(0, (G * N) // tile, step, 0)
-
-
-def products_first(tile, rows, cols, *refs):
-    products(True, tile, rows, cols, *refs)
-
-
-def products_last(tile, rows, cols, mine, before, out, right, dirs, halves, left):
-    products(False, tile, rows, cols, before, out, right, dirs, halves, left)
-    gram = cols[0, DIRS:GRAM] + mine[0, DIRS:GRAM]
-    for j in range(1, G):
-        gram += cols[j, DIRS:GRAM] + mine[j, DIRS:GRAM]
-    for j in range(G):
-        out[j, Q:] = gram
+    lax.fori_loop(0, R // per, step, 0)
 
 
 def summed(pieces):
     total = pieces[0]
-    for j in range(1, G):
+    for j in range(1, pieces.shape[0]):
         total += pieces[j]
     return total
 
@@ -211,32 +204,40 @@
     return lax.ppermute(value, "core", [(0, 1), (1, 0)])
 
 
+def across(value, k):
+    return lax.ppermute(value, "z", [(i, i ^ k) for i in range(4)])
+
+
 def exchanged(value, axes):
     return lax.all_to_all(value, axes, 0, 0, tiled=True)
 
 
 def on_device(points, lengthscales, noise_level, iterate, residual, direction):
     iterate, residual, direction = iterate.T, residual.T, direction.T
-    rows, cols = call(prep, [f32(G, N, F), f32(G, ROWS, 128)])(
+    rows, own = call(prep, [f32(R, N, F), f32(ROWS, 128)])(
         points, lengthscales.reshape(1, F), direction, residual
     )
-    cols = exchanged(cols, BLK)
-    rows = exchanged(rows, CHIPS)
-    other = swapped(cols)
-    tile = 512
-    scratch = [
-        pltpu.VMEM((G * N, 6 * F), jnp.bfloat16),
-        pltpu.VMEM((2 * Q, G * N), jnp.bfloat16),
-        pltpu.VMEM((8, G * N), jnp.float32),
-        pltpu.VMEM((tile, 6 * F), jnp.bfloat16),
-    ]
-    part = call(
-        functools.partial(products_first, tile), f32(G * N, 2 * Q), scratch, 4 * 10**9, 16
-    )(rows, cols)
+    rows = exchanged(rows, PLANE)
+    mine = [own] + [across(own, k) for k in range(1, 4)]
+    cols = mine + [swapped(m) for m in mine]
+    spread = call(
+        spread_cols,
+        [
+            jax.ShapeDtypeStruct((C * N, 6 * F), jnp.bfloat16),
+            jax.ShapeDtypeStruct((2 * Q, C * N), jnp.bfloat16),
+            f32(8, C * N),
+            f32(Q // 2, 128),
+        ],
+        flops=10**8,
+    )(*cols)
     sent = call(
-        functools.partial(products_last, tile), f32(G, Q + Q // 2, 128), scratch, 4 * 10**9, 16
-    )(rows, other, cols, part)
-    pieces = exchanged(sent, CHIPS)
+        products,
+        f32(R, Q + Q // 2, 128),
+        [pltpu.VMEM((TILE, 6 * F), jnp.bfloat16)],
+        8 * 10**9,
+        24,
+    )(rows, *spread)
+    pieces = exchanged(sent, PLANE)
     image, gram, sums = call(grams, [f32(Q, N), f32(Q, Q), f32(Q + Q // 2, 128)])(
         pieces, noise_level.reshape(1, 1), direction, residual
     )

time: 99.7 us -> 90.8 us (0.911)
  blocking collectives: 52.9 us -> 16.4 us
  starting transfers between devices: 7.12 us -> 22.5 us
  waiting for transfers between devices: 16.8 us -> 29.2 us
    all_to_all x3 -> x1, blocking collectives: 52.9 us -> 16.4 us  [exchanged(): return lax.all_to_all(value, axes, 0, 0, tiled=True)]
    all_to_all x2 -> x3, starting transfers between devices: 7.03 us -> 16.3 us  [exchanged(): return lax.all_to_all(value, axes, 0, 0, tiled=True)]
    ppermute x0 -> x3, waiting for transfers between devices: none -> 6.6 us  [across(): return lax.ppermute(value, 'z', [(i, i ^ k) for i in range(4)])]
    ppermute x0 -> x3, starting transfers between devices: none -> 5.58 us  [across(): return lax.ppermute(value, 'z', [(i, i ^ k) for i in range(4)])]
    all_to_all x2 -> x3, waiting for transfers between devices: 15.6 us -> 20 us  [exchanged(): return lax.all_to_all(value, axes, 0, 0, tiled=True)]
    ppermute x2 -> x5, waiting for transfers between devices: 1.22 us -> 2.53 us  [swapped(): return lax.ppermute(value, 'core', [(0, 1), (1, 0)])]
  transfers between devices with their start and end apart: 4 -> 11, of which waited for: 3 -> 7; matrix products, arithmetic and copies ran while one was open for 0% -> 0% of each run, Pallas kernels for 6% -> 2%
where the time goes in v3:
time: 90.8 us; the launch traced here: 90.1 us
  waiting for transfers between devices  29.2 us (32%)
  starting transfers between devices  22.5 us (25%)
  Pallas kernels  17.7 us (19%)
  blocking collectives  16.4 us (18%)
  local copies, waits for them, and re-layouts  3.02 us (3%)
  between operations  1.37 us (2%)
    all_to_all x3, waiting for transfers between devices, exchanged(): return lax.all_to_all(value, axes, 0, 0, tiled=True)  20 us
    all_to_all x1, blocking collectives, exchanged(): return lax.all_to_all(value, axes, 0, 0, tiled=True)  16.4 us
    all_to_all x3, starting transfers between devices, exchanged(): return lax.all_to_all(value, axes, 0, 0, tiled=True)  16.3 us
    pallas_call x1, Pallas kernels, on_device(): call(products, f32(R, Q + Q // 2, 128), [pltpu.VMEM((TILE, 6 * F), jnp.bf...  9.06 us
    ppermute x3, waiting for transfers between devices, across(): return lax.ppermute(value, 'z', [(i, i ^ k) for i in range(4)])  6.6 us
    ppermute x3, starting transfers between devices, across(): return lax.ppermute(value, 'z', [(i, i ^ k) for i in range(4)])  5.58 us
    pallas_call x1, Pallas kernels, on_device(): call(finish, [f32(Q, N)] * 3)  4.18 us
    unnamed x14, local copies, waits for them, and re-layouts  3.02 us
  transfers between devices with their start and end apart: 11, of which 7 were waited for; matrix products, arithmetic and copies ran while one was open for 0% of the time, Pallas kernels for 2%

profile of v3, /device:TPU:0, one launch (start us, length us, event | category | flops | bytes accessed | tf_op | source)
XLA Modules:
  0.0 90.1 jit_solution(10484138012042065657)
XLA Ops:
  0.6 0.0 copy-start
  0.6 0.7 copy-done
  1.4 0.0 copy-start.2
  1.4 0.8 copy-done.2
  2.1 0.0 copy-start.4
  2.2 0.8 copy-done.4
  3.0 0.0 copy-start.6
  3.0 0.7 copy-done.6
  3.6 1.1 %shard_map.85 = (f32[16,128,128]{2,1,0:T(8,128)}, f32[232,128]{1,0:T(8,128)S(1)}) custom-call(f32[128,128]{1,0:T(8,128)S(1)} %copy-done.4, f32[1,128]{1,0:T(1,128)S(1)} %bitcast.16, f32[64,128]{1,0:T(8,128)S(1)} %bitcast.9, f32[64,128]{1,0:T(8,128)S(1)} %bitcast.12), custom_call_target="tpu_custom_call" | custom-call | flops 1000000 | bytes 1000000 | tf_op jit(solution)/shard_map/pallas_call | solution.py:217
  4.8 7.1 %all-to-all-start = ((f32[16,128,128]{2,1,0:T(8,128)}), f32[16,128,128]{2,1,0:T(8,128)S(1)}, u32[]{:S(2)}, u32[]{:S(2)}) async-start(f32[16,128,128]{2,1,0:T(8,128)} %get-tuple-element.15), calls=%async_computation | async-start | bytes 2097152 | tf_op jit(solution)/shard_map/all_to_all | solution.py:212
  11.9 2.0 %collective-permute-start = (f32[232,128]{1,0:T(8,128)S(1)}, f32[232,128]{1,0:T(8,128)S(1)}, u32[]{:S(2)}, u32[]{:S(2)}) collective-permute-start(f32[232,128]{1,0:T(8,128)S(1)} %get-tuple-element.16.refs_0_), channel_id=1, source_target_pairs={{0,4},{4,0},{8,12},{12,8},{1,5},{5,1},{9,13},{13,9},{2,6},{6,2},{1... | collective-permute-start | bytes 356360 | tf_op jit(solution)/shard_map/ppermute | solution.py:208
  13.9 3.6 %collective-permute-start.1 = (f32[232,128]{1,0:T(8,128)S(1)}, f32[232,128]{1,0:T(8,128)S(1)}, u32[]{:S(2)}, u32[]{:S(2)}) collective-permute-start(f32[232,128]{1,0:T(8,128)S(1)} %get-tuple-element.16.refs_0_), channel_id=1, source_target_pairs={{0,8},{4,12},{8,0},{12,4},{1,9},{5,13},{9,1},{13,5},{2,10},{6,14},... | collective-permute-start | bytes 356360 | tf_op jit(solution)/shard_map/ppermute | solution.py:208
  17.5 0.0 collective-permute-start.2
  17.5 0.0 collective-permute-start.3
  17.5 0.0 collective-permute-done.refs_1_
  17.5 0.5 collective-permute-start.4
  18.0 4.8 %collective-permute-done.1.refs_2_ = f32[232,128]{1,0:T(8,128)S(1)} collective-permute-done((f32[232,128]{1,0:T(8,128)S(1)}, f32[232,128]{1,0:T(8,128)S(1)}, u32[]{:S(2)}, u32[]{:S(2)}) %collective-permute-start.1) | collective-permute-done | bytes 118816 | tf_op jit(solution)/shard_map/ppermute | solution.py:208
  22.8 0.0 collective-permute-start.5
  22.8 1.8 %collective-permute-done.2.refs_3_ = f32[232,128]{1,0:T(8,128)S(1)} collective-permute-done((f32[232,128]{1,0:T(8,128)S(1)}, f32[232,128]{1,0:T(8,128)S(1)}, u32[]{:S(2)}, u32[]{:S(2)}) %collective-permute-start.2) | collective-permute-done | bytes 118816 | tf_op jit(solution)/shard_map/ppermute | solution.py:208
  24.6 0.0 collective-permute-start.6
  24.6 0.0 collective-permute-done.3.refs_4_
  24.6 0.0 collective-permute-done.4.refs_5_
  24.6 0.0 collective-permute-done.5.refs_6_
  24.6 1.3 %collective-permute-done.6.refs_7_ = f32[232,128]{1,0:T(8,128)S(1)} collective-permute-done((f32[232,128]{1,0:T(8,128)S(1)}, f32[232,128]{1,0:T(8,128)S(1)}, u32[]{:S(2)}, u32[]{:S(2)}) %collective-permute-start.6) | collective-permute-done | bytes 118816 | tf_op jit(solution)/shard_map/ppermute | solution.py:204
  25.9 0.2 shard_map.86
  26.1 1.5 %all-to-all-done.rows = f32[16,128,128]{2,1,0:T(8,128)S(1)} async-done(((f32[16,128,128]{2,1,0:T(8,128)}), f32[16,128,128]{2,1,0:T(8,128)S(1)}, u32[]{:S(2)}, u32[]{:S(2)}) %all-to-all-start) | async-done | bytes 1048608 | tf_op jit(solution)/shard_map/all_to_all | solution.py:212
  27.6 9.1 %shard_map.87 = f32[16,96,128]{2,1,0:T(8,128)} custom-call(f32[16,128,128]{2,1,0:T(8,128)S(1)} %all-to-all-done.rows, bf16[1024,768]{1,0:T(8,128)(2,1)S(1)} %get-tuple-element.17.right, bf16[128,1024]{1,0:T(8,128)(2,1)S(1)} %get-tuple-element.18.dirs, f32[8,1024]{1,0:T(8,128)S(1)} %get-tuple-element.19.halves, f32[32,128]{1,0:T(8,128)S(1)} %get-tuple-element.20.gram), custom_call_target="tpu_custom_call" | custom-call | flops 8000000000 | bytes 1000000 | tf_op jit(solution)/shard_map/pallas_call | solution.py:233
  36.7 0.0 copy-start.1
  36.7 0.0 copy-start.3
  36.7 5.7 %all-to-all-start.1 = ((f32[16,96,128]{2,1,0:T(8,128)}), f32[16,96,128]{2,1,0:T(8,128)S(1)}, u32[]{:S(2)}, u32[]{:S(2)}) async-start(f32[16,96,128]{2,1,0:T(8,128)} %shard_map.87), calls=%async_computation.1 | async-start | bytes 1572864 | tf_op jit(solution)/shard_map/all_to_all | solution.py:212
  43.0 12.5 %all-to-all-done.1.pieces = f32[16,96,128]{2,1,0:T(8,128)S(1)} async-done(((f32[16,96,128]{2,1,0:T(8,128)}), f32[16,96,128]{2,1,0:T(8,128)S(1)}, u32[]{:S(2)}, u32[]{:S(2)}) %all-to-all-start.1) | async-done | bytes 786464 | tf_op jit(solution)/shard_map/all_to_all | solution.py:212
  55.5 0.0 copy-done.1
  55.5 0.0 copy-done.3
  55.6 0.4 shard_map.88
  56.0 0.0 copy-start.5
  56.0 0.1 collective-permute-start.7
  56.1 1.2 %collective-permute-done.7.b = f32[96,128]{1,0:T(8,128)S(1)} collective-permute-done((f32[96,128]{1,0:T(8,128)S(1)}, f32[96,128]{1,0:T(8,128)S(1)}, u32[]{:S(2)}, u32[]{:S(2)}) %collective-permute-start.7) | collective-permute-done | bytes 49184 | tf_op jit(solution)/shard_map/ppermute | solution.py:204
  57.3 16.4 %all_to_all.20.pieces = f32[8,96,128]{2,1,0:T(8,128)S(1)} all-to-all(f32[8,96,128]{2,1,0:T(8,128)S(1)} %shard_map.89), channel_id=1, replica_groups=mesh['y'=4,'xl'=2,'z'=4,'xh'=2,'core'=2] {'z','xh'}, dimensions={0} | all-to-all | bytes 786432 | tf_op jit(solution)/shard_map/all_to_all | solution.py:212
  73.7 0.8 shard_map.90
  74.5 3.5 %all-to-all-start.3 = ((f32[8,96,128]{2,1,0:T(8,128)}), f32[8,96,128]{2,1,0:T(8,128)S(1)}, u32[]{:S(2)}, u32[]{:S(2)}) async-start(f32[8,96,128]{2,1,0:T(8,128)} %shard_map.90), calls=%async_computation.3 | async-start | bytes 786432 | tf_op jit(solution)/shard_map/all_to_all | solution.py:212
  78.0 1.9 %shard_map.91.inverse = f32[64,64]{1,0:T(8,128)S(1)} custom-call(f32[64,64]{1,0:T(8,128)S(1)} %get-tuple-element.22.gram), custom_call_target="tpu_custom_call" | custom-call | flops 100000000 | bytes 1000000 | tf_op jit(solution)/shard_map/pallas_call | solution.py:245
  79.8 6.1 %all-to-all-done.3.pieces = f32[8,96,128]{2,1,0:T(8,128)S(1)} async-done(((f32[8,96,128]{2,1,0:T(8,128)}), f32[8,96,128]{2,1,0:T(8,128)S(1)}, u32[]{:S(2)}, u32[]{:S(2)}) %all-to-all-start.3) | async-done | bytes 393248 | tf_op jit(solution)/shard_map/all_to_all | solution.py:212
  85.9 0.0 copy-done.5
  85.9 4.2 %shard_map.92 = (f32[64,128]{1,0:T(8,128)}, f32[64,128]{1,0:T(8,128)}, f32[64,128]{1,0:T(8,128)}) custom-call(f32[8,96,128]{2,1,0:T(8,128)S(1)} %all-to-all-done.3.pieces, f32[64,64]{1,0:T(8,128)S(1)} %get-tuple-element.22.gram, f32[64,64]{1,0:T(8,128)S(1)} %shard_map.91.inverse, f32[64,128]{1,0:T(8,128)S(1)} %get-tuple-element.23.image, ...), custom_call_target="tpu_custom_call" | custom-call | flops 1000000 | bytes 1000000 | tf_op jit(solution)/shard_map/pallas_call | solution.py:248
  (1 shorter events, 0.0 us)
Async XLA Ops:
  0.6 0.8 copy-start
  1.4 0.8 copy-start.2
  2.1 0.8 copy-start.4
  3.0 0.7 copy-start.6
  4.8 22.8 %all-to-all-start = ((f32[16,128,128]{2,1,0:T(8,128)}), f32[16,128,128]{2,1,0:T(8,128)S(1)}, u32[]{:S(2)}, u32[]{:S(2)}) async-start(f32[16,128,128]{2,1,0:T(8,128)} %get-tuple-element.15), calls=%async_computation | async-start | bytes 2097152 | tf_op jit(solution)/shard_map/all_to_all | solution.py:212
  11.9 5.6 %collective-permute-start = (f32[232,128]{1,0:T(8,128)S(1)}, f32[232,128]{1,0:T(8,128)S(1)}, u32[]{:S(2)}, u32[]{:S(2)}) collective-permute-start(f32[232,128]{1,0:T(8,128)S(1)} %get-tuple-element.16.refs_0_), channel_id=1, source_target_pairs={{0,4},{4,0},{8,12},{12,8},{1,5},{5,1},{9,13},{13,9},{2,6},{6,2},{1... | collective-permute-start | bytes 356360 | tf_op jit(solution)/shard_map/ppermute | solution.py:208
  13.9 8.9 %collective-permute-start.1 = (f32[232,128]{1,0:T(8,128)S(1)}, f32[232,128]{1,0:T(8,128)S(1)}, u32[]{:S(2)}, u32[]{:S(2)}) collective-permute-start(f32[232,128]{1,0:T(8,128)S(1)} %get-tuple-element.16.refs_0_), channel_id=1, source_target_pairs={{0,8},{4,12},{8,0},{12,4},{1,9},{5,13},{9,1},{13,5},{2,10},{6,14},... | collective-permute-start | bytes 356360 | tf_op jit(solution)/shard_map/ppermute | solution.py:208
  17.5 7.1 %collective-permute-start.2 = (f32[232,128]{1,0:T(8,128)S(1)}, f32[232,128]{1,0:T(8,128)S(1)}, u32[]{:S(2)}, u32[]{:S(2)}) collective-permute-start(f32[232,128]{1,0:T(8,128)S(1)} %get-tuple-element.16.refs_0_), channel_id=1, source_target_pairs={{0,12},{4,8},{8,4},{12,0},{1,13},{5,9},{9,5},{13,1},{2,14},{6,10},... | collective-permute-start | bytes 356360 | tf_op jit(solution)/shard_map/ppermute | solution.py:208
  17.5 7.1 %collective-permute-start.3 = (f32[232,128]{1,0:T(8,128)S(1)}, f32[232,128]{1,0:T(8,128)S(1)}, u32[]{:S(2)}, u32[]{:S(2)}) collective-permute-start(f32[232,128]{1,0:T(8,128)S(1)} %get-tuple-element.16.refs_0_), channel_id=1, source_target_pairs={{0,1},{1,0},{2,3},{3,2},{4,5},{5,4},{6,7},{7,6},{8,9},{9,8},{10,11... | collective-permute-start | bytes 356360 | tf_op jit(solution)/shard_map/ppermute | solution.py:204
  17.5 7.1 %collective-permute-start.4 = (f32[232,128]{1,0:T(8,128)S(1)}, f32[232,128]{1,0:T(8,128)S(1)}, u32[]{:S(2)}, u32[]{:S(2)}) collective-permute-start(f32[232,128]{1,0:T(8,128)S(1)} %collective-permute-done.refs_1_), channel_id=1, source_target_pairs={{0,1},{1,0},{2,3},{3,2},{4,5},{5,4},{6,7},{7,6},{8,9},{9,8},{10,11... | collective-permute-start | bytes 356360 | tf_op jit(solution)/shard_map/ppermute | solution.py:204
  22.8 1.8 %collective-permute-start.5 = (f32[232,128]{1,0:T(8,128)S(1)}, f32[232,128]{1,0:T(8,128)S(1)}, u32[]{:S(2)}, u32[]{:S(2)}) collective-permute-start(f32[232,128]{1,0:T(8,128)S(1)} %collective-permute-done.1.refs_2_), channel_id=1, source_target_pairs={{0,1},{1,0},{2,3},{3,2},{4,5},{5,4},{6,7},{7,6},{8,9},{9,8},{10,11... | collective-permute-start | bytes 356360 | tf_op jit(solution)/shard_map/ppermute | solution.py:204
  24.6 1.3 %collective-permute-start.6 = (f32[232,128]{1,0:T(8,128)S(1)}, f32[232,128]{1,0:T(8,128)S(1)}, u32[]{:S(2)}, u32[]{:S(2)}) collective-permute-start(f32[232,128]{1,0:T(8,128)S(1)} %collective-permute-done.2.refs_3_), channel_id=1, source_target_pairs={{0,1},{1,0},{2,3},{3,2},{4,5},{5,4},{6,7},{7,6},{8,9},{9,8},{10,11... | collective-permute-start | bytes 356360 | tf_op jit(solution)/shard_map/ppermute | solution.py:204
  36.7 18.9 %copy-start.1 = (f32[128,64]{0,1:T(8,128)S(1)}, f32[128,64]{0,1:T(8,128)}, u32[]{:S(2)}) copy-start(f32[128,64]{0,1:T(8,128)} %param.11) | copy-start | bytes 98308
  36.7 18.9 %copy-start.3 = (f32[128,64]{0,1:T(8,128)S(1)}, f32[128,64]{0,1:T(8,128)}, u32[]{:S(2)}) copy-start(f32[128,64]{0,1:T(8,128)} %param.10) | copy-start | bytes 98308
  36.7 18.9 %all-to-all-start.1 = ((f32[16,96,128]{2,1,0:T(8,128)}), f32[16,96,128]{2,1,0:T(8,128)S(1)}, u32[]{:S(2)}, u32[]{:S(2)}) async-start(f32[16,96,128]{2,1,0:T(8,128)} %shard_map.87), calls=%async_computation.1 | async-start | bytes 1572864 | tf_op jit(solution)/shard_map/all_to_all | solution.py:212
  56.0 29.9 %copy-start.5 = (f32[128,64]{0,1:T(8,128)S(1)}, f32[128,64]{0,1:T(8,128)}, u32[]{:S(2)}) copy-start(f32[128,64]{0,1:T(8,128)} %param.9) | copy-start | bytes 98308
  56.0 1.3 %collective-permute-start.7 = (f32[96,128]{1,0:T(8,128)S(1)}, f32[96,128]{1,0:T(8,128)S(1)}, u32[]{:S(2)}, u32[]{:S(2)}) collective-permute-start(f32[96,128]{1,0:T(8,128)S(1)} %get-tuple-element.21.a), channel_id=1, source_target_pairs={{0,1},{1,0},{2,3},{3,2},{4,5},{5,4},{6,7},{7,6},{8,9},{9,8},{10,11... | collective-permute-start | bytes 147464 | tf_op jit(solution)/shard_map/ppermute | solution.py:204
  74.5 11.4 %all-to-all-start.3 = ((f32[8,96,128]{2,1,0:T(8,128)}), f32[8,96,128]{2,1,0:T(8,128)S(1)}, u32[]{:S(2)}, u32[]{:S(2)}) async-start(f32[8,96,128]{2,1,0:T(8,128)} %shard_map.90), calls=%async_computation.3 | async-start | bytes 786432 | tf_op jit(solution)/shard_map/all_to_all | solution.py:212

commit v4 on v3

--- a/solution.py
+++ b/solution.py
@@ -17,20 +17,25 @@
 G = 8
 R = 16
 C = 8
-TILE = 512
+TILE = 1024
 CHUNK = 256
 HI = lax.Precision.HIGHEST
 ROOT = math.sqrt(math.log2(math.e))
 DIRS = N + Q
 GRAM = DIRS + Q // 2
 ROWS = GRAM + 8
+ITER, RES, DIR, NOISE = 0, Q, 2 * Q, 3 * Q
+SUMS = Q + 8
+HBM = pl.BlockSpec(memory_space=pltpu.MemorySpace.HBM)
+ROOM = 62
 VM = pl.BlockSpec(memory_space=pltpu.VMEM)
 
 
-def call(body, outs, scratch=(), flops=10**6, room=4):
+def call(body, outs, scratch=(), flops=10**6, room=4, ins=None):
     return pl.pallas_call(
         body,
         out_shape=outs,
+        **({} if ins is None else {"in_specs": ins}),
         out_specs=jax.tree.map(lambda _: VM, outs),
         scratch_shapes=list(scratch),
         compiler_params=pltpu.CompilerParams(vmem_limit_bytes=room * 2**20),
@@ -61,16 +66,31 @@
     return jnp.concatenate([packed[:, :Q], packed[:, Q:]], axis=0)
 
 
-def prep(points, scales, direction, residual, rows, cols):
-    unit = points[...] / scales[...] * ROOT
+def prep(points, scales, noise, iterate, residual, direction, rows, cols, kept, place, sems):
+    points_in, scales_in = place
+    copies = [
+        pltpu.make_async_copy(points, points_in, sems.at[0]),
+        pltpu.make_async_copy(scales, scales_in, sems.at[1]),
+        pltpu.make_async_copy(residual, kept.at[RES : RES + Q], sems.at[2]),
+        pltpu.make_async_copy(direction, kept.at[DIR : DIR + Q], sems.at[3]),
+        pltpu.make_async_copy(iterate, kept.at[ITER : ITER + Q], sems.at[4]),
+    ]
+    for copy in copies:
+        copy.start()
+    for copy in copies[:2]:
+        copy.wait()
+    unit = points_in[...] / scales_in[...] * ROOT
     half = 0.5 * jnp.sum(unit * unit, axis=1, keepdims=True)
-    twice = jnp.concatenate([residual[...], residual[...]], axis=0)
     for i in range(R):
         rows[i] = unit
     cols[:N] = unit
-    cols[N:DIRS] = direction[...]
-    cols[DIRS:GRAM] = fold(dot(residual[...], twice, 1, 1))
+    for copy in copies[2:]:
+        copy.wait()
+    residual = kept[RES : RES + Q]
+    cols[N:DIRS] = kept[DIR : DIR + Q]
+    cols[DIRS:GRAM] = fold(dot(residual, jnp.concatenate([residual, residual], axis=0), 1, 1))
     cols[GRAM:] = jnp.broadcast_to(half, (N, N)).T[:8]
+    kept[NOISE:] = jnp.full((8, 128), noise[0])
 
 
 def split(value):
@@ -128,16 +148,29 @@
     return total
 
 
-def grams(pieces, noise, direction, residual, image_out, gram_out, sums):
+def lower(shape):
+    return lax.broadcasted_iota(jnp.int32, shape, 0) > lax.broadcasted_iota(jnp.int32, shape, 1)
+
+
+def diagonal(shape):
+    return lax.broadcasted_iota(jnp.int32, shape, 0) == lax.broadcasted_iota(jnp.int32, shape, 1)
+
+
+def grams(pieces, kept, image_out, gram_out, sums):
     total = summed(pieces)
     turned = total[:Q].T
-    image = jnp.concatenate([turned[:Q], turned[Q:]], axis=1) + noise[0, 0] * direction[...]
+    direction = kept[DIR : DIR + Q]
+    image = jnp.concatenate([turned[:Q], turned[Q:]], axis=1) + kept[NOISE : NOISE + 1] * direction
     image_out[...] = image
     gram_out[...] = unfold(total[Q:])
-    side = jnp.concatenate([direction[...], residual[...], image, image], axis=0)
-    products_of = dot(image, side, 1, 1)
-    sums[:Q] = products_of[:, : 2 * Q]
-    sums[Q:] = fold(products_of[:, 2 * Q :])
+    side = jnp.concatenate([direction, kept[RES : RES + Q], image], axis=0)
+    wide = dot(image, side, 1, 1)
+    gram = 0.5 * (wide[:, :Q] + dot(direction, image, 1, 1))
+    cross, square = wide[:, Q : 2 * Q], wide[:, 2 * Q :]
+    both = jnp.where(lower((Q, Q)), gram, square)
+    sums[:Q] = jnp.concatenate([cross, both], axis=1)
+    along = jnp.sum(jnp.where(diagonal((Q, Q)), gram, 0.0), axis=0, keepdims=True)
+    sums[Q:] = jnp.broadcast_to(jnp.concatenate([along, along], axis=1), (8, 128))
 
 
 def eliminate(matrix):
@@ -170,11 +203,11 @@
 
 
 def invert(gram, out):
-    eye = lax.broadcasted_iota(jnp.int32, (Q, Q), 0) == lax.broadcasted_iota(jnp.int32, (Q, Q), 1)
-    out[...] = eliminate(jnp.concatenate([gram[...], eye.astype(jnp.float32)], axis=1))
-
-
-def pair_sum(a, b, out):
+    out[...] = eliminate(jnp.concatenate([gram[...], diagonal((Q, Q)).astype(jnp.float32)], axis=1))
+
+
+def pair_sum(a, b, inverse, out, inverse_out):
+    inverse_out[...] = inverse[...]
     total = a[...] + b[...]
     for j in range(G):
         out[j] = total
@@ -186,18 +219,22 @@
         out[j] = total
 
 
-def finish(pieces, gram, inverse, image, iterate, residual, direction, x_out, r_out, d_out):
+def finish(pieces, gram, inverse, image, kept, x_out, r_out, d_out):
     total = summed(pieces)
-    raw, cross = total[:Q, :Q], total[:Q, Q:]
-    square = unfold(total[Q:])
+    cross, both = total[:Q, :Q], total[:Q, Q:]
+    below, at = lower((Q, Q)), diagonal((Q, Q))
+    under = jnp.where(below, both, 0.0)
+    over = both - under
+    matrix = jnp.where(at, total[Q : Q + 1, :Q], under + under.T)
+    square = over + jnp.where(below, over.T, 0.0)
     res = gram[...]
-    step = eliminate(jnp.concatenate([0.5 * (raw + raw.T), res], axis=1))
-    x_out[...] = iterate[...] + dot(step, direction[...], 0, 0)
-    new_res = residual[...] - dot(step, image[...], 0, 0)
+    direction = kept[DIR : DIR + Q]
+    step = eliminate(jnp.concatenate([matrix, res], axis=1))
+    x_out[...] = kept[ITER : ITER + Q] + dot(step, direction, 0, 0)
+    new_res = kept[RES : RES + Q] - dot(step, image[...], 0, 0)
     r_out[...] = new_res
-    term = dot(step, cross, 0, 0)
-    new_gram = res - term - term.T + dot(step, dot(square, step), 0, 0)
-    d_out[...] = new_res + dot(dot(inverse[...], new_gram), direction[...], 0, 0)
+    new_gram = res - dot(cross, step, 0, 0) + dot(step, dot(square, step) - cross, 0, 0)
+    d_out[...] = new_res + dot(dot(inverse[...], new_gram), direction, 0, 0)
 
 
 def swapped(value):
@@ -213,9 +250,22 @@
 
 
 def on_device(points, lengthscales, noise_level, iterate, residual, direction):
-    iterate, residual, direction = iterate.T, residual.T, direction.T
-    rows, own = call(prep, [f32(R, N, F), f32(ROWS, 128)])(
-        points, lengthscales.reshape(1, F), direction, residual
+    rows, own, kept = call(
+        prep,
+        [f32(R, N, F), f32(ROWS, 128), f32(NOISE + 8, 128)],
+        [
+            [pltpu.VMEM((N, F), jnp.float32), pltpu.VMEM((1, F), jnp.float32)],
+            pltpu.SemaphoreType.DMA((5,)),
+        ],
+        room=ROOM,
+        ins=[HBM, HBM, pl.BlockSpec(memory_space=pltpu.SMEM), HBM, HBM, HBM],
+    )(
+        points,
+        lengthscales.reshape(1, F),
+        noise_level,
+        iterate.T,
+        residual.T,
+        direction.T,
     )
     rows = exchanged(rows, PLANE)
     mine = [own] + [across(own, k) for k in range(1, 4)]
@@ -237,17 +287,14 @@
         8 * 10**9,
         24,
     )(rows, *spread)
-    pieces = exchanged(sent, PLANE)
-    image, gram, sums = call(grams, [f32(Q, N), f32(Q, Q), f32(Q + Q // 2, 128)])(
-        pieces, noise_level.reshape(1, 1), direction, residual
-    )
-    both = call(pair_sum, f32(G, Q + Q // 2, 128))(sums, swapped(sums))
+    image, gram, sums = call(grams, [f32(Q, N), f32(Q, Q), f32(SUMS, 128)])(
+        exchanged(sent, PLANE), kept
+    )
     inverse = call(invert, f32(Q, Q), flops=10**8)(gram)
-    by_chip = call(chip_sum, f32(G, Q + Q // 2, 128))(exchanged(both, CHIPS))
+    both, inverse = call(pair_sum, [f32(G, SUMS, 128), f32(Q, Q)])(sums, swapped(sums), inverse)
+    by_chip = call(chip_sum, f32(G, SUMS, 128))(exchanged(both, CHIPS))
     whole = exchanged(by_chip, BLK)
-    outs = call(finish, [f32(Q, N)] * 3)(
-        whole, gram, inverse, image, iterate, residual, direction
-    )
+    outs = call(finish, [f32(Q, N)] * 3)(whole, gram, inverse, image, kept)
     return tuple(o.T for o in outs)
 
 

time: 90.8 us -> 85.7 us (0.944)
  blocking collectives: 16.4 us -> 44.7 us
  waiting for transfers between devices: 29.2 us -> 9.89 us
  starting transfers between devices: 22.5 us -> 13 us
  local copies, waits for them, and re-layouts: 3.02 us -> 0.01 us
  Pallas kernels: 17.7 us -> 16.5 us
    all_to_all x1 -> x3, blocking collectives: 16.4 us -> 44.7 us  [exchanged(): return lax.all_to_all(value, axes, 0, 0, tiled=True)]
    all_to_all x3 -> x1, waiting for transfers between devices: 20 us -> 2.67 us  [exchanged(): return lax.all_to_all(value, axes, 0, 0, tiled=True)]
    all_to_all x3 -> x1, starting transfers between devices: 16.3 us -> 7.29 us  [exchanged(): return lax.all_to_all(value, axes, 0, 0, tiled=True)]
    unnamed x14 -> x4, local copies, waits for them, and re-layouts: 3.02 us -> 0.01 us
    pallas_call x1, Pallas kernels: 9.06 us -> 7.38 us  [on_device(): call(products, f32(R, Q + Q // 2, 128), [pltpu.VMEM((TILE, 6 * F), jnp.bf...]
    ppermute x5, waiting for transfers between devices: 2.53 us -> 0.99 us  [swapped(): return lax.ppermute(value, 'core', [(0, 1), (1, 0)])]
  transfers between devices with their start and end apart: 11 -> 9, of which waited for: 7 -> 5; matrix products, arithmetic and copies ran while one was open for 0% -> 0% of each run, Pallas kernels for 2% -> 2%
where the time goes in v4:
time: 85.7 us; the launch traced here: 85.4 us
  blocking collectives  44.7 us (52%)
  Pallas kernels  16.5 us (19%)
  starting transfers between devices  13 us (15%)
  waiting for transfers between devices  9.89 us (12%)
  between operations  1.37 us (2%)
    all_to_all x3, blocking collectives, exchanged(): return lax.all_to_all(value, axes, 0, 0, tiled=True)  44.7 us
    pallas_call x1, Pallas kernels, on_device(): call(products, f32(R, Q + Q // 2, 128), [pltpu.VMEM((TILE, 6 * F), jnp.bf...  7.38 us
    all_to_all x1, starting transfers between devices, exchanged(): return lax.all_to_all(value, axes, 0, 0, tiled=True)  7.29 us
    ppermute x3, waiting for transfers between devices, across(): return lax.ppermute(value, 'z', [(i, i ^ k) for i in range(4)])  6.24 us
    ppermute x3, starting transfers between devices, across(): return lax.ppermute(value, 'z', [(i, i ^ k) for i in range(4)])  5.07 us
    pallas_call x1, Pallas kernels, on_device(): outs = call(finish, [f32(Q, N)] * 3)(whole, gram, inverse, image, kept)  4.3 us
    all_to_all x1, waiting for transfers between devices, exchanged(): return lax.all_to_all(value, axes, 0, 0, tiled=True)  2.67 us
    pallas_call x1, Pallas kernels, on_device(): call(prep, [f32(R, N, F), f32(ROWS, 128), f32(NOISE + 8, 128)], [[pltpu.V...  2.1 us
  transfers between devices with their start and end apart: 9, of which 5 were waited for; matrix products, arithmetic and copies ran while one was open for 0% of the time, Pallas kernels for 2%

profile of v4, /device:TPU:0, one launch (start us, length us, event | category | flops | bytes accessed | tf_op | source)
XLA Modules:
  0.0 85.4 jit_solution(8897900656791902842)
XLA Ops:
  1.3 2.1 %shard_map.85 = (f32[16,128,128]{2,1,0:T(8,128)}, f32[232,128]{1,0:T(8,128)}, f32[200,128]{1,0:T(8,128)}) custom-call(f32[128,128]{1,0:T(8,128)} %points.1, f32[1,128]{1,0:T(1,128)} %bitcast.10, f32[1]{0:T(128)S(6)} %copy.9.noise, f32[64,128]{1,0:T(8,128)} %bitcast.7, f32[64,128]{1,0:T(8,128)} %bitcast.8, f32[64,128]{1,0:T(8,128)} %bitcast.9), custom_call_target="tpu_custom_call" | custom-call | flops 1000000 | bytes 1000000 | tf_op jit(solution)/shard_map/pallas_call | solution.py:253
  3.4 0.0 copy-start.1
  3.4 7.3 %all-to-all-start = ((f32[16,128,128]{2,1,0:T(8,128)}), f32[16,128,128]{2,1,0:T(8,128)S(1)}, u32[]{:S(2)}, u32[]{:S(2)}) async-start(f32[16,128,128]{2,1,0:T(8,128)} %get-tuple-element.18), calls=%async_computation | async-start | bytes 2097152 | tf_op jit(solution)/shard_map/all_to_all | solution.py:249
  10.7 0.0 copy-done.1
  10.7 4.1 %collective-permute-start.2 = (f32[232,128]{1,0:T(8,128)S(1)}, f32[232,128]{1,0:T(8,128)S(1)}, u32[]{:S(2)}, u32[]{:S(2)}) collective-permute-start(f32[232,128]{1,0:T(8,128)S(1)} %copy-done.1), channel_id=1, source_target_pairs={{0,12},{4,8},{8,4},{12,0},{1,13},{5,9},{9,5},{13,1},{2,14},{6,10},... | collective-permute-start | bytes 356360 | tf_op jit(solution)/shard_map/ppermute | solution.py:245
  14.8 0.0 collective-permute-start.1
  14.8 0.9 %collective-permute-start = (f32[232,128]{1,0:T(8,128)S(1)}, f32[232,128]{1,0:T(8,128)S(1)}, u32[]{:S(2)}, u32[]{:S(2)}) collective-permute-start(f32[232,128]{1,0:T(8,128)S(1)} %copy-done.1), channel_id=1, source_target_pairs={{0,4},{4,0},{8,12},{12,8},{1,5},{5,1},{9,13},{13,9},{2,6},{6,2},{1... | collective-permute-start | bytes 356360 | tf_op jit(solution)/shard_map/ppermute | solution.py:245
  15.8 0.0 collective-permute-start.3
  15.8 3.8 %collective-permute-done.2.refs_3_ = f32[232,128]{1,0:T(8,128)S(1)} collective-permute-done((f32[232,128]{1,0:T(8,128)S(1)}, f32[232,128]{1,0:T(8,128)S(1)}, u32[]{:S(2)}, u32[]{:S(2)}) %collective-permute-start.2) | collective-permute-done | bytes 118816 | tf_op jit(solution)/shard_map/ppermute | solution.py:245
  19.6 0.0 collective-permute-start.6
  19.6 2.4 %collective-permute-done.1.refs_2_ = f32[232,128]{1,0:T(8,128)S(1)} collective-permute-done((f32[232,128]{1,0:T(8,128)S(1)}, f32[232,128]{1,0:T(8,128)S(1)}, u32[]{:S(2)}, u32[]{:S(2)}) %collective-permute-start.1) | collective-permute-done | bytes 118816 | tf_op jit(solution)/shard_map/ppermute | solution.py:245
  22.0 0.0 collective-permute-start.5
  22.0 0.0 collective-permute-done.refs_1_
  22.0 0.5 collective-permute-start.4
  22.5 0.0 collective-permute-done.3.refs_4_
  22.5 0.0 collective-permute-done.6.refs_7_
  22.5 0.8 collective-permute-done.5.refs_6_
  23.3 0.2 collective-permute-done.4.refs_5_
  23.5 0.2 shard_map.86
  23.7 2.7 %all-to-all-done.rows = f32[16,128,128]{2,1,0:T(8,128)S(1)} async-done(((f32[16,128,128]{2,1,0:T(8,128)}), f32[16,128,128]{2,1,0:T(8,128)S(1)}, u32[]{:S(2)}, u32[]{:S(2)}) %all-to-all-start) | async-done | bytes 1048608 | tf_op jit(solution)/shard_map/all_to_all | solution.py:249
  26.4 7.4 %shard_map.87 = f32[16,96,128]{2,1,0:T(8,128)S(1)} custom-call(f32[16,128,128]{2,1,0:T(8,128)S(1)} %all-to-all-done.rows, bf16[1024,768]{1,0:T(8,128)(2,1)S(1)} %get-tuple-element.20.right, bf16[128,1024]{1,0:T(8,128)(2,1)S(1)} %get-tuple-element.21.dirs, f32[8,1024]{1,0:T(8,128)S(1)} %get-tuple-element.22.halves, f32[32,128]{1,0:T(8,128)S(1)} %get-tuple-element.23.gram), custom_call_target="tpu_custom_call" | custom-call | flops 8000000000 | bytes 1000000 | tf_op jit(solution)/shard_map/pallas_call | solution.py:283
  33.8 0.0 copy-start
  33.8 18.9 %all_to_all.20.pieces = f32[16,96,128]{2,1,0:T(8,128)S(1)} all-to-all(f32[16,96,128]{2,1,0:T(8,128)S(1)} %shard_map.87), channel_id=1, replica_groups=mesh['y'=4,'xl'=2,'z'=4,'xh'=2,'core'=2] {'y','xl','xh'}, dimensions={0} | all-to-all | bytes 1572864 | tf_op jit(solution)/shard_map/all_to_all | solution.py:249
  52.6 0.0 copy-done
  52.6 0.6 shard_map.88
  53.2 0.1 collective-permute-start.7
  53.3 1.9 %shard_map.89.inverse = f32[64,64]{1,0:T(8,128)S(1)} custom-call(f32[64,64]{1,0:T(8,128)S(1)} %get-tuple-element.26.gram), custom_call_target="tpu_custom_call" | custom-call | flops 100000000 | bytes 1000000 | tf_op jit(solution)/shard_map/pallas_call | solution.py:293
  55.2 0.0 collective-permute-done.7.b
  55.2 15.5 %all_to_all.21.pieces = f32[8,72,128]{2,1,0:T(8,128)S(1)} all-to-all(f32[8,72,128]{2,1,0:T(8,128)S(1)} %get-tuple-element.27), channel_id=1, replica_groups=mesh['y'=4,'xl'=2,'z'=4,'xh'=2,'core'=2] {'z','xh'}, dimensions={0} | all-to-all | bytes 589824 | tf_op jit(solution)/shard_map/all_to_all | solution.py:249
  70.7 10.3 %all_to_all.22.pieces = f32[8,72,128]{2,1,0:T(8,128)S(1)} all-to-all(f32[8,72,128]{2,1,0:T(8,128)S(1)} %shard_map.91), channel_id=1, replica_groups=mesh['y'=4,'xl'=2,'z'=4,'xh'=2,'core'=2] {'y','xl'}, dimensions={0} | all-to-all | bytes 589824 | tf_op jit(solution)/shard_map/all_to_all | solution.py:249
  81.1 4.3 %shard_map.92 = (f32[64,128]{1,0:T(8,128)}, f32[64,128]{1,0:T(8,128)}, f32[64,128]{1,0:T(8,128)}) custom-call(f32[8,72,128]{2,1,0:T(8,128)S(1)} %all_to_all.22.pieces, f32[64,64]{1,0:T(8,128)S(1)} %get-tuple-element.26.gram, f32[64,64]{1,0:T(8,128)S(1)} %get-tuple-element.28.inverse, f32[64,128]{1,0:T(8,128)S(1)} %get-tuple-element.29.image, ...), custom_call_target="tpu_custom_call" | custom-call | flops 1000000 | bytes 1000000 | tf_op jit(solution)/shard_map/pallas_call | solution.py:297
  (2 shorter events, 0.1 us)
Async XLA Ops:
  3.4 7.3 %copy-start.1 = (f32[232,128]{1,0:T(8,128)S(1)}, f32[232,128]{1,0:T(8,128)}, u32[]{:S(2)}) copy-start(f32[232,128]{1,0:T(8,128)} %get-tuple-element.19.refs_0_) | copy-start | bytes 356356
  3.4 23.0 %all-to-all-start = ((f32[16,128,128]{2,1,0:T(8,128)}), f32[16,128,128]{2,1,0:T(8,128)S(1)}, u32[]{:S(2)}, u32[]{:S(2)}) async-start(f32[16,128,128]{2,1,0:T(8,128)} %get-tuple-element.18), calls=%async_computation | async-start | bytes 2097152 | tf_op jit(solution)/shard_map/all_to_all | solution.py:249
  10.7 8.9 %collective-permute-start.2 = (f32[232,128]{1,0:T(8,128)S(1)}, f32[232,128]{1,0:T(8,128)S(1)}, u32[]{:S(2)}, u32[]{:S(2)}) collective-permute-start(f32[232,128]{1,0:T(8,128)S(1)} %copy-done.1), channel_id=1, source_target_pairs={{0,12},{4,8},{8,4},{12,0},{1,13},{5,9},{9,5},{13,1},{2,14},{6,10},... | collective-permute-start | bytes 356360 | tf_op jit(solution)/shard_map/ppermute | solution.py:245
  14.8 7.2 %collective-permute-start.1 = (f32[232,128]{1,0:T(8,128)S(1)}, f32[232,128]{1,0:T(8,128)S(1)}, u32[]{:S(2)}, u32[]{:S(2)}) collective-permute-start(f32[232,128]{1,0:T(8,128)S(1)} %copy-done.1), channel_id=1, source_target_pairs={{0,8},{4,12},{8,0},{12,4},{1,9},{5,13},{9,1},{13,5},{2,10},{6,14},... | collective-permute-start | bytes 356360 | tf_op jit(solution)/shard_map/ppermute | solution.py:245
  14.8 7.2 %collective-permute-start = (f32[232,128]{1,0:T(8,128)S(1)}, f32[232,128]{1,0:T(8,128)S(1)}, u32[]{:S(2)}, u32[]{:S(2)}) collective-permute-start(f32[232,128]{1,0:T(8,128)S(1)} %copy-done.1), channel_id=1, source_target_pairs={{0,4},{4,0},{8,12},{12,8},{1,5},{5,1},{9,13},{13,9},{2,6},{6,2},{1... | collective-permute-start | bytes 356360 | tf_op jit(solution)/shard_map/ppermute | solution.py:245
  15.8 6.8 %collective-permute-start.3 = (f32[232,128]{1,0:T(8,128)S(1)}, f32[232,128]{1,0:T(8,128)S(1)}, u32[]{:S(2)}, u32[]{:S(2)}) collective-permute-start(f32[232,128]{1,0:T(8,128)S(1)} %copy-done.1), channel_id=1, source_target_pairs={{0,1},{1,0},{2,3},{3,2},{4,5},{5,4},{6,7},{7,6},{8,9},{9,8},{10,11... | collective-permute-start | bytes 356360 | tf_op jit(solution)/shard_map/ppermute | solution.py:241
  19.6 2.9 %collective-permute-start.6 = (f32[232,128]{1,0:T(8,128)S(1)}, f32[232,128]{1,0:T(8,128)S(1)}, u32[]{:S(2)}, u32[]{:S(2)}) collective-permute-start(f32[232,128]{1,0:T(8,128)S(1)} %collective-permute-done.2.refs_3_), channel_id=1, source_target_pairs={{0,1},{1,0},{2,3},{3,2},{4,5},{5,4},{6,7},{7,6},{8,9},{9,8},{10,11... | collective-permute-start | bytes 356360 | tf_op jit(solution)/shard_map/ppermute | solution.py:241
  22.0 1.3 %collective-permute-start.5 = (f32[232,128]{1,0:T(8,128)S(1)}, f32[232,128]{1,0:T(8,128)S(1)}, u32[]{:S(2)}, u32[]{:S(2)}) collective-permute-start(f32[232,128]{1,0:T(8,128)S(1)} %collective-permute-done.1.refs_2_), channel_id=1, source_target_pairs={{0,1},{1,0},{2,3},{3,2},{4,5},{5,4},{6,7},{7,6},{8,9},{9,8},{10,11... | collective-permute-start | bytes 356360 | tf_op jit(solution)/shard_map/ppermute | solution.py:241
  22.0 1.5 %collective-permute-start.4 = (f32[232,128]{1,0:T(8,128)S(1)}, f32[232,128]{1,0:T(8,128)S(1)}, u32[]{:S(2)}, u32[]{:S(2)}) collective-permute-start(f32[232,128]{1,0:T(8,128)S(1)} %collective-permute-done.refs_1_), channel_id=1, source_target_pairs={{0,1},{1,0},{2,3},{3,2},{4,5},{5,4},{6,7},{7,6},{8,9},{9,8},{10,11... | collective-permute-start | bytes 356360 | tf_op jit(solution)/shard_map/ppermute | solution.py:241
  33.8 18.9 %copy-start = (f32[200,128]{1,0:T(8,128)S(1)}, f32[200,128]{1,0:T(8,128)}, u32[]{:S(2)}) copy-start(f32[200,128]{1,0:T(8,128)} %get-tuple-element.24.kept) | copy-start | bytes 307204
  53.2 2.0 %collective-permute-start.7 = (f32[72,128]{1,0:T(8,128)S(1)}, f32[72,128]{1,0:T(8,128)S(1)}, u32[]{:S(2)}, u32[]{:S(2)}) collective-permute-start(f32[72,128]{1,0:T(8,128)S(1)} %get-tuple-element.25.a), channel_id=1, source_target_pairs={{0,1},{1,0},{2,3},{3,2},{4,5},{5,4},{6,7},{7,6},{8,9},{9,8},{10,11... | collective-permute-start | bytes 110600 | tf_op jit(solution)/shard_map/ppermute | solution.py:241

commit v5 on v4

--- a/solution.py
+++ b/solution.py
@@ -8,13 +8,10 @@
 from jax.sharding import Mesh, PartitionSpec as P
 
 AXES = ("y", "xl", "z", "xh", "core")
-BLK = ("y", "xl")
-CHIPS = ("z", "xh")
 PLANE = ("y", "xl", "xh")
 N = 128
 F = 128
 Q = 64
-G = 8
 R = 16
 C = 8
 TILE = 1024
@@ -131,7 +128,8 @@
             kernel = jnp.exp2(inner - half - halves[0:1, at])
             high = kernel.astype(jnp.bfloat16)
             rest = (kernel - high.astype(jnp.float32)).astype(jnp.bfloat16)
-            total += dot(high, dirs[:, at], 1, 1, None) + dot(rest, dirs[:, at], 1, 1, None)
+            weights = jnp.concatenate([dirs[:, at], dirs[:, at]], axis=1)
+            total += dot(jnp.concatenate([high, rest], axis=1), weights, 1, 1, None)
         total += pltpu.roll(total, Q, 1)
         for b in range(per):
             out[i * per + b, :Q] = fold(total[b * N : (b + 1) * N])
@@ -206,16 +204,14 @@
     out[...] = eliminate(jnp.concatenate([gram[...], diagonal((Q, Q)).astype(jnp.float32)], axis=1))
 
 
-def pair_sum(a, b, inverse, out, inverse_out):
+def z_sum(a, b, c, d, inverse, out, inverse_out):
     inverse_out[...] = inverse[...]
+    out[...] = (a[...] + b[...]) + (c[...] + d[...])
+
+
+def pair_sum(a, b, out):
     total = a[...] + b[...]
-    for j in range(G):
-        out[j] = total
-
-
-def chip_sum(pieces, out):
-    total = summed(pieces)
-    for j in range(G):
+    for j in range(R):
         out[j] = total
 
 
@@ -291,9 +287,11 @@
         exchanged(sent, PLANE), kept
     )
     inverse = call(invert, f32(Q, Q), flops=10**8)(gram)
-    both, inverse = call(pair_sum, [f32(G, SUMS, 128), f32(Q, Q)])(sums, swapped(sums), inverse)
-    by_chip = call(chip_sum, f32(G, SUMS, 128))(exchanged(both, CHIPS))
-    whole = exchanged(by_chip, BLK)
+    column, inverse = call(z_sum, [f32(SUMS, 128), f32(Q, Q)])(
+        sums, *[across(sums, k) for k in range(1, 4)], inverse
+    )
+    both = call(pair_sum, f32(R, SUMS, 128))(column, swapped(column))
+    whole = exchanged(both, PLANE)
     outs = call(finish, [f32(Q, N)] * 3)(whole, gram, inverse, image, kept)
     return tuple(o.T for o in outs)
 

time: 85.7 us -> 83.9 us (0.979)
  blocking collectives: 44.7 us -> 34.8 us
  starting transfers between devices: 13 us -> 17.6 us
  waiting for transfers between devices: 9.89 us -> 13.8 us
    all_to_all x3 -> x2, blocking collectives: 44.7 us -> 34.8 us  [exchanged(): return lax.all_to_all(value, axes, 0, 0, tiled=True)]
    ppermute x3 -> x6, starting transfers between devices: 5.07 us -> 9.68 us  [across(): return lax.ppermute(value, 'z', [(i, i ^ k) for i in range(4)])]
    ppermute x3 -> x6, waiting for transfers between devices: 6.24 us -> 8.89 us  [across(): return lax.ppermute(value, 'z', [(i, i ^ k) for i in range(4)])]
    ppermute x5, waiting for transfers between devices: 0.99 us -> 2.18 us  [swapped(): return lax.ppermute(value, 'core', [(0, 1), (1, 0)])]
  transfers between devices with their start and end apart: 9 -> 12, of which waited for: 5 -> 7; matrix products, arithmetic and copies ran while one was open for 0% -> 0% of each run, Pallas kernels for 2% -> 2%
where the time goes in v5:
time: 83.9 us; the launch traced here: 83.5 us
  blocking collectives  34.8 us (41%)
  starting transfers between devices  17.6 us (21%)
  Pallas kernels  16 us (19%)
  waiting for transfers between devices  13.8 us (16%)
  between operations  1.36 us (2%)
    all_to_all x2, blocking collectives, exchanged(): return lax.all_to_all(value, axes, 0, 0, tiled=True)  34.8 us
    ppermute x6, starting transfers between devices, across(): return lax.ppermute(value, 'z', [(i, i ^ k) for i in range(4)])  9.68 us
    ppermute x6, waiting for transfers between devices, across(): return lax.ppermute(value, 'z', [(i, i ^ k) for i in range(4)])  8.89 us
    all_to_all x1, starting transfers between devices, exchanged(): return lax.all_to_all(value, axes, 0, 0, tiled=True)  7.29 us
    pallas_call x1, Pallas kernels, on_device(): call(products, f32(R, Q + Q // 2, 128), [pltpu.VMEM((TILE, 6 * F), jnp.bf...  6.87 us
    pallas_call x1, Pallas kernels, on_device(): outs = call(finish, [f32(Q, N)] * 3)(whole, gram, inverse, image, kept)  4.31 us
    all_to_all x1, waiting for transfers between devices, exchanged(): return lax.all_to_all(value, axes, 0, 0, tiled=True)  2.67 us
    ppermute x5, waiting for transfers between devices, swapped(): return lax.ppermute(value, 'core', [(0, 1), (1, 0)])  2.18 us
  transfers between devices with their start and end apart: 12, of which 7 were waited for; matrix products, arithmetic and copies ran while one was open for 0% of the time, Pallas kernels for 2%

profile of v5, /device:TPU:0, one launch (start us, length us, event | category | flops | bytes accessed | tf_op | source)
XLA Modules:
  0.0 83.5 jit_solution(11940717623212532262)
XLA Ops:
  1.3 2.1 %shard_map.85 = (f32[16,128,128]{2,1,0:T(8,128)}, f32[232,128]{1,0:T(8,128)}, f32[200,128]{1,0:T(8,128)}) custom-call(f32[128,128]{1,0:T(8,128)} %points.1, f32[1,128]{1,0:T(1,128)} %bitcast.10, f32[1]{0:T(128)S(6)} %copy.9.noise, f32[64,128]{1,0:T(8,128)} %bitcast.7, f32[64,128]{1,0:T(8,128)} %bitcast.8, f32[64,128]{1,0:T(8,128)} %bitcast.9), custom_call_target="tpu_custom_call" | custom-call | flops 1000000 | bytes 1000000 | tf_op jit(solution)/shard_map/pallas_call | solution.py:249
  3.4 0.0 copy-start.1
  3.4 7.3 %all-to-all-start = ((f32[16,128,128]{2,1,0:T(8,128)}), f32[16,128,128]{2,1,0:T(8,128)S(1)}, u32[]{:S(2)}, u32[]{:S(2)}) async-start(f32[16,128,128]{2,1,0:T(8,128)} %get-tuple-element.18), calls=%async_computation | async-start | bytes 2097152 | tf_op jit(solution)/shard_map/all_to_all | solution.py:245
  10.7 0.0 copy-done.1
  10.7 4.1 %collective-permute-start.2 = (f32[232,128]{1,0:T(8,128)S(1)}, f32[232,128]{1,0:T(8,128)S(1)}, u32[]{:S(2)}, u32[]{:S(2)}) collective-permute-start(f32[232,128]{1,0:T(8,128)S(1)} %copy-done.1), channel_id=1, source_target_pairs={{0,12},{4,8},{8,4},{12,0},{1,13},{5,9},{9,5},{13,1},{2,14},{6,10},... | collective-permute-start | bytes 356360 | tf_op jit(solution)/shard_map/ppermute | solution.py:241
  14.8 0.0 collective-permute-start.1
  14.8 0.9 %collective-permute-start = (f32[232,128]{1,0:T(8,128)S(1)}, f32[232,128]{1,0:T(8,128)S(1)}, u32[]{:S(2)}, u32[]{:S(2)}) collective-permute-start(f32[232,128]{1,0:T(8,128)S(1)} %copy-done.1), channel_id=1, source_target_pairs={{0,4},{4,0},{8,12},{12,8},{1,5},{5,1},{9,13},{13,9},{2,6},{6,2},{1... | collective-permute-start | bytes 356360 | tf_op jit(solution)/shard_map/ppermute | solution.py:241
  15.8 0.0 collective-permute-start.3
  15.8 3.8 %collective-permute-done.2.refs_3_ = f32[232,128]{1,0:T(8,128)S(1)} collective-permute-done((f32[232,128]{1,0:T(8,128)S(1)}, f32[232,128]{1,0:T(8,128)S(1)}, u32[]{:S(2)}, u32[]{:S(2)}) %collective-permute-start.2) | collective-permute-done | bytes 118816 | tf_op jit(solution)/shard_map/ppermute | solution.py:241
  19.6 0.0 collective-permute-start.6
  19.6 2.4 %collective-permute-done.1.refs_2_ = f32[232,128]{1,0:T(8,128)S(1)} collective-permute-done((f32[232,128]{1,0:T(8,128)S(1)}, f32[232,128]{1,0:T(8,128)S(1)}, u32[]{:S(2)}, u32[]{:S(2)}) %collective-permute-start.1) | collective-permute-done | bytes 118816 | tf_op jit(solution)/shard_map/ppermute | solution.py:241
  22.0 0.0 collective-permute-start.5
  22.0 0.0 collective-permute-done.refs_1_
  22.0 0.5 collective-permute-start.4
  22.5 0.0 collective-permute-done.3.refs_4_
  22.5 0.0 collective-permute-done.6.refs_7_
  22.6 0.8 collective-permute-done.5.refs_6_
  23.4 0.2 collective-permute-done.4.refs_5_
  23.5 0.2 shard_map.86
  23.7 2.7 %all-to-all-done.rows = f32[16,128,128]{2,1,0:T(8,128)S(1)} async-done(((f32[16,128,128]{2,1,0:T(8,128)}), f32[16,128,128]{2,1,0:T(8,128)S(1)}, u32[]{:S(2)}, u32[]{:S(2)}) %all-to-all-start) | async-done | bytes 1048608 | tf_op jit(solution)/shard_map/all_to_all | solution.py:245
  26.4 6.9 %shard_map.87 = f32[16,96,128]{2,1,0:T(8,128)S(1)} custom-call(f32[16,128,128]{2,1,0:T(8,128)S(1)} %all-to-all-done.rows, bf16[1024,768]{1,0:T(8,128)(2,1)S(1)} %get-tuple-element.20.right, bf16[128,1024]{1,0:T(8,128)(2,1)S(1)} %get-tuple-element.21.dirs, f32[8,1024]{1,0:T(8,128)S(1)} %get-tuple-element.22.halves, f32[32,128]{1,0:T(8,128)S(1)} %get-tuple-element.23.gram), custom_call_target="tpu_custom_call" | custom-call | flops 8000000000 | bytes 1000000 | tf_op jit(solution)/shard_map/pallas_call | solution.py:279
  33.3 0.0 copy-start
  33.3 18.9 %all_to_all.15.pieces = f32[16,96,128]{2,1,0:T(8,128)S(1)} all-to-all(f32[16,96,128]{2,1,0:T(8,128)S(1)} %shard_map.87), channel_id=1, replica_groups=mesh['y'=4,'xl'=2,'z'=4,'xh'=2,'core'=2] {'y','xl','xh'}, dimensions={0} | all-to-all | bytes 1572864 | tf_op jit(solution)/shard_map/all_to_all | solution.py:245
  52.2 0.0 copy-done
  52.2 0.6 shard_map.88
  52.7 3.7 %collective-permute-start.9 = (f32[72,128]{1,0:T(8,128)S(1)}, f32[72,128]{1,0:T(8,128)S(1)}, u32[]{:S(2)}, u32[]{:S(2)}) collective-permute-start(f32[72,128]{1,0:T(8,128)S(1)} %get-tuple-element.25.a), channel_id=1, source_target_pairs={{0,12},{4,8},{8,4},{12,0},{1,13},{5,9},{9,5},{13,1},{2,14},{6,10},... | collective-permute-start | bytes 110600 | tf_op jit(solution)/shard_map/ppermute | solution.py:241
  56.4 0.0 collective-permute-start.8
  56.4 0.9 %collective-permute-start.7 = (f32[72,128]{1,0:T(8,128)S(1)}, f32[72,128]{1,0:T(8,128)S(1)}, u32[]{:S(2)}, u32[]{:S(2)}) collective-permute-start(f32[72,128]{1,0:T(8,128)S(1)} %get-tuple-element.25.a), channel_id=1, source_target_pairs={{0,4},{4,0},{8,12},{12,8},{1,5},{5,1},{9,13},{13,9},{2,6},{6,2},{1... | collective-permute-start | bytes 110600 | tf_op jit(solution)/shard_map/ppermute | solution.py:241
  57.4 1.9 %shard_map.89.inverse = f32[64,64]{1,0:T(8,128)S(1)} custom-call(f32[64,64]{1,0:T(8,128)S(1)} %get-tuple-element.26.gram), custom_call_target="tpu_custom_call" | custom-call | flops 100000000 | bytes 1000000 | tf_op jit(solution)/shard_map/pallas_call | solution.py:289
  59.2 0.0 collective-permute-done.9.d
  59.2 2.7 %collective-permute-done.8.c = f32[72,128]{1,0:T(8,128)S(1)} collective-permute-done((f32[72,128]{1,0:T(8,128)S(1)}, f32[72,128]{1,0:T(8,128)S(1)}, u32[]{:S(2)}, u32[]{:S(2)}) %collective-permute-start.8) | collective-permute-done | bytes 36896 | tf_op jit(solution)/shard_map/ppermute | solution.py:241
  61.9 0.0 collective-permute-done.7.b
  61.9 0.1 collective-permute-start.10
  62.0 1.2 %collective-permute-done.10.b = f32[72,128]{1,0:T(8,128)S(1)} collective-permute-done((f32[72,128]{1,0:T(8,128)S(1)}, f32[72,128]{1,0:T(8,128)S(1)}, u32[]{:S(2)}, u32[]{:S(2)}) %collective-permute-start.10) | collective-permute-done | bytes 36896 | tf_op jit(solution)/shard_map/ppermute | solution.py:237
  63.2 16.0 %all_to_all.16.pieces = f32[16,72,128]{2,1,0:T(8,128)S(1)} all-to-all(f32[16,72,128]{2,1,0:T(8,128)S(1)} %shard_map.91), channel_id=1, replica_groups=mesh['y'=4,'xl'=2,'z'=4,'xh'=2,'core'=2] {'y','xl','xh'}, dimensions={0} | all-to-all | bytes 1179648 | tf_op jit(solution)/shard_map/all_to_all | solution.py:245
  79.2 4.3 %shard_map.92 = (f32[64,128]{1,0:T(8,128)}, f32[64,128]{1,0:T(8,128)}, f32[64,128]{1,0:T(8,128)}) custom-call(f32[16,72,128]{2,1,0:T(8,128)S(1)} %all_to_all.16.pieces, f32[64,64]{1,0:T(8,128)S(1)} %get-tuple-element.26.gram, f32[64,64]{1,0:T(8,128)S(1)} %get-tuple-element.28.inverse, f32[64,128]{1,0:T(8,128)S(1)} %get-tuple-element.29.image, ...), custom_call_target="tpu_custom_call" | custom-call | flops 1000000 | bytes 1000000 | tf_op jit(solution)/shard_map/pallas_call | solution.py:295
  (2 shorter events, 0.1 us)
Async XLA Ops:
  3.4 7.3 %copy-start.1 = (f32[232,128]{1,0:T(8,128)S(1)}, f32[232,128]{1,0:T(8,128)}, u32[]{:S(2)}) copy-start(f32[232,128]{1,0:T(8,128)} %get-tuple-element.19.refs_0_) | copy-start | bytes 356356
  3.4 23.0 %all-to-all-start = ((f32[16,128,128]{2,1,0:T(8,128)}), f32[16,128,128]{2,1,0:T(8,128)S(1)}, u32[]{:S(2)}, u32[]{:S(2)}) async-start(f32[16,128,128]{2,1,0:T(8,128)} %get-tuple-element.18), calls=%async_computation | async-start | bytes 2097152 | tf_op jit(solution)/shard_map/all_to_all | solution.py:245
  10.7 8.9 %collective-permute-start.2 = (f32[232,128]{1,0:T(8,128)S(1)}, f32[232,128]{1,0:T(8,128)S(1)}, u32[]{:S(2)}, u32[]{:S(2)}) collective-permute-start(f32[232,128]{1,0:T(8,128)S(1)} %copy-done.1), channel_id=1, source_target_pairs={{0,12},{4,8},{8,4},{12,0},{1,13},{5,9},{9,5},{13,1},{2,14},{6,10},... | collective-permute-start | bytes 356360 | tf_op jit(solution)/shard_map/ppermute | solution.py:241
  14.8 7.2 %collective-permute-start.1 = (f32[232,128]{1,0:T(8,128)S(1)}, f32[232,128]{1,0:T(8,128)S(1)}, u32[]{:S(2)}, u32[]{:S(2)}) collective-permute-start(f32[232,128]{1,0:T(8,128)S(1)} %copy-done.1), channel_id=1, source_target_pairs={{0,8},{4,12},{8,0},{12,4},{1,9},{5,13},{9,1},{13,5},{2,10},{6,14},... | collective-permute-start | bytes 356360 | tf_op jit(solution)/shard_map/ppermute | solution.py:241
  14.8 7.2 %collective-permute-start = (f32[232,128]{1,0:T(8,128)S(1)}, f32[232,128]{1,0:T(8,128)S(1)}, u32[]{:S(2)}, u32[]{:S(2)}) collective-permute-start(f32[232,128]{1,0:T(8,128)S(1)} %copy-done.1), channel_id=1, source_target_pairs={{0,4},{4,0},{8,12},{12,8},{1,5},{5,1},{9,13},{13,9},{2,6},{6,2},{1... | collective-permute-start | bytes 356360 | tf_op jit(solution)/shard_map/ppermute | solution.py:241
  15.8 6.8 %collective-permute-start.3 = (f32[232,128]{1,0:T(8,128)S(1)}, f32[232,128]{1,0:T(8,128)S(1)}, u32[]{:S(2)}, u32[]{:S(2)}) collective-permute-start(f32[232,128]{1,0:T(8,128)S(1)} %copy-done.1), channel_id=1, source_target_pairs={{0,1},{1,0},{2,3},{3,2},{4,5},{5,4},{6,7},{7,6},{8,9},{9,8},{10,11... | collective-permute-start | bytes 356360 | tf_op jit(solution)/shard_map/ppermute | solution.py:237
  19.6 2.9 %collective-permute-start.6 = (f32[232,128]{1,0:T(8,128)S(1)}, f32[232,128]{1,0:T(8,128)S(1)}, u32[]{:S(2)}, u32[]{:S(2)}) collective-permute-start(f32[232,128]{1,0:T(8,128)S(1)} %collective-permute-done.2.refs_3_), channel_id=1, source_target_pairs={{0,1},{1,0},{2,3},{3,2},{4,5},{5,4},{6,7},{7,6},{8,9},{9,8},{10,11... | collective-permute-start | bytes 356360 | tf_op jit(solution)/shard_map/ppermute | solution.py:237
  22.0 1.3 %collective-permute-start.5 = (f32[232,128]{1,0:T(8,128)S(1)}, f32[232,128]{1,0:T(8,128)S(1)}, u32[]{:S(2)}, u32[]{:S(2)}) collective-permute-start(f32[232,128]{1,0:T(8,128)S(1)} %collective-permute-done.1.refs_2_), channel_id=1, source_target_pairs={{0,1},{1,0},{2,3},{3,2},{4,5},{5,4},{6,7},{7,6},{8,9},{9,8},{10,11... | collective-permute-start | bytes 356360 | tf_op jit(solution)/shard_map/ppermute | solution.py:237
  22.0 1.5 %collective-permute-start.4 = (f32[232,128]{1,0:T(8,128)S(1)}, f32[232,128]{1,0:T(8,128)S(1)}, u32[]{:S(2)}, u32[]{:S(2)}) collective-permute-start(f32[232,128]{1,0:T(8,128)S(1)} %collective-permute-done.refs_1_), channel_id=1, source_target_pairs={{0,1},{1,0},{2,3},{3,2},{4,5},{5,4},{6,7},{7,6},{8,9},{9,8},{10,11... | collective-permute-start | bytes 356360 | tf_op jit(solution)/shard_map/ppermute | solution.py:237
  33.3 18.9 %copy-start = (f32[200,128]{1,0:T(8,128)S(1)}, f32[200,128]{1,0:T(8,128)}, u32[]{:S(2)}) copy-start(f32[200,128]{1,0:T(8,128)} %get-tuple-element.24.kept) | copy-start | bytes 307204
  52.7 6.5 %collective-permute-start.9 = (f32[72,128]{1,0:T(8,128)S(1)}, f32[72,128]{1,0:T(8,128)S(1)}, u32[]{:S(2)}, u32[]{:S(2)}) collective-permute-start(f32[72,128]{1,0:T(8,128)S(1)} %get-tuple-element.25.a), channel_id=1, source_target_pairs={{0,12},{4,8},{8,4},{12,0},{1,13},{5,9},{9,5},{13,1},{2,14},{6,10},... | collective-permute-start | bytes 110600 | tf_op jit(solution)/shard_map/ppermute | solution.py:241
  56.4 5.5 %collective-permute-start.8 = (f32[72,128]{1,0:T(8,128)S(1)}, f32[72,128]{1,0:T(8,128)S(1)}, u32[]{:S(2)}, u32[]{:S(2)}) collective-permute-start(f32[72,128]{1,0:T(8,128)S(1)} %get-tuple-element.25.a), channel_id=1, source_target_pairs={{0,8},{4,12},{8,0},{12,4},{1,9},{5,13},{9,1},{13,5},{2,10},{6,14},... | collective-permute-start | bytes 110600 | tf_op jit(solution)/shard_map/ppermute | solution.py:241
  56.4 5.5 %collective-permute-start.7 = (f32[72,128]{1,0:T(8,128)S(1)}, f32[72,128]{1,0:T(8,128)S(1)}, u32[]{:S(2)}, u32[]{:S(2)}) collective-permute-start(f32[72,128]{1,0:T(8,128)S(1)} %get-tuple-element.25.a), channel_id=1, source_target_pairs={{0,4},{4,0},{8,12},{12,8},{1,5},{5,1},{9,13},{13,9},{2,6},{6,2},{1... | collective-permute-start | bytes 110600 | tf_op jit(solution)/shard_map/ppermute | solution.py:241
  61.9 1.3 %collective-permute-start.10 = (f32[72,128]{1,0:T(8,128)S(1)}, f32[72,128]{1,0:T(8,128)S(1)}, u32[]{:S(2)}, u32[]{:S(2)}) collective-permute-start(f32[72,128]{1,0:T(8,128)S(1)} %get-tuple-element.27.a), channel_id=1, source_target_pairs={{0,1},{1,0},{2,3},{3,2},{4,5},{5,4},{6,7},{7,6},{8,9},{9,8},{10,11... | collective-permute-start | bytes 110600 | tf_op jit(solution)/shard_map/ppermute | solution.py:237

commit v6 on v5

v6 whole, which is shorter than its diff:
```python
import math

import jax
import jax.numpy as jnp
from jax import lax
from jax.experimental import pallas as pl
from jax.experimental.pallas import tpu as pltpu
from jax.sharding import Mesh, PartitionSpec as P

AXES = ("y", "xl", "z", "xh", "core")
PLANE = ("y", "xl", "xh")
N = 128
F = 128
Q = 64
R = 16
Z = 4
CHUNK = 256
H = Q // 2
HI = lax.Precision.HIGHEST
ROOT = math.sqrt(math.log2(math.e))
DIRS = N + Q
COLS = DIRS + 8
ROWS = DIRS + Q
ITER, RES, DIR = 0, Q, 2 * Q
DIAG, GRAM, SUMS = Q, Q + 8, Q + 32
SMEM = pl.BlockSpec(memory_space=pltpu.SMEM)
HBM = pl.BlockSpec(memory_space=pltpu.MemorySpace.HBM)
ROOM = 62
VM = pl.BlockSpec(memory_space=pltpu.VMEM)


def call(body, outs, scratch=(), flops=10**6, room=4, ins=None):
    return pl.pallas_call(
        body,
        out_shape=outs,
        **({} if ins is None else {"in_specs": ins}),
        out_specs=jax.tree.map(lambda _: VM, outs),
        scratch_shapes=list(scratch),
        compiler_params=pltpu.CompilerParams(vmem_limit_bytes=room * 2**20),
        cost_estimate=pl.CostEstimate(flops=flops, bytes_accessed=10**6, transcendentals=0),
    )


def f32(*shape):
    return jax.ShapeDtypeStruct(shape, jnp.float32)


def dot(a, b, ca=1, cb=0, precision=HI):
    return lax.dot_general(
        a, b, (((ca,), (cb,)), ((), ())), precision=precision, preferred_element_type=jnp.float32
    )


def low_lanes(shape):
    return lax.broadcasted_iota(jnp.int32, shape, 1) < Q


def fold(wide):
    half = wide.shape[0] // 2
    return jnp.where(low_lanes((half, 128)), wide[:half], wide[half:])


def unfold(packed):
    return jnp.concatenate([packed[:, :Q], packed[:, Q:]], axis=0)


def prep(points, scales, iterate, residual, direction, rows, cols, kept, place, sems):
    points_in, scales_in = place
    copies = [
        pltpu.make_async_copy(points, points_in, sems.at[0]),
        pltpu.make_async_copy(scales, scales_in, sems.at[1]),
        pltpu.make_async_copy(residual, kept.at[RES : RES + Q], sems.at[2]),
        pltpu.make_async_copy(direction, kept.at[DIR : DIR + Q], sems.at[3]),
        pltpu.make_async_copy(iterate, kept.at[ITER : ITER + Q], sems.at[4]),
    ]
    for copy in copies:
        copy.start()
    for copy in copies[:2]:
        copy.wait()
    unit = points_in[...] / scales_in[...] * ROOT
    half = 0.5 * jnp.sum(unit * unit, axis=1, keepdims=True)
    as_row = jnp.broadcast_to(half, (N, N)).T[:8]
    for copy in copies[2:]:
        copy.wait()
    for i in range(R):
        cols[i, :N] = unit
        cols[i, N:DIRS] = kept[DIR : DIR + Q]
        cols[i, DIRS:] = as_row
    rows[:N] = unit
    rows[N:DIRS] = kept[DIR : DIR + Q]
    rows[DIRS:] = kept[RES : RES + Q]


def split(value):
    top = value.astype(jnp.bfloat16)
    rest = value - top.astype(jnp.float32)
    mid = rest.astype(jnp.bfloat16)
    low = (rest - mid.astype(jnp.float32)).astype(jnp.bfloat16)
    return top, mid, low


def halved(residual):
    wide = dot(residual, jnp.concatenate([residual, residual], axis=0), 1, 1)
    corner = dot(residual[H:], jnp.concatenate([residual[H:]] * 4, axis=0), 1, 1)
    group = lax.broadcasted_iota(jnp.int32, (8, 128), 1) // H
    last = corner[:8]
    for g in range(1, 4):
        last = jnp.where(group == g, corner[8 * g : 8 * g + 8], last)
    return jnp.concatenate([fold(wide[:H]), last], axis=0)


def restored(packed):
    top = unfold(packed[:16])
    corner = jnp.concatenate([packed[16:, H * g : H * (g + 1)] for g in range(4)], axis=0)
    under = jnp.concatenate([jnp.zeros((H, H), jnp.float32), corner], axis=1)
    full = jnp.concatenate([top, under], axis=0)
    row = lax.broadcasted_iota(jnp.int32, (Q, Q), 0)
    column = lax.broadcasted_iota(jnp.int32, (Q, Q), 1)
    return jnp.where((row >= H) & (column < H), full.T, full)


def spread_rows(a, b, c, d, left, halves, side, gram):
    for k, rows in enumerate((a, b, c, d)):
        at = slice(k * N, (k + 1) * N)
        unit = rows[:N]
        top, mid, low = split(unit)
        left[at] = jnp.concatenate([top, top, mid, top, low, mid], axis=1)
        half = 0.5 * jnp.sum(unit * unit, axis=1, keepdims=True)
        halves[at] = jnp.broadcast_to(half, (N, CHUNK))
        side[:, at] = rows[N:]
    residual = side[Q:]
    gram[...] = halved(residual)


def partial(left, own, cols, right, dirs, halves):
    for j in range(R):
        at = slice(j * N, (j + 1) * N)
        top, mid, low = split(cols[j, :N])
        right[at] = jnp.concatenate([top, mid, top, low, top, mid], axis=1)
        high, rest, _ = split(cols[j, N:DIRS])
        dirs[:, at] = jnp.concatenate([high, rest], axis=0)
        halves[:, at] = cols[j, DIRS:]
    total = jnp.zeros((Z * N, 2 * Q), jnp.float32)
    for j in range(R * N // CHUNK):
        at = slice(j * CHUNK, (j + 1) * CHUNK)
        inner = dot(left[...], right[at], 1, 1, None)
        kernel = jnp.exp2(inner - own[...] - halves[0:1, at])
        high = kernel.astype(jnp.bfloat16)
        rest = (kernel - high.astype(jnp.float32)).astype(jnp.bfloat16)
        weights = jnp.concatenate([dirs[:, at], dirs[:, at]], axis=1)
        total += dot(jnp.concatenate([high, rest], axis=1), weights, 1, 1, None)
    return total


def products_first(left, own, cols, out, right, dirs, halves):
    out[...] = partial(left, own, cols, right, dirs, halves)


def products_last(left, own, cols, before, out, right, dirs, halves):
    total = before[...] + partial(left, own, cols, right, dirs, halves)
    total += pltpu.roll(total, Q, 1)
    for k in range(Z):
        out[k * Q : (k + 1) * Q] = fold(total[k * N : (k + 1) * N])


def summed(pieces):
    total = pieces[0]
    for j in range(1, pieces.shape[0]):
        total += pieces[j]
    return total


def lower(shape):
    return lax.broadcasted_iota(jnp.int32, shape, 0) > lax.broadcasted_iota(jnp.int32, shape, 1)


def diagonal(shape):
    return lax.broadcasted_iota(jnp.int32, shape, 0) == lax.broadcasted_iota(jnp.int32, shape, 1)


def grams(a, b, c, d, sides, res_gram, noise, image_out, sums):
    pieces = (a, b, c, d)
    parts = []
    for k in range(Z):
        total = a[k * Q : (k + 1) * Q]
        for place in range(1, Z):
            total += pieces[place][(k ^ place) * Q : ((k ^ place) + 1) * Q]
        turned = total.T
        parts += [turned[:Q], turned[Q:]]
    direction = sides[:Q]
    image = jnp.concatenate(parts, axis=1) + noise[0, 0] * direction
    image_out[...] = image[:, :N]
    wide = dot(image, jnp.concatenate([sides[...], image], axis=0), 1, 1)
    gram = 0.5 * (wide[:, :Q] + dot(direction, image, 1, 1))
    cross, square = wide[:, Q : 2 * Q], wide[:, 2 * Q :]
    both = jnp.where(lower((Q, Q)), gram, square)
    sums[:Q] = jnp.concatenate([cross, both], axis=1)
    along = jnp.sum(jnp.where(diagonal((Q, Q)), gram, 0.0), axis=0, keepdims=True)
    sums[DIAG:GRAM] = jnp.broadcast_to(jnp.concatenate([along, along], axis=1), (8, 128))
    sums[GRAM:] = res_gram[...]


def eliminate(*matrices):
    sub = lax.broadcasted_iota(jnp.int32, (8, 128), 0)
    each = range(len(matrices))
    slabs = [[m[8 * r : 8 * r + 8] for r in range(8)] for m in matrices]
    for k in range(8):
        spread = [
            [
                [
                    jnp.broadcast_to(slabs[m][r][:, 8 * k + j : 8 * k + j + 1], (8, 128))
                    for j in range(8)
                ]
                for r in range(8)
            ]
            for m in each
        ]
        own = [spread[m][k] for m in each]
        pivot = [slabs[m][k] for m in each]
        for j in range(8):
            inverse = [1.0 / jnp.broadcast_to(own[m][j][j : j + 1], (8, 128)) for m in each]

            def cleared(value, m):
                row = jnp.broadcast_to(value[j : j + 1], (8, 128)) * inverse[m]
                return jnp.where(sub == j, row, value - own[m][j] * row)

            pivot = [cleared(pivot[m], m) for m in each]
            own = [own[m][: j + 1] + [cleared(c, m) for c in own[m][j + 1 :]] for m in each]
        for r in range(8):
            if r != k:
                for j in range(8):
                    for m in each:
                        slabs[m][r] = slabs[m][r] - spread[m][r][j] * jnp.broadcast_to(
                            pivot[m][j : j + 1], (8, 128)
                        )
        for m in each:
            slabs[m][k] = pivot[m]
    return [jnp.concatenate(rows, axis=0)[:, Q:] for rows in slabs]


def half_of(core, total):
    return jnp.where(core[0] == 0, total[: SUMS // 2], total[SUMS // 2 :])


def pair_sum(core, a, b, out):
    total = half_of(core, a[...] + b[...])
    for j in range(R):
        out[j] = total


def plane_sum(pieces, out):
    out[...] = summed(pieces)


def finish(core, mine, theirs, image, kept, x_out, r_out, d_out):
    first = core[0] == 0
    mine, theirs = mine[...], theirs[...]
    total = jnp.concatenate(
        [jnp.where(first, mine, theirs), jnp.where(first, theirs, mine)], axis=0
    )
    cross, both = total[:Q, :Q], total[:Q, Q:]
    below, at = lower((Q, Q)), diagonal((Q, Q))
    under = jnp.where(below, both, 0.0)
    over = both - under
    matrix = jnp.where(at, total[DIAG : DIAG + 1, :Q], under + under.T)
    square = over + jnp.where(below, over.T, 0.0)
    res = restored(total[GRAM:])
    direction = kept[DIR : DIR + Q]
    step, inverse = eliminate(
        jnp.concatenate([matrix, res], axis=1),
        jnp.concatenate([res, at.astype(jnp.float32)], axis=1),
    )
    x_out[...] = kept[ITER : ITER + Q] + dot(step, direction, 0, 0)
    new_res = kept[RES : RES + Q] - dot(step, image[...], 0, 0)
    r_out[...] = new_res
    new_gram = res - dot(cross, step, 0, 0) + dot(step, dot(square, step) - cross, 0, 0)
    d_out[...] = new_res + dot(dot(inverse, new_gram), direction, 0, 0)


def swapped(value):
    return lax.ppermute(value, "core", [(0, 1), (1, 0)])


def across(value, k):
    return lax.ppermute(value, "z", [(i, i ^ k) for i in range(4)])


def exchanged(value, axes):
    return lax.all_to_all(value, axes, 0, 0, tiled=True)


def on_device(points, lengthscales, noise_level, iterate, residual, direction):
    own, cols, kept = call(
        prep,
        [f32(ROWS, 128), f32(R, COLS, 128), f32(3 * Q, 128)],
        [
            [pltpu.VMEM((N, F), jnp.float32), pltpu.VMEM((1, F), jnp.float32)],
            pltpu.SemaphoreType.DMA((5,)),
        ],
        room=ROOM,
        ins=[HBM] * 5,
    )(
        points,
        lengthscales.reshape(1, F),
        iterate.T,
        residual.T,
        direction.T,
    )
    cols = exchanged(cols, PLANE)
    rows = [own] + [across(own, k) for k in range(1, Z)]
    left, halves, sides, res_gram = call(
        spread_rows,
        [
            jax.ShapeDtypeStruct((Z * N, 6 * F), jnp.bfloat16),
            f32(Z * N, CHUNK),
            f32(2 * Q, Z * N),
            f32(SUMS - GRAM, 128),
        ],
        flops=10**8,
    )(*rows)
    other = swapped(cols)
    scratch = [
        pltpu.VMEM((R * N, 6 * F), jnp.bfloat16),
        pltpu.VMEM((2 * Q, R * N), jnp.bfloat16),
        pltpu.VMEM((8, R * N), jnp.float32),
    ]
    part = call(products_first, f32(Z * N, 2 * Q), scratch, 4 * 10**9, 24)(left, halves, cols)
    sent = call(products_last, f32(Z * Q, 128), scratch, 4 * 10**9, 24)(
        left, halves, other, part
    )
    got = [sent] + [across(sent, k) for k in range(1, Z)]
    image, sums = call(grams, [f32(Q, N), f32(SUMS, 128)])(
        *got, sides, res_gram, noise_level.reshape(1, 1)
    )
    core = lax.axis_index("core").reshape(1)
    both = call(pair_sum, f32(R, SUMS // 2, 128), ins=[SMEM, VM, VM])(core, sums, swapped(sums))
    half = call(plane_sum, f32(SUMS // 2, 128))(exchanged(both, PLANE))
    outs = call(finish, [f32(Q, N)] * 3, ins=[SMEM] + [VM] * 4)(
        core, half, swapped(half), image, kept
    )
    return tuple(o.T for o in outs)


def solution(mesh):
    fine = Mesh(mesh.devices.reshape(4, 2, 4, 2, 2), AXES)
    split_rows = P(AXES, None)
    return jax.shard_map(
        on_device,
        mesh=fine,
        in_specs=(split_rows, P(), P(), split_rows, split_rows, split_rows),
        out_specs=(split_rows,) * 3,
        check_vma=False,
    )
```

time: 83.9 us -> 90.8 us (1.082)
  blocking collectives: 34.8 us -> 43.8 us
  starting transfers between devices: 17.6 us -> 10.6 us
  waiting for transfers between devices: 13.8 us -> 16.2 us
  Pallas kernels: 16 us -> 17.5 us
    all_to_all x2, blocking collectives: 34.8 us -> 43.8 us  [exchanged(): return lax.all_to_all(value, axes, 0, 0, tiled=True)]
    all_to_all x1 -> x0, starting transfers between devices: 7.29 us -> none  [exchanged(): return lax.all_to_all(value, axes, 0, 0, tiled=True)]
    ppermute x6, waiting for transfers between devices: 8.89 us -> 13.8 us  [across(): return lax.ppermute(value, 'z', [(i, i ^ k) for i in range(4)])]
    all_to_all x1 -> x0, waiting for transfers between devices: 2.67 us -> none  [exchanged(): return lax.all_to_all(value, axes, 0, 0, tiled=True)]
    pallas_call x8, Pallas kernels: 16 us -> 17.5 us  [the longest x1 5.1 us: on_device(): call(products_last, f32(Z * Q, 128), scratch, 4 * 10 ** 9, 24)]
    ppermute x5 -> x3, waiting for transfers between devices: 2.18 us -> 2.4 us  [swapped(): return lax.ppermute(value, 'core', [(0, 1), (1, 0)])]
  transfers between devices with their start and end apart: 12 -> 9, of which waited for: 7 -> 8; matrix products, arithmetic and copies ran while one was open for 0% -> 0% of each run, Pallas kernels for 2% -> 5%
where the time goes in v6:
time: 90.8 us; the launch traced here: 89.5 us
  blocking collectives  43.8 us (48%)
  Pallas kernels  17.5 us (19%)
  waiting for transfers between devices  16.2 us (18%)
  starting transfers between devices  10.6 us (12%)
  between operations  1.38 us (2%)
    all_to_all x2, blocking collectives, exchanged(): return lax.all_to_all(value, axes, 0, 0, tiled=True)  43.8 us
    ppermute x6, waiting for transfers between devices, across(): return lax.ppermute(value, 'z', [(i, i ^ k) for i in range(4)])  13.8 us
    ppermute x6, starting transfers between devices, across(): return lax.ppermute(value, 'z', [(i, i ^ k) for i in range(4)])  10.3 us
    pallas_call x1, Pallas kernels, on_device(): call(products_last, f32(Z * Q, 128), scratch, 4 * 10 ** 9, 24)  5.1 us
    pallas_call x1, Pallas kernels, on_device(): call(finish, [f32(Q, N)] * 3, ins=[SMEM] + [VM] * 4)  4.69 us
    pallas_call x1, Pallas kernels, on_device(): call(products_first, f32(Z * N, 2 * Q), scratch, 4 * 10 ** 9, 24)  3.79 us
    pallas_call x1, Pallas kernels, on_device(): call(prep, [f32(ROWS, 128), f32(R, COLS, 128), f32(3 * Q, 128)], [[pltpu....  2.43 us
    ppermute x3, waiting for transfers between devices, swapped(): return lax.ppermute(value, 'core', [(0, 1), (1, 0)])  2.4 us
  transfers between devices with their start and end apart: 9, of which 8 were waited for; matrix products, arithmetic and copies ran while one was open for 0% of the time, Pallas kernels for 5%

profile of v6, /device:TPU:0, one launch (start us, length us, event | category | flops | bytes accessed | tf_op | source)
XLA Modules:
  0.0 89.5 jit_solution(10452981840460050354)
XLA Ops:
  0.6 2.4 %shard_map.85 = (f32[256,128]{1,0:T(8,128)}, f32[16,200,128]{2,1,0:T(8,128)}, f32[192,128]{1,0:T(8,128)}) custom-call(f32[128,128]{1,0:T(8,128)} %points.1, f32[1,128]{1,0:T(1,128)} %bitcast.13, f32[64,128]{1,0:T(8,128)} %bitcast.10, f32[64,128]{1,0:T(8,128)} %bitcast.11, f32[64,128]{1,0:T(8,128)} %bitcast.12), custom_call_target="tpu_custom_call" | custom-call | flops 1000000 | bytes 1000000 | tf_op jit(solution)/shard_map/pallas_call | solution.py:293
  3.1 0.0 copy-start
  3.1 30.9 %all_to_all.10.cols = f32[16,200,128]{2,1,0:T(8,128)S(1)} all-to-all(f32[16,200,128]{2,1,0:T(8,128)} %get-tuple-element.18), channel_id=1, replica_groups=mesh['y'=4,'xl'=2,'z'=4,'xh'=2,'core'=2] {'y','xl','xh'}, dimensions={0} | all-to-all | bytes 3276800 | tf_op jit(solution)/shard_map/all_to_all | solution.py:289
  34.0 0.0 collective-permute-start.3
  34.0 0.0 copy-done
  34.0 1.9 %collective-permute-start = (f32[256,128]{1,0:T(8,128)S(1)}, f32[256,128]{1,0:T(8,128)S(1)}, u32[]{:S(2)}, u32[]{:S(2)}) collective-permute-start(f32[256,128]{1,0:T(8,128)S(1)} %copy-done), channel_id=1, source_target_pairs={{0,4},{4,0},{8,12},{12,8},{1,5},{5,1},{9,13},{13,9},{2,6},{6,2},{1... | collective-permute-start | bytes 393224 | tf_op jit(solution)/shard_map/ppermute | solution.py:285
  35.9 3.6 %collective-permute-start.1 = (f32[256,128]{1,0:T(8,128)S(1)}, f32[256,128]{1,0:T(8,128)S(1)}, u32[]{:S(2)}, u32[]{:S(2)}) collective-permute-start(f32[256,128]{1,0:T(8,128)S(1)} %copy-done), channel_id=1, source_target_pairs={{0,8},{4,12},{8,0},{12,4},{1,9},{5,13},{9,1},{13,5},{2,10},{6,14},... | collective-permute-start | bytes 393224 | tf_op jit(solution)/shard_map/ppermute | solution.py:285
  39.5 0.0 collective-permute-start.2
  39.5 0.6 collective-permute-done.b
  40.0 6.2 %collective-permute-done.1.c = f32[256,128]{1,0:T(8,128)S(1)} collective-permute-done((f32[256,128]{1,0:T(8,128)S(1)}, f32[256,128]{1,0:T(8,128)S(1)}, u32[]{:S(2)}, u32[]{:S(2)}) %collective-permute-start.1) | collective-permute-done | bytes 131104 | tf_op jit(solution)/shard_map/ppermute | solution.py:285
  46.3 2.4 %collective-permute-done.2.d = f32[256,128]{1,0:T(8,128)S(1)} collective-permute-done((f32[256,128]{1,0:T(8,128)S(1)}, f32[256,128]{1,0:T(8,128)S(1)}, u32[]{:S(2)}, u32[]{:S(2)}) %collective-permute-start.2) | collective-permute-done | bytes 131104 | tf_op jit(solution)/shard_map/ppermute | solution.py:285
  48.7 0.6 shard_map.86
  49.3 3.8 %shard_map.87.before = f32[512,128]{1,0:T(8,128)S(1)} custom-call(bf16[512,768]{1,0:T(8,128)(2,1)S(1)} %get-tuple-element.16.left, f32[512,256]{1,0:T(8,128)S(1)} %get-tuple-element.17.own, f32[16,200,128]{2,1,0:T(8,128)S(1)} %all_to_all.10.cols), custom_call_target="tpu_custom_call" | custom-call | flops 4000000000 | bytes 1000000 | tf_op jit(solution)/shard_map/pallas_call | solution.py:327
  53.1 0.0 collective-permute-done.3.cols
  53.1 5.1 %shard_map.88.a = f32[256,128]{1,0:T(8,128)S(1)} custom-call(bf16[512,768]{1,0:T(8,128)(2,1)S(1)} %get-tuple-element.16.left, f32[512,256]{1,0:T(8,128)S(1)} %get-tuple-element.17.own, f32[16,200,128]{2,1,0:T(8,128)S(1)} %collective-permute-done.3.cols, f32[512,128]{1,0:T(8,128)S(1)} %shard_map.87.before), custom_call_target="tpu_custom_call" | custom-call | flops 4000000000 | bytes 1000000 | tf_op jit(solution)/shard_map/pallas_call | solution.py:328
  58.2 0.0 copy-start.1
  58.2 0.1 collective-permute-start.4
  58.3 1.1 %collective-permute-start.5 = (f32[256,128]{1,0:T(8,128)S(1)}, f32[256,128]{1,0:T(8,128)S(1)}, u32[]{:S(2)}, u32[]{:S(2)}) collective-permute-start(f32[256,128]{1,0:T(8,128)S(1)} %shard_map.88.a), channel_id=1, source_target_pairs={{0,8},{4,12},{8,0},{12,4},{1,9},{5,13},{9,1},{13,5},{2,10},{6,14},... | collective-permute-start | bytes 393224 | tf_op jit(solution)/shard_map/ppermute | solution.py:285
  59.5 3.6 %collective-permute-start.6 = (f32[256,128]{1,0:T(8,128)S(1)}, f32[256,128]{1,0:T(8,128)S(1)}, u32[]{:S(2)}, u32[]{:S(2)}) collective-permute-start(f32[256,128]{1,0:T(8,128)S(1)} %shard_map.88.a), channel_id=1, source_target_pairs={{0,12},{4,8},{8,4},{12,0},{1,13},{5,9},{9,5},{13,1},{2,14},{6,10},... | collective-permute-start | bytes 393224 | tf_op jit(solution)/shard_map/ppermute | solution.py:285
  63.7 1.0 %collective-permute-done.4.b = f32[256,128]{1,0:T(8,128)S(1)} collective-permute-done((f32[256,128]{1,0:T(8,128)S(1)}, f32[256,128]{1,0:T(8,128)S(1)}, u32[]{:S(2)}, u32[]{:S(2)}) %collective-permute-start.4) | collective-permute-done | bytes 131104 | tf_op jit(solution)/shard_map/ppermute | solution.py:285
  64.7 1.1 %collective-permute-done.5.c = f32[256,128]{1,0:T(8,128)S(1)} collective-permute-done((f32[256,128]{1,0:T(8,128)S(1)}, f32[256,128]{1,0:T(8,128)S(1)}, u32[]{:S(2)}, u32[]{:S(2)}) %collective-permute-start.5) | collective-permute-done | bytes 131104 | tf_op jit(solution)/shard_map/ppermute | solution.py:285
  65.8 2.5 %collective-permute-done.6.d = f32[256,128]{1,0:T(8,128)S(1)} collective-permute-done((f32[256,128]{1,0:T(8,128)S(1)}, f32[256,128]{1,0:T(8,128)S(1)}, u32[]{:S(2)}, u32[]{:S(2)}) %collective-permute-start.6) | collective-permute-done | bytes 131104 | tf_op jit(solution)/shard_map/ppermute | solution.py:285
  68.3 0.8 shard_map.89
  69.1 0.1 collective-permute-start.7
  69.1 1.2 %collective-permute-done.7.b = f32[96,128]{1,0:T(8,128)S(1)} collective-permute-done((f32[96,128]{1,0:T(8,128)S(1)}, f32[96,128]{1,0:T(8,128)S(1)}, u32[]{:S(2)}, u32[]{:S(2)}) %collective-permute-start.7) | collective-permute-done | bytes 49184 | tf_op jit(solution)/shard_map/ppermute | solution.py:281
  70.4 13.0 %all_to_all.11.pieces = f32[16,48,128]{2,1,0:T(8,128)S(1)} all-to-all(f32[16,48,128]{2,1,0:T(8,128)S(1)} %shard_map.90), channel_id=1, replica_groups=mesh['y'=4,'xl'=2,'z'=4,'xh'=2,'core'=2] {'y','xl','xh'}, dimensions={0} | all-to-all | bytes 786432 | tf_op jit(solution)/shard_map/all_to_all | solution.py:289
  83.4 0.3 collective-permute-start.8
  83.7 1.2 %collective-permute-done.8.theirs = f32[48,128]{1,0:T(8,128)S(1)} collective-permute-done((f32[48,128]{1,0:T(8,128)S(1)}, f32[48,128]{1,0:T(8,128)S(1)}, u32[]{:S(2)}, u32[]{:S(2)}) %collective-permute-start.8) | collective-permute-done | bytes 24608 | tf_op jit(solution)/shard_map/ppermute | solution.py:281
  84.8 0.0 copy-done.1
  84.8 4.7 %shard_map.92 = (f32[64,128]{1,0:T(8,128)}, f32[64,128]{1,0:T(8,128)}, f32[64,128]{1,0:T(8,128)}) custom-call(s32[1]{0:T(128)} %bitcast.core, f32[48,128]{1,0:T(8,128)S(1)} %shard_map.91.mine, f32[48,128]{1,0:T(8,128)S(1)} %collective-permute-done.8.theirs, f32[64,128]{1,0:T(8,128)S(1)} %get-tuple-element.22.image, f32[192,128]{1,0:T(8,128)S(1)} %copy-done.1), custom_call_target="tpu_custom_call" | custom-call | flops 1000000 | bytes 1000000 | tf_op jit(solution)/shard_map/pallas_call | solution.py:338
  (2 shorter events, 0.1 us)
Async XLA Ops:
  3.1 30.9 %copy-start = (f32[256,128]{1,0:T(8,128)S(1)}, f32[256,128]{1,0:T(8,128)}, u32[]{:S(2)}) copy-start(f32[256,128]{1,0:T(8,128)} %get-tuple-element.15.a) | copy-start | bytes 393220
  34.0 19.2 %collective-permute-start.3 = (f32[16,200,128]{2,1,0:T(8,128)S(1)}, f32[16,200,128]{2,1,0:T(8,128)S(1)}, u32[]{:S(2)}, u32[]{:S(2)}) collective-permute-start(f32[16,200,128]{2,1,0:T(8,128)S(1)} %all_to_all.10.cols), channel_id=1, source_target_pairs={{0,1},{1,0},{2,3},{3,2},{4,5},{5,4},{6,7},{7,6},{8,9},{9,8},{10,11... | collective-permute-start | bytes 4915208 | tf_op jit(solution)/shard_map/ppermute | solution.py:281
  34.0 6.1 %collective-permute-start = (f32[256,128]{1,0:T(8,128)S(1)}, f32[256,128]{1,0:T(8,128)S(1)}, u32[]{:S(2)}, u32[]{:S(2)}) collective-permute-start(f32[256,128]{1,0:T(8,128)S(1)} %copy-done), channel_id=1, source_target_pairs={{0,4},{4,0},{8,12},{12,8},{1,5},{5,1},{9,13},{13,9},{2,6},{6,2},{1... | collective-permute-start | bytes 393224 | tf_op jit(solution)/shard_map/ppermute | solution.py:285
  35.9 10.4 %collective-permute-start.1 = (f32[256,128]{1,0:T(8,128)S(1)}, f32[256,128]{1,0:T(8,128)S(1)}, u32[]{:S(2)}, u32[]{:S(2)}) collective-permute-start(f32[256,128]{1,0:T(8,128)S(1)} %copy-done), channel_id=1, source_target_pairs={{0,8},{4,12},{8,0},{12,4},{1,9},{5,13},{9,1},{13,5},{2,10},{6,14},... | collective-permute-start | bytes 393224 | tf_op jit(solution)/shard_map/ppermute | solution.py:285
  39.5 9.2 %collective-permute-start.2 = (f32[256,128]{1,0:T(8,128)S(1)}, f32[256,128]{1,0:T(8,128)S(1)}, u32[]{:S(2)}, u32[]{:S(2)}) collective-permute-start(f32[256,128]{1,0:T(8,128)S(1)} %copy-done), channel_id=1, source_target_pairs={{0,12},{4,8},{8,4},{12,0},{1,13},{5,9},{9,5},{13,1},{2,14},{6,10},... | collective-permute-start | bytes 393224 | tf_op jit(solution)/shard_map/ppermute | solution.py:285
  58.2 26.6 %copy-start.1 = (f32[192,128]{1,0:T(8,128)S(1)}, f32[192,128]{1,0:T(8,128)}, u32[]{:S(2)}) copy-start(f32[192,128]{1,0:T(8,128)} %get-tuple-element.23.kept) | copy-start | bytes 294916
  58.2 6.4 %collective-permute-start.4 = (f32[256,128]{1,0:T(8,128)S(1)}, f32[256,128]{1,0:T(8,128)S(1)}, u32[]{:S(2)}, u32[]{:S(2)}) collective-permute-start(f32[256,128]{1,0:T(8,128)S(1)} %shard_map.88.a), channel_id=1, source_target_pairs={{0,4},{4,0},{8,12},{12,8},{1,5},{5,1},{9,13},{13,9},{2,6},{6,2},{1... | collective-permute-start | bytes 393224 | tf_op jit(solution)/shard_map/ppermute | solution.py:285
  58.3 7.5 %collective-permute-start.5 = (f32[256,128]{1,0:T(8,128)S(1)}, f32[256,128]{1,0:T(8,128)S(1)}, u32[]{:S(2)}, u32[]{:S(2)}) collective-permute-start(f32[256,128]{1,0:T(8,128)S(1)} %shard_map.88.a), channel_id=1, source_target_pairs={{0,8},{4,12},{8,0},{12,4},{1,9},{5,13},{9,1},{13,5},{2,10},{6,14},... | collective-permute-start | bytes 393224 | tf_op jit(solution)/shard_map/ppermute | solution.py:285
  59.5 8.8 %collective-permute-start.6 = (f32[256,128]{1,0:T(8,128)S(1)}, f32[256,128]{1,0:T(8,128)S(1)}, u32[]{:S(2)}, u32[]{:S(2)}) collective-permute-start(f32[256,128]{1,0:T(8,128)S(1)} %shard_map.88.a), channel_id=1, source_target_pairs={{0,12},{4,8},{8,4},{12,0},{1,13},{5,9},{9,5},{13,1},{2,14},{6,10},... | collective-permute-start | bytes 393224 | tf_op jit(solution)/shard_map/ppermute | solution.py:285
  69.1 1.3 %collective-permute-start.7 = (f32[96,128]{1,0:T(8,128)S(1)}, f32[96,128]{1,0:T(8,128)S(1)}, u32[]{:S(2)}, u32[]{:S(2)}) collective-permute-start(f32[96,128]{1,0:T(8,128)S(1)} %get-tuple-element.21.a), channel_id=1, source_target_pairs={{0,1},{1,0},{2,3},{3,2},{4,5},{5,4},{6,7},{7,6},{8,9},{9,8},{10,11... | collective-permute-start | bytes 147464 | tf_op jit(solution)/shard_map/ppermute | solution.py:281
  83.4 1.5 %collective-permute-start.8 = (f32[48,128]{1,0:T(8,128)S(1)}, f32[48,128]{1,0:T(8,128)S(1)}, u32[]{:S(2)}, u32[]{:S(2)}) collective-permute-start(f32[48,128]{1,0:T(8,128)S(1)} %shard_map.91.mine), channel_id=1, source_target_pairs={{0,1},{1,0},{2,3},{3,2},{4,5},{5,4},{6,7},{7,6},{8,9},{9,8},{10,11... | collective-permute-start | bytes 73736 | tf_op jit(solution)/shard_map/ppermute | solution.py:281

commit v7 on v6

--- a/solution.py
+++ b/solution.py
@@ -132,35 +132,49 @@
     gram[...] = halved(residual)
 
 
-def partial(left, own, cols, right, dirs, halves):
-    for j in range(R):
-        at = slice(j * N, (j + 1) * N)
-        top, mid, low = split(cols[j, :N])
-        right[at] = jnp.concatenate([top, mid, top, low, top, mid], axis=1)
-        high, rest, _ = split(cols[j, N:DIRS])
-        dirs[:, at] = jnp.concatenate([high, rest], axis=0)
-        halves[:, at] = cols[j, DIRS:]
-    total = jnp.zeros((Z * N, 2 * Q), jnp.float32)
-    for j in range(R * N // CHUNK):
-        at = slice(j * CHUNK, (j + 1) * CHUNK)
-        inner = dot(left[...], right[at], 1, 1, None)
-        kernel = jnp.exp2(inner - own[...] - halves[0:1, at])
+def partial(left, own, cols, total):
+    per = CHUNK // N
+    for j in range(R // per):
+        blocks = [cols[j * per + i] for i in range(per)]
+        tops = [split(b[:N]) for b in blocks]
+        right = jnp.concatenate(
+            [jnp.concatenate([t, m, t, w, t, m], axis=1) for t, m, w in tops], axis=0
+        )
+        pairs = [split(b[N:DIRS]) for b in blocks]
+        dirs = jnp.concatenate([jnp.concatenate(p[:2], axis=0) for p in pairs], axis=1)
+        half = jnp.concatenate([b[DIRS : DIRS + 1] for b in blocks], axis=1)
+        inner = dot(left[...], right, 1, 1, None)
+        kernel = jnp.exp2(inner - own[...] - half)
         high = kernel.astype(jnp.bfloat16)
         rest = (kernel - high.astype(jnp.float32)).astype(jnp.bfloat16)
-        weights = jnp.concatenate([dirs[:, at], dirs[:, at]], axis=1)
+        weights = jnp.concatenate([dirs, dirs], axis=1)
         total += dot(jnp.concatenate([high, rest], axis=1), weights, 1, 1, None)
     return total
 
 
-def products_first(left, own, cols, out, right, dirs, halves):
-    out[...] = partial(left, own, cols, right, dirs, halves)
-
-
-def products_last(left, own, cols, before, out, right, dirs, halves):
-    total = before[...] + partial(left, own, cols, right, dirs, halves)
+def products_first(left, own, cols, out):
+    out[...] = partial(left, own, cols, jnp.zeros((Z * N, 2 * Q), jnp.float32))
+
+
+def products_last(left, own, cols, before, up, down):
+    total = partial(left, own, cols, before[...])
     total += pltpu.roll(total, Q, 1)
     for k in range(Z):
-        out[k * Q : (k + 1) * Q] = fold(total[k * N : (k + 1) * N])
+        block = fold(total[k * N : (k + 1) * N])
+        up[k * H : (k + 1) * H] = block[:H]
+        down[k * H : (k + 1) * H] = block[H:]
+
+
+def met(mine, theirs, place):
+    return [
+        mine[k * H : (k + 1) * H] + theirs[(k ^ place) * H : ((k ^ place) + 1) * H]
+        for k in range(Z)
+    ]
+
+
+def half_way(up, up_theirs, down, down_theirs, up_out, down_out):
+    up_out[...] = jnp.concatenate(met(up, up_theirs, 1), axis=0)
+    down_out[...] = jnp.concatenate(met(down, down_theirs, 3), axis=0)
 
 
 def summed(pieces):
@@ -178,14 +192,10 @@
     return lax.broadcasted_iota(jnp.int32, shape, 0) == lax.broadcasted_iota(jnp.int32, shape, 1)
 
 
-def grams(a, b, c, d, sides, res_gram, noise, image_out, sums):
-    pieces = (a, b, c, d)
+def grams(up, up_theirs, down, down_theirs, sides, res_gram, noise, image_out, sums):
     parts = []
-    for k in range(Z):
-        total = a[k * Q : (k + 1) * Q]
-        for place in range(1, Z):
-            total += pieces[place][(k ^ place) * Q : ((k ^ place) + 1) * Q]
-        turned = total.T
+    for block in zip(met(up, up_theirs, 3), met(down, down_theirs, 1)):
+        turned = jnp.concatenate(block, axis=0).T
         parts += [turned[:Q], turned[Q:]]
     direction = sides[:Q]
     image = jnp.concatenate(parts, axis=1) + noise[0, 0] * direction
@@ -319,16 +329,12 @@
         flops=10**8,
     )(*rows)
     other = swapped(cols)
-    scratch = [
-        pltpu.VMEM((R * N, 6 * F), jnp.bfloat16),
-        pltpu.VMEM((2 * Q, R * N), jnp.bfloat16),
-        pltpu.VMEM((8, R * N), jnp.float32),
-    ]
-    part = call(products_first, f32(Z * N, 2 * Q), scratch, 4 * 10**9, 24)(left, halves, cols)
-    sent = call(products_last, f32(Z * Q, 128), scratch, 4 * 10**9, 24)(
+    part = call(products_first, f32(Z * N, 2 * Q), (), 4 * 10**9, 24)(left, halves, cols)
+    up, down = call(products_last, [f32(Z * H, 128)] * 2, (), 4 * 10**9, 24)(
         left, halves, other, part
     )
-    got = [sent] + [across(sent, k) for k in range(1, Z)]
+    up, down = call(half_way, [f32(Z * H, 128)] * 2)(up, across(up, 1), down, across(down, 3))
+    got = [up, across(up, 3), down, across(down, 1)]
     image, sums = call(grams, [f32(Q, N), f32(SUMS, 128)])(
         *got, sides, res_gram, noise_level.reshape(1, 1)
     )

time: 90.8 us -> 90.4 us (level)
  waiting for transfers between devices: 16.2 us -> 21.1 us
  starting transfers between devices: 10.6 us -> 6.91 us
  Pallas kernels: 17.5 us -> 15.9 us
    ppermute x6 -> x7, waiting for transfers between devices: 13.8 us -> 18.7 us  [across(): return lax.ppermute(value, 'z', [(i, i ^ k) for i in range(4)])]
    ppermute x6 -> x7, starting transfers between devices: 10.3 us -> 6.56 us  [across(): return lax.ppermute(value, 'z', [(i, i ^ k) for i in range(4)])]
    pallas_call x2 -> x3, Pallas kernels: 8.89 us -> 7.29 us  [the longest x1 3.72 us: on_device(): call(products_first, f32(Z * N, 2 * Q), (), 4 * 10 ** 9, 24)]
  transfers between devices with their start and end apart: 9 -> 10, of which waited for: 8 -> 8; matrix products, arithmetic and copies ran while one was open for 0% -> 0% of each run, Pallas kernels for 5% -> 5%
where the time goes in v7:
time: 90.4 us; the launch traced here: 89.1 us
  blocking collectives  43.8 us (48%)
  waiting for transfers between devices  21.1 us (23%)
  Pallas kernels  15.9 us (18%)
  starting transfers between devices  6.91 us (8%)
  between operations  1.4 us (2%)
    all_to_all x2, blocking collectives, exchanged(): return lax.all_to_all(value, axes, 0, 0, tiled=True)  43.8 us
    ppermute x7, waiting for transfers between devices, across(): return lax.ppermute(value, 'z', [(i, i ^ k) for i in range(4)])  18.7 us
    ppermute x7, starting transfers between devices, across(): return lax.ppermute(value, 'z', [(i, i ^ k) for i in range(4)])  6.56 us
    pallas_call x1, Pallas kernels, on_device(): call(finish, [f32(Q, N)] * 3, ins=[SMEM] + [VM] * 4)  4.69 us
    pallas_call x1, Pallas kernels, on_device(): call(products_first, f32(Z * N, 2 * Q), (), 4 * 10 ** 9, 24)  3.72 us
    pallas_call x1, Pallas kernels, on_device(): call(products_last, [f32(Z * H, 128)] * 2, (), 4 * 10 ** 9, 24)  3.55 us
    pallas_call x1, Pallas kernels, on_device(): call(prep, [f32(ROWS, 128), f32(R, COLS, 128), f32(3 * Q, 128)], [[pltpu....  2.42 us
    ppermute x3, waiting for transfers between devices, swapped(): return lax.ppermute(value, 'core', [(0, 1), (1, 0)])  2.4 us
  transfers between devices with their start and end apart: 10, of which 8 were waited for; matrix products, arithmetic and copies ran while one was open for 0% of the time, Pallas kernels for 5%

profile of v7, /device:TPU:0, one launch (start us, length us, event | category | flops | bytes accessed | tf_op | source)
XLA Modules:
  0.0 89.1 jit_solution(11875244810941429978)
XLA Ops:
  0.6 2.4 %shard_map.85 = (f32[256,128]{1,0:T(8,128)}, f32[16,200,128]{2,1,0:T(8,128)}, f32[192,128]{1,0:T(8,128)}) custom-call(f32[128,128]{1,0:T(8,128)} %points.1, f32[1,128]{1,0:T(1,128)} %bitcast.13, f32[64,128]{1,0:T(8,128)} %bitcast.10, f32[64,128]{1,0:T(8,128)} %bitcast.11, f32[64,128]{1,0:T(8,128)} %bitcast.12), custom_call_target="tpu_custom_call" | custom-call | flops 1000000 | bytes 1000000 | tf_op jit(solution)/shard_map/pallas_call | solution.py:303
  3.1 0.0 copy-start
  3.1 30.9 %all_to_all.10.cols = f32[16,200,128]{2,1,0:T(8,128)S(1)} all-to-all(f32[16,200,128]{2,1,0:T(8,128)} %get-tuple-element.22), channel_id=1, replica_groups=mesh['y'=4,'xl'=2,'z'=4,'xh'=2,'core'=2] {'y','xl','xh'}, dimensions={0} | all-to-all | bytes 3276800 | tf_op jit(solution)/shard_map/all_to_all | solution.py:299
  33.9 0.0 collective-permute-start.3
  33.9 0.0 copy-done
  34.0 1.9 %collective-permute-start = (f32[256,128]{1,0:T(8,128)S(1)}, f32[256,128]{1,0:T(8,128)S(1)}, u32[]{:S(2)}, u32[]{:S(2)}) collective-permute-start(f32[256,128]{1,0:T(8,128)S(1)} %copy-done), channel_id=1, source_target_pairs={{0,4},{4,0},{8,12},{12,8},{1,5},{5,1},{9,13},{13,9},{2,6},{6,2},{1... | collective-permute-start | bytes 393224 | tf_op jit(solution)/shard_map/ppermute | solution.py:295
  35.9 3.6 %collective-permute-start.1 = (f32[256,128]{1,0:T(8,128)S(1)}, f32[256,128]{1,0:T(8,128)S(1)}, u32[]{:S(2)}, u32[]{:S(2)}) collective-permute-start(f32[256,128]{1,0:T(8,128)S(1)} %copy-done), channel_id=1, source_target_pairs={{0,8},{4,12},{8,0},{12,4},{1,9},{5,13},{9,1},{13,5},{2,10},{6,14},... | collective-permute-start | bytes 393224 | tf_op jit(solution)/shard_map/ppermute | solution.py:295
  39.5 0.0 collective-permute-start.2
  39.5 0.6 collective-permute-done.b
  40.0 6.2 %collective-permute-done.1.c = f32[256,128]{1,0:T(8,128)S(1)} collective-permute-done((f32[256,128]{1,0:T(8,128)S(1)}, f32[256,128]{1,0:T(8,128)S(1)}, u32[]{:S(2)}, u32[]{:S(2)}) %collective-permute-start.1) | collective-permute-done | bytes 131104 | tf_op jit(solution)/shard_map/ppermute | solution.py:295
  46.2 2.4 %collective-permute-done.2.d = f32[256,128]{1,0:T(8,128)S(1)} collective-permute-done((f32[256,128]{1,0:T(8,128)S(1)}, f32[256,128]{1,0:T(8,128)S(1)}, u32[]{:S(2)}, u32[]{:S(2)}) %collective-permute-start.2) | collective-permute-done | bytes 131104 | tf_op jit(solution)/shard_map/ppermute | solution.py:295
  48.7 0.6 shard_map.86
  49.3 3.7 %shard_map.87.before = f32[512,128]{1,0:T(8,128)S(1)} custom-call(bf16[512,768]{1,0:T(8,128)(2,1)S(1)} %get-tuple-element.20.left, f32[512,256]{1,0:T(8,128)S(1)} %get-tuple-element.21.own, f32[16,200,128]{2,1,0:T(8,128)S(1)} %all_to_all.10.cols), custom_call_target="tpu_custom_call" | custom-call | flops 4000000000 | bytes 1000000 | tf_op jit(solution)/shard_map/pallas_call | solution.py:332
  53.0 0.0 collective-permute-done.3.cols
  53.0 3.6 %shard_map.88 = (f32[128,128]{1,0:T(8,128)S(1)}, f32[128,128]{1,0:T(8,128)S(1)}) custom-call(bf16[512,768]{1,0:T(8,128)(2,1)S(1)} %get-tuple-element.20.left, f32[512,256]{1,0:T(8,128)S(1)} %get-tuple-element.21.own, f32[16,200,128]{2,1,0:T(8,128)S(1)} %collective-permute-done.3.cols, f32[512,128]{1,0:T(8,128)S(1)} %shard_map.87.before), custom_call_target="tpu_custom_call" | custom-call | flops 4000000000 | bytes 1000000 | tf_op jit(solution)/shard_map/pallas_call | solution.py:333
  56.6 0.0 copy-start.1
  56.6 0.1 collective-permute-start.4
  56.7 0.1 collective-permute-start.5
  56.8 4.2 %collective-permute-done.4.up_theirs = f32[128,128]{1,0:T(8,128)S(1)} collective-permute-done((f32[128,128]{1,0:T(8,128)S(1)}, f32[128,128]{1,0:T(8,128)S(1)}, u32[]{:S(2)}, u32[]{:S(2)}) %collective-permute-start.4) | collective-permute-done | bytes 65568 | tf_op jit(solution)/shard_map/ppermute | solution.py:295
  61.0 1.3 %collective-permute-done.5.down_theirs = f32[128,128]{1,0:T(8,128)S(1)} collective-permute-done((f32[128,128]{1,0:T(8,128)S(1)}, f32[128,128]{1,0:T(8,128)S(1)}, u32[]{:S(2)}, u32[]{:S(2)}) %collective-permute-start.5) | collective-permute-done | bytes 65568 | tf_op jit(solution)/shard_map/ppermute | solution.py:295
  62.3 0.1 collective-permute-start.6
  62.4 0.8 collective-permute-start.7
  63.8 4.0 %collective-permute-done.6.up_theirs = f32[128,128]{1,0:T(8,128)S(1)} collective-permute-done((f32[128,128]{1,0:T(8,128)S(1)}, f32[128,128]{1,0:T(8,128)S(1)}, u32[]{:S(2)}, u32[]{:S(2)}) %collective-permute-start.6) | collective-permute-done | bytes 65568 | tf_op jit(solution)/shard_map/ppermute | solution.py:295
  67.8 0.0 collective-permute-done.7.down_theirs
  67.8 0.8 shard_map.90
  68.6 0.1 collective-permute-start.8
  68.7 1.2 %collective-permute-done.8.b = f32[96,128]{1,0:T(8,128)S(1)} collective-permute-done((f32[96,128]{1,0:T(8,128)S(1)}, f32[96,128]{1,0:T(8,128)S(1)}, u32[]{:S(2)}, u32[]{:S(2)}) %collective-permute-start.8) | collective-permute-done | bytes 49184 | tf_op jit(solution)/shard_map/ppermute | solution.py:291
  70.0 13.0 %all_to_all.11.pieces = f32[16,48,128]{2,1,0:T(8,128)S(1)} all-to-all(f32[16,48,128]{2,1,0:T(8,128)S(1)} %shard_map.91), channel_id=1, replica_groups=mesh['y'=4,'xl'=2,'z'=4,'xh'=2,'core'=2] {'y','xl','xh'}, dimensions={0} | all-to-all | bytes 786432 | tf_op jit(solution)/shard_map/all_to_all | solution.py:299
  83.0 0.3 collective-permute-start.9
  83.3 1.2 %collective-permute-done.9.theirs = f32[48,128]{1,0:T(8,128)S(1)} collective-permute-done((f32[48,128]{1,0:T(8,128)S(1)}, f32[48,128]{1,0:T(8,128)S(1)}, u32[]{:S(2)}, u32[]{:S(2)}) %collective-permute-start.9) | collective-permute-done | bytes 24608 | tf_op jit(solution)/shard_map/ppermute | solution.py:291
  84.4 0.0 copy-done.1
  84.4 4.7 %shard_map.93 = (f32[64,128]{1,0:T(8,128)}, f32[64,128]{1,0:T(8,128)}, f32[64,128]{1,0:T(8,128)}) custom-call(s32[1]{0:T(128)} %bitcast.core, f32[48,128]{1,0:T(8,128)S(1)} %shard_map.92.mine, f32[48,128]{1,0:T(8,128)S(1)} %collective-permute-done.9.theirs, f32[64,128]{1,0:T(8,128)S(1)} %get-tuple-element.30.image, f32[192,128]{1,0:T(8,128)S(1)} %copy-done.1), custom_call_target="tpu_custom_call" | custom-call | flops 1000000 | bytes 1000000 | tf_op jit(solution)/shard_map/pallas_call | solution.py:344
  (3 shorter events, 0.1 us)
Async XLA Ops:
  3.1 30.9 %copy-start = (f32[256,128]{1,0:T(8,128)S(1)}, f32[256,128]{1,0:T(8,128)}, u32[]{:S(2)}) copy-start(f32[256,128]{1,0:T(8,128)} %get-tuple-element.19.a) | copy-start | bytes 393220
  33.9 19.1 %collective-permute-start.3 = (f32[16,200,128]{2,1,0:T(8,128)S(1)}, f32[16,200,128]{2,1,0:T(8,128)S(1)}, u32[]{:S(2)}, u32[]{:S(2)}) collective-permute-start(f32[16,200,128]{2,1,0:T(8,128)S(1)} %all_to_all.10.cols), channel_id=1, source_target_pairs={{0,1},{1,0},{2,3},{3,2},{4,5},{5,4},{6,7},{7,6},{8,9},{9,8},{10,11... | collective-permute-start | bytes 4915208 | tf_op jit(solution)/shard_map/ppermute | solution.py:291
  34.0 6.1 %collective-permute-start = (f32[256,128]{1,0:T(8,128)S(1)}, f32[256,128]{1,0:T(8,128)S(1)}, u32[]{:S(2)}, u32[]{:S(2)}) collective-permute-start(f32[256,128]{1,0:T(8,128)S(1)} %copy-done), channel_id=1, source_target_pairs={{0,4},{4,0},{8,12},{12,8},{1,5},{5,1},{9,13},{13,9},{2,6},{6,2},{1... | collective-permute-start | bytes 393224 | tf_op jit(solution)/shard_map/ppermute | solution.py:295
  35.9 10.4 %collective-permute-start.1 = (f32[256,128]{1,0:T(8,128)S(1)}, f32[256,128]{1,0:T(8,128)S(1)}, u32[]{:S(2)}, u32[]{:S(2)}) collective-permute-start(f32[256,128]{1,0:T(8,128)S(1)} %copy-done), channel_id=1, source_target_pairs={{0,8},{4,12},{8,0},{12,4},{1,9},{5,13},{9,1},{13,5},{2,10},{6,14},... | collective-permute-start | bytes 393224 | tf_op jit(solution)/shard_map/ppermute | solution.py:295
  39.5 9.2 %collective-permute-start.2 = (f32[256,128]{1,0:T(8,128)S(1)}, f32[256,128]{1,0:T(8,128)S(1)}, u32[]{:S(2)}, u32[]{:S(2)}) collective-permute-start(f32[256,128]{1,0:T(8,128)S(1)} %copy-done), channel_id=1, source_target_pairs={{0,12},{4,8},{8,4},{12,0},{1,13},{5,9},{9,5},{13,1},{2,14},{6,10},... | collective-permute-start | bytes 393224 | tf_op jit(solution)/shard_map/ppermute | solution.py:295
  56.6 27.8 %copy-start.1 = (f32[192,128]{1,0:T(8,128)S(1)}, f32[192,128]{1,0:T(8,128)}, u32[]{:S(2)}) copy-start(f32[192,128]{1,0:T(8,128)} %get-tuple-element.31.kept) | copy-start | bytes 294916
  56.6 4.3 %collective-permute-start.4 = (f32[128,128]{1,0:T(8,128)S(1)}, f32[128,128]{1,0:T(8,128)S(1)}, u32[]{:S(2)}, u32[]{:S(2)}) collective-permute-start(f32[128,128]{1,0:T(8,128)S(1)} %get-tuple-element.23.up), channel_id=1, source_target_pairs={{0,4},{4,0},{8,12},{12,8},{1,5},{5,1},{9,13},{13,9},{2,6},{6,2},{1... | collective-permute-start | bytes 196616 | tf_op jit(solution)/shard_map/ppermute | solution.py:295
  56.7 5.6 %collective-permute-start.5 = (f32[128,128]{1,0:T(8,128)S(1)}, f32[128,128]{1,0:T(8,128)S(1)}, u32[]{:S(2)}, u32[]{:S(2)}) collective-permute-start(f32[128,128]{1,0:T(8,128)S(1)} %get-tuple-element.24.down), channel_id=1, source_target_pairs={{0,12},{4,8},{8,4},{12,0},{1,13},{5,9},{9,5},{13,1},{2,14},{6,10},... | collective-permute-start | bytes 196616 | tf_op jit(solution)/shard_map/ppermute | solution.py:295
  62.3 5.6 %collective-permute-start.6 = (f32[128,128]{1,0:T(8,128)S(1)}, f32[128,128]{1,0:T(8,128)S(1)}, u32[]{:S(2)}, u32[]{:S(2)}) collective-permute-start(f32[128,128]{1,0:T(8,128)S(1)} %get-tuple-element.25.up), channel_id=1, source_target_pairs={{0,12},{4,8},{8,4},{12,0},{1,13},{5,9},{9,5},{13,1},{2,14},{6,10},... | collective-permute-start | bytes 196616 | tf_op jit(solution)/shard_map/ppermute | solution.py:295
  62.4 5.5 %collective-permute-start.7 = (f32[128,128]{1,0:T(8,128)S(1)}, f32[128,128]{1,0:T(8,128)S(1)}, u32[]{:S(2)}, u32[]{:S(2)}) collective-permute-start(f32[128,128]{1,0:T(8,128)S(1)} %get-tuple-element.26.down), channel_id=1, source_target_pairs={{0,4},{4,0},{8,12},{12,8},{1,5},{5,1},{9,13},{13,9},{2,6},{6,2},{1... | collective-permute-start | bytes 196616 | tf_op jit(solution)/shard_map/ppermute | solution.py:295
  68.6 1.3 %collective-permute-start.8 = (f32[96,128]{1,0:T(8,128)S(1)}, f32[96,128]{1,0:T(8,128)S(1)}, u32[]{:S(2)}, u32[]{:S(2)}) collective-permute-start(f32[96,128]{1,0:T(8,128)S(1)} %get-tuple-element.29.a), channel_id=1, source_target_pairs={{0,1},{1,0},{2,3},{3,2},{4,5},{5,4},{6,7},{7,6},{8,9},{9,8},{10,11... | collective-permute-start | bytes 147464 | tf_op jit(solution)/shard_map/ppermute | solution.py:291
  83.0 1.5 %collective-permute-start.9 = (f32[48,128]{1,0:T(8,128)S(1)}, f32[48,128]{1,0:T(8,128)S(1)}, u32[]{:S(2)}, u32[]{:S(2)}) collective-permute-start(f32[48,128]{1,0:T(8,128)S(1)} %shard_map.92.mine), channel_id=1, source_target_pairs={{0,1},{1,0},{2,3},{3,2},{4,5},{5,4},{6,7},{7,6},{8,9},{9,8},{10,11... | collective-permute-start | bytes 73736 | tf_op jit(solution)/shard_map/ppermute | solution.py:291

commit v8 on v7

--- a/solution.py
+++ b/solution.py
@@ -156,25 +156,22 @@
     out[...] = partial(left, own, cols, jnp.zeros((Z * N, 2 * Q), jnp.float32))
 
 
-def products_last(left, own, cols, before, up, down):
+def products_last(left, own, cols, before, out):
     total = partial(left, own, cols, before[...])
     total += pltpu.roll(total, Q, 1)
     for k in range(Z):
-        block = fold(total[k * N : (k + 1) * N])
-        up[k * H : (k + 1) * H] = block[:H]
-        down[k * H : (k + 1) * H] = block[H:]
+        out[k * Q : (k + 1) * Q] = fold(total[k * N : (k + 1) * N])
 
 
 def met(mine, theirs, place):
     return [
-        mine[k * H : (k + 1) * H] + theirs[(k ^ place) * H : ((k ^ place) + 1) * H]
+        mine[k * Q : (k + 1) * Q] + theirs[(k ^ place) * Q : ((k ^ place) + 1) * Q]
         for k in range(Z)
     ]
 
 
-def half_way(up, up_theirs, down, down_theirs, up_out, down_out):
-    up_out[...] = jnp.concatenate(met(up, up_theirs, 1), axis=0)
-    down_out[...] = jnp.concatenate(met(down, down_theirs, 3), axis=0)
+def half_way(mine, theirs, out):
+    out[...] = jnp.concatenate(met(mine, theirs, 1), axis=0)
 
 
 def summed(pieces):
@@ -192,10 +189,10 @@
     return lax.broadcasted_iota(jnp.int32, shape, 0) == lax.broadcasted_iota(jnp.int32, shape, 1)
 
 
-def grams(up, up_theirs, down, down_theirs, sides, res_gram, noise, image_out, sums):
+def grams(mine, theirs, sides, res_gram, noise, image_out, sums):
     parts = []
-    for block in zip(met(up, up_theirs, 3), met(down, down_theirs, 1)):
-        turned = jnp.concatenate(block, axis=0).T
+    for block in met(mine, theirs, 2):
+        turned = block.T
         parts += [turned[:Q], turned[Q:]]
     direction = sides[:Q]
     image = jnp.concatenate(parts, axis=1) + noise[0, 0] * direction
@@ -284,7 +281,7 @@
     new_res = kept[RES : RES + Q] - dot(step, image[...], 0, 0)
     r_out[...] = new_res
     new_gram = res - dot(cross, step, 0, 0) + dot(step, dot(square, step) - cross, 0, 0)
-    d_out[...] = new_res + dot(dot(inverse, new_gram), direction, 0, 0)
+    d_out[...] = new_res + dot(new_gram, dot(inverse, direction, 1, 0), 0, 0)
 
 
 def swapped(value):
@@ -330,11 +327,11 @@
     )(*rows)
     other = swapped(cols)
     part = call(products_first, f32(Z * N, 2 * Q), (), 4 * 10**9, 24)(left, halves, cols)
-    up, down = call(products_last, [f32(Z * H, 128)] * 2, (), 4 * 10**9, 24)(
+    sent = call(products_last, f32(Z * Q, 128), (), 4 * 10**9, 24)(
         left, halves, other, part
     )
-    up, down = call(half_way, [f32(Z * H, 128)] * 2)(up, across(up, 1), down, across(down, 3))
-    got = [up, across(up, 3), down, across(down, 1)]
+    sent = call(half_way, f32(Z * Q, 128))(sent, across(sent, 1))
+    got = [sent, across(sent, 2)]
     image, sums = call(grams, [f32(Q, N), f32(SUMS, 128)])(
         *got, sides, res_gram, noise_level.reshape(1, 1)
     )

time: 90.4 us -> 90.8 us (level)
  waiting for transfers between devices: 21.1 us -> 22.5 us
    ppermute x7 -> x5, waiting for transfers between devices: 18.7 us -> 20.1 us  [across(): return lax.ppermute(value, 'z', [(i, i ^ k) for i in range(4)])]
    ppermute x7 -> x5, starting transfers between devices: 6.56 us -> 5.68 us  [across(): return lax.ppermute(value, 'z', [(i, i ^ k) for i in range(4)])]
  transfers between devices with their start and end apart: 10 -> 8, of which waited for: 8 -> 7; matrix products, arithmetic and copies ran while one was open for 0% -> 0% of each run, Pallas kernels for 5% -> 5%
where the time goes in v8:
time: 90.8 us; the launch traced here: 89.5 us
  blocking collectives  43.8 us (48%)
  waiting for transfers between devices  22.5 us (25%)
  Pallas kernels  15.7 us (17%)
  starting transfers between devices  6.03 us (7%)
  between operations  1.39 us (2%)
    all_to_all x2, blocking collectives, exchanged(): return lax.all_to_all(value, axes, 0, 0, tiled=True)  43.8 us
    ppermute x5, waiting for transfers between devices, across(): return lax.ppermute(value, 'z', [(i, i ^ k) for i in range(4)])  20.1 us
    ppermute x5, starting transfers between devices, across(): return lax.ppermute(value, 'z', [(i, i ^ k) for i in range(4)])  5.68 us
    pallas_call x1, Pallas kernels, on_device(): call(finish, [f32(Q, N)] * 3, ins=[SMEM] + [VM] * 4)  4.47 us
    pallas_call x1, Pallas kernels, on_device(): call(products_first, f32(Z * N, 2 * Q), (), 4 * 10 ** 9, 24)  3.72 us
    pallas_call x1, Pallas kernels, on_device(): call(products_last, f32(Z * Q, 128), (), 4 * 10 ** 9, 24)  3.55 us
    pallas_call x1, Pallas kernels, on_device(): call(prep, [f32(ROWS, 128), f32(R, COLS, 128), f32(3 * Q, 128)], [[pltpu....  2.44 us
    ppermute x3, waiting for transfers between devices, swapped(): return lax.ppermute(value, 'core', [(0, 1), (1, 0)])  2.4 us
  transfers between devices with their start and end apart: 8, of which 7 were waited for; matrix products, arithmetic and copies ran while one was open for 0% of the time, Pallas kernels for 5%

profile of v8, /device:TPU:0, one launch (start us, length us, event | category | flops | bytes accessed | tf_op | source)
XLA Modules:
  0.0 89.5 jit_solution(14259673947496866342)
XLA Ops:
  0.6 2.4 %shard_map.85 = (f32[256,128]{1,0:T(8,128)}, f32[16,200,128]{2,1,0:T(8,128)}, f32[192,128]{1,0:T(8,128)}) custom-call(f32[128,128]{1,0:T(8,128)} %points.1, f32[1,128]{1,0:T(1,128)} %bitcast.13, f32[64,128]{1,0:T(8,128)} %bitcast.10, f32[64,128]{1,0:T(8,128)} %bitcast.11, f32[64,128]{1,0:T(8,128)} %bitcast.12), custom_call_target="tpu_custom_call" | custom-call | flops 1000000 | bytes 1000000 | tf_op jit(solution)/shard_map/pallas_call | solution.py:300
  3.1 0.0 copy-start
  3.1 30.9 %all_to_all.10.cols = f32[16,200,128]{2,1,0:T(8,128)S(1)} all-to-all(f32[16,200,128]{2,1,0:T(8,128)} %get-tuple-element.18), channel_id=1, replica_groups=mesh['y'=4,'xl'=2,'z'=4,'xh'=2,'core'=2] {'y','xl','xh'}, dimensions={0} | all-to-all | bytes 3276800 | tf_op jit(solution)/shard_map/all_to_all | solution.py:296
  34.0 0.0 collective-permute-start.3
  34.0 0.0 copy-done
  34.0 1.9 %collective-permute-start = (f32[256,128]{1,0:T(8,128)S(1)}, f32[256,128]{1,0:T(8,128)S(1)}, u32[]{:S(2)}, u32[]{:S(2)}) collective-permute-start(f32[256,128]{1,0:T(8,128)S(1)} %copy-done), channel_id=1, source_target_pairs={{0,4},{4,0},{8,12},{12,8},{1,5},{5,1},{9,13},{13,9},{2,6},{6,2},{1... | collective-permute-start | bytes 393224 | tf_op jit(solution)/shard_map/ppermute | solution.py:292
  35.9 3.6 %collective-permute-start.1 = (f32[256,128]{1,0:T(8,128)S(1)}, f32[256,128]{1,0:T(8,128)S(1)}, u32[]{:S(2)}, u32[]{:S(2)}) collective-permute-start(f32[256,128]{1,0:T(8,128)S(1)} %copy-done), channel_id=1, source_target_pairs={{0,8},{4,12},{8,0},{12,4},{1,9},{5,13},{9,1},{13,5},{2,10},{6,14},... | collective-permute-start | bytes 393224 | tf_op jit(solution)/shard_map/ppermute | solution.py:292
  39.5 0.0 collective-permute-start.2
  39.5 0.6 collective-permute-done.b
  40.1 6.2 %collective-permute-done.1.c = f32[256,128]{1,0:T(8,128)S(1)} collective-permute-done((f32[256,128]{1,0:T(8,128)S(1)}, f32[256,128]{1,0:T(8,128)S(1)}, u32[]{:S(2)}, u32[]{:S(2)}) %collective-permute-start.1) | collective-permute-done | bytes 131104 | tf_op jit(solution)/shard_map/ppermute | solution.py:292
  46.3 2.4 %collective-permute-done.2.d = f32[256,128]{1,0:T(8,128)S(1)} collective-permute-done((f32[256,128]{1,0:T(8,128)S(1)}, f32[256,128]{1,0:T(8,128)S(1)}, u32[]{:S(2)}, u32[]{:S(2)}) %collective-permute-start.2) | collective-permute-done | bytes 131104 | tf_op jit(solution)/shard_map/ppermute | solution.py:292
  48.7 0.6 shard_map.86
  49.3 3.7 %shard_map.87.before = f32[512,128]{1,0:T(8,128)S(1)} custom-call(bf16[512,768]{1,0:T(8,128)(2,1)S(1)} %get-tuple-element.16.left, f32[512,256]{1,0:T(8,128)S(1)} %get-tuple-element.17.own, f32[16,200,128]{2,1,0:T(8,128)S(1)} %all_to_all.10.cols), custom_call_target="tpu_custom_call" | custom-call | flops 4000000000 | bytes 1000000 | tf_op jit(solution)/shard_map/pallas_call | solution.py:329
  53.1 0.0 collective-permute-done.3.cols
  53.1 3.6 %shard_map.88.mine = f32[256,128]{1,0:T(8,128)S(1)} custom-call(bf16[512,768]{1,0:T(8,128)(2,1)S(1)} %get-tuple-element.16.left, f32[512,256]{1,0:T(8,128)S(1)} %get-tuple-element.17.own, f32[16,200,128]{2,1,0:T(8,128)S(1)} %collective-permute-done.3.cols, f32[512,128]{1,0:T(8,128)S(1)} %shard_map.87.before), custom_call_target="tpu_custom_call" | custom-call | flops 4000000000 | bytes 1000000 | tf_op jit(solution)/shard_map/pallas_call | solution.py:330
  56.6 0.0 copy-start.1
  56.6 0.1 collective-permute-start.4
  56.7 5.1 %collective-permute-done.4.theirs = f32[256,128]{1,0:T(8,128)S(1)} collective-permute-done((f32[256,128]{1,0:T(8,128)S(1)}, f32[256,128]{1,0:T(8,128)S(1)}, u32[]{:S(2)}, u32[]{:S(2)}) %collective-permute-start.4) | collective-permute-done | bytes 131104 | tf_op jit(solution)/shard_map/ppermute | solution.py:292
  61.9 0.1 collective-permute-start.5
  62.6 5.8 %collective-permute-done.5.theirs = f32[256,128]{1,0:T(8,128)S(1)} collective-permute-done((f32[256,128]{1,0:T(8,128)S(1)}, f32[256,128]{1,0:T(8,128)S(1)}, u32[]{:S(2)}, u32[]{:S(2)}) %collective-permute-start.5) | collective-permute-done | bytes 131104 | tf_op jit(solution)/shard_map/ppermute | solution.py:292
  68.4 0.8 shard_map.90
  69.2 0.1 collective-permute-start.6
  69.3 1.2 %collective-permute-done.6.b = f32[96,128]{1,0:T(8,128)S(1)} collective-permute-done((f32[96,128]{1,0:T(8,128)S(1)}, f32[96,128]{1,0:T(8,128)S(1)}, u32[]{:S(2)}, u32[]{:S(2)}) %collective-permute-start.6) | collective-permute-done | bytes 49184 | tf_op jit(solution)/shard_map/ppermute | solution.py:288
  70.5 13.0 %all_to_all.11.pieces = f32[16,48,128]{2,1,0:T(8,128)S(1)} all-to-all(f32[16,48,128]{2,1,0:T(8,128)S(1)} %shard_map.91), channel_id=1, replica_groups=mesh['y'=4,'xl'=2,'z'=4,'xh'=2,'core'=2] {'y','xl','xh'}, dimensions={0} | all-to-all | bytes 786432 | tf_op jit(solution)/shard_map/all_to_all | solution.py:296
  83.5 0.3 collective-permute-start.7
  83.8 1.2 %collective-permute-done.7.theirs = f32[48,128]{1,0:T(8,128)S(1)} collective-permute-done((f32[48,128]{1,0:T(8,128)S(1)}, f32[48,128]{1,0:T(8,128)S(1)}, u32[]{:S(2)}, u32[]{:S(2)}) %collective-permute-start.7) | collective-permute-done | bytes 24608 | tf_op jit(solution)/shard_map/ppermute | solution.py:288
  85.0 0.0 copy-done.1
  85.0 4.5 %shard_map.93 = (f32[64,128]{1,0:T(8,128)}, f32[64,128]{1,0:T(8,128)}, f32[64,128]{1,0:T(8,128)}) custom-call(s32[1]{0:T(128)} %bitcast.core, f32[48,128]{1,0:T(8,128)S(1)} %shard_map.92.mine, f32[48,128]{1,0:T(8,128)S(1)} %collective-permute-done.7.theirs, f32[64,128]{1,0:T(8,128)S(1)} %get-tuple-element.22.image, f32[192,128]{1,0:T(8,128)S(1)} %copy-done.1), custom_call_target="tpu_custom_call" | custom-call | flops 1000000 | bytes 1000000 | tf_op jit(solution)/shard_map/pallas_call | solution.py:341
  (3 shorter events, 0.1 us)
Async XLA Ops:
  3.1 30.9 %copy-start = (f32[256,128]{1,0:T(8,128)S(1)}, f32[256,128]{1,0:T(8,128)}, u32[]{:S(2)}) copy-start(f32[256,128]{1,0:T(8,128)} %get-tuple-element.15.a) | copy-start | bytes 393220
  34.0 19.1 %collective-permute-start.3 = (f32[16,200,128]{2,1,0:T(8,128)S(1)}, f32[16,200,128]{2,1,0:T(8,128)S(1)}, u32[]{:S(2)}, u32[]{:S(2)}) collective-permute-start(f32[16,200,128]{2,1,0:T(8,128)S(1)} %all_to_all.10.cols), channel_id=1, source_target_pairs={{0,1},{1,0},{2,3},{3,2},{4,5},{5,4},{6,7},{7,6},{8,9},{9,8},{10,11... | collective-permute-start | bytes 4915208 | tf_op jit(solution)/shard_map/ppermute | solution.py:288
  34.0 6.1 %collective-permute-start = (f32[256,128]{1,0:T(8,128)S(1)}, f32[256,128]{1,0:T(8,128)S(1)}, u32[]{:S(2)}, u32[]{:S(2)}) collective-permute-start(f32[256,128]{1,0:T(8,128)S(1)} %copy-done), channel_id=1, source_target_pairs={{0,4},{4,0},{8,12},{12,8},{1,5},{5,1},{9,13},{13,9},{2,6},{6,2},{1... | collective-permute-start | bytes 393224 | tf_op jit(solution)/shard_map/ppermute | solution.py:292
  35.9 10.4 %collective-permute-start.1 = (f32[256,128]{1,0:T(8,128)S(1)}, f32[256,128]{1,0:T(8,128)S(1)}, u32[]{:S(2)}, u32[]{:S(2)}) collective-permute-start(f32[256,128]{1,0:T(8,128)S(1)} %copy-done), channel_id=1, source_target_pairs={{0,8},{4,12},{8,0},{12,4},{1,9},{5,13},{9,1},{13,5},{2,10},{6,14},... | collective-permute-start | bytes 393224 | tf_op jit(solution)/shard_map/ppermute | solution.py:292
  39.5 9.2 %collective-permute-start.2 = (f32[256,128]{1,0:T(8,128)S(1)}, f32[256,128]{1,0:T(8,128)S(1)}, u32[]{:S(2)}, u32[]{:S(2)}) collective-permute-start(f32[256,128]{1,0:T(8,128)S(1)} %copy-done), channel_id=1, source_target_pairs={{0,12},{4,8},{8,4},{12,0},{1,13},{5,9},{9,5},{13,1},{2,14},{6,10},... | collective-permute-start | bytes 393224 | tf_op jit(solution)/shard_map/ppermute | solution.py:292
  56.6 28.4 %copy-start.1 = (f32[192,128]{1,0:T(8,128)S(1)}, f32[192,128]{1,0:T(8,128)}, u32[]{:S(2)}) copy-start(f32[192,128]{1,0:T(8,128)} %get-tuple-element.23.kept) | copy-start | bytes 294916
  56.6 5.2 %collective-permute-start.4 = (f32[256,128]{1,0:T(8,128)S(1)}, f32[256,128]{1,0:T(8,128)S(1)}, u32[]{:S(2)}, u32[]{:S(2)}) collective-permute-start(f32[256,128]{1,0:T(8,128)S(1)} %shard_map.88.mine), channel_id=1, source_target_pairs={{0,4},{4,0},{8,12},{12,8},{1,5},{5,1},{9,13},{13,9},{2,6},{6,2},{1... | collective-permute-start | bytes 393224 | tf_op jit(solution)/shard_map/ppermute | solution.py:292
  61.9 6.6 %collective-permute-start.5 = (f32[256,128]{1,0:T(8,128)S(1)}, f32[256,128]{1,0:T(8,128)S(1)}, u32[]{:S(2)}, u32[]{:S(2)}) collective-permute-start(f32[256,128]{1,0:T(8,128)S(1)} %shard_map.89.mine), channel_id=1, source_target_pairs={{0,8},{4,12},{8,0},{12,4},{1,9},{5,13},{9,1},{13,5},{2,10},{6,14},... | collective-permute-start | bytes 393224 | tf_op jit(solution)/shard_map/ppermute | solution.py:292
  69.2 1.3 %collective-permute-start.6 = (f32[96,128]{1,0:T(8,128)S(1)}, f32[96,128]{1,0:T(8,128)S(1)}, u32[]{:S(2)}, u32[]{:S(2)}) collective-permute-start(f32[96,128]{1,0:T(8,128)S(1)} %get-tuple-element.21.a), channel_id=1, source_target_pairs={{0,1},{1,0},{2,3},{3,2},{4,5},{5,4},{6,7},{7,6},{8,9},{9,8},{10,11... | collective-permute-start | bytes 147464 | tf_op jit(solution)/shard_map/ppermute | solution.py:288
  83.5 1.5 %collective-permute-start.7 = (f32[48,128]{1,0:T(8,128)S(1)}, f32[48,128]{1,0:T(8,128)S(1)}, u32[]{:S(2)}, u32[]{:S(2)}) collective-permute-start(f32[48,128]{1,0:T(8,128)S(1)} %shard_map.92.mine), channel_id=1, source_target_pairs={{0,1},{1,0},{2,3},{3,2},{4,5},{5,4},{6,7},{7,6},{8,9},{9,8},{10,11... | collective-permute-start | bytes 73736 | tf_op jit(solution)/shard_map/ppermute | solution.py:288
